TPU v7x, 128 devices: a whole 4x4x4 slice. The times are simulated.
128 devices in a mesh: fr: 2 (over core), sr: 16 (over z, x), sc: 4 (over y).
Axes of the slice: x: 4, y: 4, z: 4, core: 2. Of those that a mesh axis runs over, the one named last changes fastest.
Arguments:
- spec_re: bfloat16 [8, 8192, 256], P('fr', ('sr', 'sc')), may hold values from -6 to 6
- spec_im: bfloat16 [8, 8192, 256], P('fr', ('sr', 'sc')), may hold values from -6 to 6
- offsets: int32 [64, 33], P(('sr', 'sc')), may hold values from 0 to 32, each once within a row
Outputs:
- cross: float32 [8, 64, 33, 128, 256], P('fr', ('sr', 'sc'))
Inputs may be any that keep to these rules, and one draw needn't show every extreme that they name: Each row of offsets names every offset 0 to 32 exactly once.
All inputs are finite; a program needn't handle non-finite values.
Results may differ from a plain program's by a relative error of at most 0.0003.
Values may be sent and summed in bfloat16 or wider, within the bound.
A program may use at most 128 MiB of HBM per device.

v0:
```python
import math

import jax
import jax.numpy as jnp
from jax import lax
from jax.sharding import PartitionSpec as P


def over_pieces(array, axis):
    blocks = lax.all_gather(array, axis)
    return blocks.sum(axis=0)


def in_order(blocks, dim):
    shape = list(blocks.shape[1:])
    shape[dim] *= blocks.shape[0]
    return jnp.moveaxis(blocks, 0, dim).reshape(shape)


def sent_to_all(array, axis):
    copies = jnp.broadcast_to(array, (lax.axis_size(axis), *array.shape))
    return lax.all_to_all(copies, axis, split_axis=0, concat_axis=0, tiled=True)


def gathered_copies(array, axis, dim):
    return in_order(sent_to_all(array, axis), dim)


def passed_along(array, axis, by):
    size = lax.axis_size(axis)
    return lax.ppermute(array, axis, [(i, (i + by) % size) for i in range(size)])


def products(prepared, visiting):

    def multiply(left_side, other):
        return jnp.einsum("fis,mfjs->fmij", left_side, other, preferred_element_type=jnp.float32)

    real_part = multiply(prepared[0], visiting[:, 0]) + multiply(prepared[1], visiting[:, 1])
    imag_part = multiply(prepared[1], visiting[:, 0]) - multiply(prepared[0], visiting[:, 1])
    return (real_part, imag_part)


def local(spec_re, spec_im, offsets):
    bin_count, block_rows, seg_count = spec_re.shape
    block_count = lax.axis_size(("sr", "sc"))
    slot_count = block_count // 2 + 1
    bin_total = bin_count * lax.axis_size("fr")
    real_own = spec_re.astype(jnp.float32)
    imag_own = spec_im.astype(jnp.float32)
    local_power = jnp.sum(real_own * real_own + imag_own * imag_own, axis=(0, 2))
    band_power = over_pieces(local_power, "fr")
    gain_own = lax.rsqrt(band_power / (bin_total * seg_count))
    all_gains = gathered_copies(gain_own, ("sr", "sc"), 0).reshape(block_count, block_rows)
    own_index = lax.axis_index(("sr", "sc"))
    partner_index = (own_index + jnp.arange(slot_count, dtype=jnp.int32)) % block_count
    partner_gain = jnp.take(all_gains, partner_index, axis=0)
    own_parts = jnp.stack([spec_re, spec_im])
    gathered = own_parts[None]
    held_count = 1
    while held_count < slot_count:
        send_count = min(held_count, slot_count - held_count)
        received = passed_along(gathered[:send_count], ("sr", "sc"), -held_count)
        gathered = jnp.concatenate([gathered, received], axis=0)
        held_count = held_count + send_count
    real_part, imag_part = products(own_parts, gathered)
    weight = (
        gain_own[None, None, :, None]
        * partner_gain[None, :, None, :]
        * (1.0 / math.sqrt(seg_count))
    )
    joined = jnp.concatenate([real_part * weight, imag_part * weight], axis=-1)
    slot_order = offsets[0]
    cross = jnp.take(joined, slot_order, axis=1)
    return cross[:, None]


def solution(mesh):
    placed = (P("fr", ("sr", "sc"), None), P("fr", ("sr", "sc"), None), P(("sr", "sc"), None))
    return jax.shard_map(
        local,
        mesh=mesh,
        in_specs=placed,
        out_specs=P("fr", ("sr", "sc"), None, None, None),
        check_vma=False,
    )
```

profile of v0, /device:TPU:30, one launch (start us, length us, event | category | flops | bytes accessed | tf_op | source)
XLA Modules:
  0.0 499.5 jit_solution(8147476896506988403)
XLA Ops:
  0.0 0.0 copy-start
  0.0 0.0 copy-start.1
  0.0 1.1 maximum_bitcast_fusion
  1.1 0.8 collective-permute-start
  2.0 17.1 %collective-permute-done = bf16[1,2,4,128,256]{4,3,0,2,1:T(8,128)(2,1)S(1)} collective-permute-done((bf16[1,2,4,128,256]{4,3,0,2,1:T(8,128)(2,1)S(1)}, bf16[1,2,4,128,256]{4,3,0,2,1:T(8,128)(2,1)S(1)}, u32[]{:S(2)}, u32[]{:S(2)}) %collective-permute-start) | collective-permute-done | bytes 524320 | tf_op jit(solution)/shard_map/ppermute | solution.py:31
  19.1 0.1 pad_maximum_fusion.3
  19.2 0.1 collective-permute-start.1
  19.3 28.5 %collective-permute-done.1 = bf16[2,2,4,128,256]{4,3,0,2,1:T(8,128)(2,1)S(1)} collective-permute-done((bf16[2,2,4,128,256]{4,3,0,2,1:T(8,128)(2,1)S(1)}, bf16[2,2,4,128,256]{4,3,0,2,1:T(8,128)(2,1)S(1)}, u32[]{:S(2)}, u32[]{:S(2)}) %collective-permute-start.1) | collective-permute-done | bytes 1048608 | tf_op jit(solution)/shard_map/ppermute | solution.py:31
  47.8 0.2 pad_maximum_fusion.2
  48.0 0.1 collective-permute-start.2
  48.1 47.8 %collective-permute-done.2 = bf16[4,2,4,128,256]{4,3,0,2,1:T(8,128)(2,1)S(1)} collective-permute-done((bf16[4,2,4,128,256]{4,3,0,2,1:T(8,128)(2,1)S(1)}, bf16[4,2,4,128,256]{4,3,0,2,1:T(8,128)(2,1)S(1)}, u32[]{:S(2)}, u32[]{:S(2)}) %collective-permute-start.2) | collective-permute-done | bytes 2097184 | tf_op jit(solution)/shard_map/ppermute | solution.py:31
  95.9 0.4 pad_maximum_fusion.1
  96.3 0.1 collective-permute-start.3
  96.4 0.0 copy-done
  96.4 0.0 copy-done.1
  96.4 1.1 constant_dynamic-update-slice_fusion.4
  97.5 1.1 constant_dynamic-update-slice_fusion.3
  98.6 1.6 constant_dynamic-update-slice_fusion.2
  100.1 0.0 copy-start.2
  100.1 2.5 constant_dynamic-update-slice_fusion.1
  102.6 85.9 %collective-permute-done.3 = bf16[8,2,4,128,256]{4,3,0,2,1:T(8,128)(2,1)S(1)} collective-permute-done((bf16[8,2,4,128,256]{4,3,0,2,1:T(8,128)(2,1)S(1)}, bf16[8,2,4,128,256]{4,3,0,2,1:T(8,128)(2,1)S(1)}, u32[]{:S(2)}, u32[]{:S(2)}) %collective-permute-start.3) | collective-permute-done | bytes 4194336 | tf_op jit(solution)/shard_map/ppermute | solution.py:31
  188.5 4.4 constant_dynamic-update-slice_fusion
  193.0 8.9 %collective-permute-start.4 = (bf16[16,2,4,128,256]{4,3,0,2,1:T(8,128)(2,1)}, bf16[16,2,4,128,256]{4,3,0,2,1:T(8,128)(2,1)}, u32[]{:S(2)}, u32[]{:S(2)}) collective-permute-start(bf16[16,2,4,128,256]{4,3,0,2,1:T(8,128)(2,1)} %get-tuple-element.5), channel_id=1, source_target_pairs={{0,48},{1,49},{2,50},{3,51},{4,52},{5,53},{6,54},{7,55},{8,56},{9,... | collective-permute-start | bytes 25165832 | tf_op jit(solution)/shard_map/ppermute | solution.py:31
  201.9 0.0 collective-permute-start.5
  201.9 0.2 add_reduce_fusion
  202.0 1.8 all-gather.1
  203.9 0.6 broadcast_in_dim.32
  204.5 10.2 %all-to-all-start = ((f32[64,1,128]{2,1,0:T(1,128)}), f32[64,1,128]{2,1,0:T(1,128)S(1)}, u32[]{:S(2)}, u32[]{:S(2)}) async-start(f32[64,1,128]{2,1,0:T(1,128)} %broadcast_in_dim.32), calls=%async_computation | async-start | bytes 65536 | tf_op jit(solution)/shard_map/all_to_all | solution.py:22
  214.7 0.0 copy-done.2
  214.8 175.3 %all-to-all-done = f32[64,1,128]{2,1,0:T(1,128)S(1)} async-done(((f32[64,1,128]{2,1,0:T(1,128)}), f32[64,1,128]{2,1,0:T(1,128)S(1)}, u32[]{:S(2)}, u32[]{:S(2)}) %all-to-all-start) | async-done | bytes 32800 | tf_op jit(solution)/shard_map/all_to_all | solution.py:22
  390.0 0.6 gather_fusion
  390.6 0.1 broadcast_select_fusion
  390.7 0.6 multiply_multiply_fusion
  391.3 0.0 collective-permute-done.4
  391.3 7.9 %constant_dynamic-update-slice_fusion.6 = bf16[33,2,4,128,256]{4,3,0,2,1:T(8,128)(2,1)} fusion(bf16[33,2,4,128,256]{4,3,0,2,1:T(8,128)(2,1)} %get-tuple-element.6, bf16[16,2,4,128,256]{4,3,0,2,1:T(8,128)(2,1)} %collective-permute-done.4), kind=kLoop, calls=%fused_computation.28 | loop fusion | bytes 16777216
  399.2 0.0 collective-permute-done.5
  399.2 0.8 constant_dynamic-update-slice_fusion.5
  400.1 9.2 %fusion.3 = f32[4,33,128,128]{3,2,1,0:T(8,128)} fusion(bf16[33,2,4,128,256]{4,3,0,2,1:T(8,128)(2,1)} %constant_dynamic-update-slice_fusion.5, bf16[4,128,256]{2,1,0:T(8,128)(2,1)S(1)} %copy-done.1), kind=kOutput, calls=%fused_computation.11 | convolution fusion | flops 1107296256 | bytes 17563648 | tf_op jit(solution)/shard_map/fis,mfjs->fmij/dot_general | solution.py:37
  409.2 9.2 %fusion.2 = f32[4,33,128,128]{3,2,1,0:T(8,128)} fusion(bf16[33,2,4,128,256]{4,3,0,2,1:T(8,128)(2,1)} %constant_dynamic-update-slice_fusion.5, bf16[4,128,256]{2,1,0:T(8,128)(2,1)S(1)} %copy-done), kind=kOutput, calls=%fused_computation.10 | convolution fusion | flops 1107296256 | bytes 17563648 | tf_op jit(solution)/shard_map/fis,mfjs->fmij/dot_general | solution.py:37
  418.5 12.0 %bitcast_multiply_fusion.1 = f32[4,33,128,128]{2,3,1,0:T(8,128)} fusion(f32[4,33,128,128]{3,2,1,0:T(8,128)} %fusion.3, f32[33,128,128]{1,2,0:T(8,128)S(1)} %multiply_multiply_fusion, bf16[33,2,4,128,256]{4,3,0,2,1:T(8,128)(2,1)} %constant_dynamic-update-slice_fusion.5, bf16[4,128,256]{2,1,0:T(8,128)(2,1)S(1)} %copy-done), kind=kOutput, calls=%fused_computation.7 | convolution fusion | flops 1111621632 | bytes 28377088 | tf_op jit(solution)/shard_map/fis,mfjs->fmij/dot_general | solution.py:37
  430.5 12.0 %bitcast_multiply_fusion = f32[4,33,128,128]{2,3,1,0:T(8,128)} fusion(f32[4,33,128,128]{3,2,1,0:T(8,128)} %fusion.2, f32[33,128,128]{1,2,0:T(8,128)S(1)} %multiply_multiply_fusion, bf16[33,2,4,128,256]{4,3,0,2,1:T(8,128)(2,1)} %constant_dynamic-update-slice_fusion.5, bf16[4,128,256]{2,1,0:T(8,128)(2,1)S(1)} %copy-done.1), kind=kOutput, calls=%fused_computation.6 | convolution fusion | flops 1111621632 | bytes 28377088 | tf_op jit(solution)/shard_map/fis,mfjs->fmij/dot_general | solution.py:37
  442.5 12.1 %pad_maximum_fusion = f32[4,33,128,256]{2,3,1,0:T(8,128)} fusion(f32[4,33,128,128]{2,3,1,0:T(8,128)} %bitcast_multiply_fusion, f32[4,33,128,128]{2,3,1,0:T(8,128)} %bitcast_multiply_fusion.1), kind=kLoop, calls=%fused_computation.2 | loop fusion | flops 4325376 | bytes 34603008 | tf_op jit(solution)/shard_map/concatenate | solution.py:72
  454.6 14.7 %gather_fusion.1 = f32[33,4,128,256]{2,3,1,0:T(8,128)} fusion(f32[4,33,128,256]{2,3,1,0:T(8,128)} %pad_maximum_fusion, s32[1024]{0:T(1024)S(1)} %pad_clamp_fusion), kind=kCustom, calls=%fused_computation.1 | custom fusion | bytes 34603140 | tf_op jit(solution)/shard_map/jit(_take)/gather | solution.py:74
  469.3 12.1 %bitcast_select_fusion = f32[4,1,33,128,256]{3,4,0,2,1:T(8,128)} fusion(f32[33,4,128,256]{2,3,1,0:T(8,128)} %gather_fusion.1, pred[33]{0:T(512)(128)(4,1)S(1)} %compare_and_fusion.1), kind=kLoop, calls=%fused_computation.3 | loop fusion | flops 4325376 | bytes 34603040 | tf_op jit(solution)/shard_map/jit(_take)/select_n | solution.py:74
  481.4 18.1 %copy.5 = f32[4,1,33,128,256]{4,3,2,1,0:T(8,128)} copy(f32[4,1,33,128,256]{3,4,0,2,1:T(8,128)} %bitcast_select_fusion) | data formatting | bytes 34603008 | tf_op jit(solution)/shard_map/jit(_take)/select_n | solution.py:74
  (8 shorter events, 0.1 us)
Async XLA Ops:
  0.0 96.4 %copy-start = (bf16[4,128,256]{2,1,0:T(8,128)(2,1)S(1)}, bf16[4,128,256]{2,1,0:T(8,128)(2,1)}, u32[]{:S(2)}) copy-start(bf16[4,128,256]{2,1,0:T(8,128)(2,1)} %param.3) | copy-start | bytes 786436
  0.0 96.4 %copy-start.1 = (bf16[4,128,256]{2,1,0:T(8,128)(2,1)S(1)}, bf16[4,128,256]{2,1,0:T(8,128)(2,1)}, u32[]{:S(2)}) copy-start(bf16[4,128,256]{2,1,0:T(8,128)(2,1)} %param.4) | copy-start | bytes 786436
  1.1 18.0 %collective-permute-start = (bf16[1,2,4,128,256]{4,3,0,2,1:T(8,128)(2,1)S(1)}, bf16[1,2,4,128,256]{4,3,0,2,1:T(8,128)(2,1)S(1)}, u32[]{:S(2)}, u32[]{:S(2)}) collective-permute-start(bf16[1,2,4,128,256]{4,3,0,2,1:T(8,128)(2,1)S(1)} %maximum_bitcast_fusion), channel_id=1, source_target_pairs={{0,63},{1,0},{2,1},{3,2},{4,3},{5,4},{6,5},{7,6},{8,7},{9,8},{10,9... | collective-permute-start | bytes 1572872 | tf_op jit(solution)/shard_map/ppermute | solution.py:31
  19.2 28.6 %collective-permute-start.1 = (bf16[2,2,4,128,256]{4,3,0,2,1:T(8,128)(2,1)S(1)}, bf16[2,2,4,128,256]{4,3,0,2,1:T(8,128)(2,1)S(1)}, u32[]{:S(2)}, u32[]{:S(2)}) collective-permute-start(bf16[2,2,4,128,256]{4,3,0,2,1:T(8,128)(2,1)S(1)} %pad_maximum_fusion.3), channel_id=1, source_target_pairs={{0,62},{1,63},{2,0},{3,1},{4,2},{5,3},{6,4},{7,5},{8,6},{9,7},{10,... | collective-permute-start | bytes 3145736 | tf_op jit(solution)/shard_map/ppermute | solution.py:31
  48.0 47.8 %collective-permute-start.2 = (bf16[4,2,4,128,256]{4,3,0,2,1:T(8,128)(2,1)S(1)}, bf16[4,2,4,128,256]{4,3,0,2,1:T(8,128)(2,1)S(1)}, u32[]{:S(2)}, u32[]{:S(2)}) collective-permute-start(bf16[4,2,4,128,256]{4,3,0,2,1:T(8,128)(2,1)S(1)} %pad_maximum_fusion.2), channel_id=1, source_target_pairs={{0,60},{1,61},{2,62},{3,63},{4,0},{5,1},{6,2},{7,3},{8,4},{9,5},{1... | collective-permute-start | bytes 6291464 | tf_op jit(solution)/shard_map/ppermute | solution.py:31
  96.3 92.2 %collective-permute-start.3 = (bf16[8,2,4,128,256]{4,3,0,2,1:T(8,128)(2,1)S(1)}, bf16[8,2,4,128,256]{4,3,0,2,1:T(8,128)(2,1)S(1)}, u32[]{:S(2)}, u32[]{:S(2)}) collective-permute-start(bf16[8,2,4,128,256]{4,3,0,2,1:T(8,128)(2,1)S(1)} %pad_maximum_fusion.1), channel_id=1, source_target_pairs={{0,56},{1,57},{2,58},{3,59},{4,60},{5,61},{6,62},{7,63},{8,0},{9,1... | collective-permute-start | bytes 12582920 | tf_op jit(solution)/shard_map/ppermute | solution.py:31
  100.1 114.6 %copy-start.2 = (s32[1,33]{1,0:T(1,128)S(1)}, s32[1,33]{1,0:T(1,128)}, u32[]{:S(2)}) copy-start(s32[1,33]{1,0:T(1,128)} %param.5) | copy-start | bytes 400
  193.0 198.3 %collective-permute-start.4 = (bf16[16,2,4,128,256]{4,3,0,2,1:T(8,128)(2,1)}, bf16[16,2,4,128,256]{4,3,0,2,1:T(8,128)(2,1)}, u32[]{:S(2)}, u32[]{:S(2)}) collective-permute-start(bf16[16,2,4,128,256]{4,3,0,2,1:T(8,128)(2,1)} %get-tuple-element.5), channel_id=1, source_target_pairs={{0,48},{1,49},{2,50},{3,51},{4,52},{5,53},{6,54},{7,55},{8,56},{9,... | collective-permute-start | bytes 25165832 | tf_op jit(solution)/shard_map/ppermute | solution.py:31
  201.9 197.4 %collective-permute-start.5 = (bf16[1,2,4,128,256]{4,3,0,2,1:T(8,128)(2,1)S(1)}, bf16[1,2,4,128,256]{4,3,0,2,1:T(8,128)(2,1)S(1)}, u32[]{:S(2)}, u32[]{:S(2)}) collective-permute-start(bf16[1,2,4,128,256]{4,3,0,2,1:T(8,128)(2,1)S(1)} %maximum_bitcast_fusion), channel_id=1, source_target_pairs={{0,32},{1,33},{2,34},{3,35},{4,36},{5,37},{6,38},{7,39},{8,40},{9,... | collective-permute-start | bytes 1572872 | tf_op jit(solution)/shard_map/ppermute | solution.py:31
  204.5 185.5 %all-to-all-start = ((f32[64,1,128]{2,1,0:T(1,128)}), f32[64,1,128]{2,1,0:T(1,128)S(1)}, u32[]{:S(2)}, u32[]{:S(2)}) async-start(f32[64,1,128]{2,1,0:T(1,128)} %broadcast_in_dim.32), calls=%async_computation | async-start | bytes 65536 | tf_op jit(solution)/shard_map/all_to_all | solution.py:22
where the time goes:
time: 500 us
  waiting for transfers between devices  355 us (71%)
  local copies, waits for them, and re-layouts  52.3 us (10%)
  matrix products  42.4 us (8%)
  other arithmetic  28.1 us (6%)
  starting transfers between devices  20.1 us (4%)
    ppermute x6, waiting for transfers between devices, passed_along(): lax.ppermute(array, axis, [(i, (i + by) % size) for i in range(size)])  179 us
    all_to_all x1, waiting for transfers between devices, sent_to_all(): return lax.all_to_all(copies, axis, split_axis=0, concat_axis=0, tiled=True)  175 us
    dot_general x4, matrix products, multiply(): jnp.einsum('fis,mfjs->fmij', left_side, other, preferred_element_type=jnp...  42.4 us
    select_n x1, local copies, waits for them, and re-layouts, local(): cross = jnp.take(joined, slot_order, axis=1)  18.1 us
    gather x1, local copies, waits for them, and re-layouts, local(): cross = jnp.take(joined, slot_order, axis=1)  14.7 us
    unnamed x10, local copies, waits for them, and re-layouts  13 us
    select_n x2, other arithmetic, local(): cross = jnp.take(joined, slot_order, axis=1)  12.1 us
    concatenate x1, other arithmetic, local(): joined = jnp.concatenate([real_part * weight, imag_part * weight], axis=-1)  12.1 us
  transfers between devices with their start and end apart: 7, of which 5 were waited for; matrix products, arithmetic and copies ran while one was open for 3% of the time, Pallas kernels for 0%

commit v1 on v0

v1 whole, which is shorter than its diff:
```python
import functools
import math

import jax
import jax.numpy as jnp
from jax import lax
from jax.experimental import pallas as pl
from jax.experimental.pallas import tpu as pltpu
from jax.sharding import PartitionSpec as P

MESH = pl.DeviceIdType.MESH

PLAN = (
    (0x00000100ffffffffffffffffffffffff, 0x010201030301010300030200ffffffff, 0x00ffffff03ffffff00ffffff00ffffff, 0x030003ff000301ff030101ff030200ff, 0xffffffffffffffffffffffffffffffff, 0x03010002020200010103020000030002),
    (0x02030201ffffffffffffffffffffffff, 0x020302010100020002000302ffffffff, 0x02ffffff01ffffff02ffffff01ffffff, 0x020302ff010002ff020000ff020002ff, 0xffffffffffffffffffffffffffffffff, 0x02030201010002000202000101000303),
    (0x0102030252525051515352503c535052, 0x03010008020303025115060350535052, 0x01515052155250515115521703535052, 0x01025052525250515115061750530152, 0xffffffffffffffffffffffffffffffff, 0x01020303000103020301010303010101),
    (0x0404040451505250525250515150533c, 0x04040404040404040404040451505353, 0x04535251045015500452505104505353, 0x04040451040404500404045104045353, 0xffffffffffffffffffffffffffffffff, 0x04040404040404040404040404040400),
    (0x03513c53503f53525351515353515151, 0x4c000500500550175317510653515151, 0x53525353503f53525317515302515151, 0x00080553030553521708175314511751, 0xffffff55ff575755ff56ff60655558ff, 0x00000500030301060000030202020204),
    (0x434b4d3d545454545454545454545450, 0x434d4d5242104c014d52121854545450, 0x15543e543e5454544d5454544b545450, 0x153c01543e3e15543d52055451545450, 0xffffffffffffffffffffffffffffff58, 0x15140117423e15540854125444545450),
    (0x423e4c3c53533e3c5050535252525254, 0x4d05530f4d024b56424d4c5152525254, 0x3d4e54506053513c3f4b535252525254, 0x3d2b3e503f513c3c501c535252520754, 0xffffff6260ffff5864ff6462678d788f, 0x141515163a3f3e3c424d535252525254),
    (0x4f404f3e403d403f584f623d94554e53, 0x4e4b4f674f4f4d2444514e0a424b4c5a, 0x4e4d4067404f181840511816544b4040, 0x4040403e40574018403c3c1694555040, 0xffffffff5761616656ff575c61875659, 0x18401415403d403f404f3c0a424b1a51),
    (0x3e3c4b433c4c514192a44d4e7e8d3fa4, 0x4f654b6661574f1c4f4b4f6a564d60a0, 0x4050656661513d14164c16283e4c3f3c, 0x173f166616403d143f553d6a3e19083c, 0xffffffff61ff566f61555f6a567a6078, 0x171717503c4c3c413f3f3f28434c4d18),
    (0x3d420d4c3e433f4d4341415a403788a0, 0x50640d624b4e191a434e4d1c45a45aa4, 0x4f4f51134b3c3f24121417388b3b173f, 0x3f454114183c051718533e2b4017093f, 0xffff625d625f5c5f63ff60588b61887a, 0x54093f133e195323281c213840294016),
    (0x4839440a44444e4245454090a24fa44d, 0x651165244561378c58116305634f6359, 0x3e6567644e798c704f11639063616314, 0x3c6567642d793e8f75428f186756787f, 0x576061ff637967706a7963ff585f637f, 0x40393e433d1b4e423d114e254c4e3e4d),
    (0x4e4c4a0d4c3c56463e3e714f36a29088, 0x64684a5512116576174f71884da25761, 0x3f678f684f8d636f118f5f8c65797863, 0x6468303c923d061c1c8f581492796a78, 0xffffff5e7e78ff76756b74ff797e6188, 0x3f113c3c41514b501c1d2d2e4e434930),
    (0x4b4140458d38434f8e565a41929c809a, 0x4b625f63076b571f141318215c5f5972, 0x2868120f8d259e3a131333395c878b9a, 0x2f41452e8d4479928e2902886c7a8014, 0x60625f6c74877e5d5b7a8b5e847c8072, 0x3c3b40453f4f1f3a474c51434b3c0f46),
    (0x492f4139319790456a8f944293979d59, 0x4a0f1151785e11690f09107e61975e6f, 0x64298c25783a674f224f7c1318633874, 0x2c302b1d808f427c1a1d7c8a086c9018, 0x628a63ff78975e698a5e7c5d57638679, 0x2f2f27392f3a394622414130364f3f1c),
    (0x2f340a3780326f1f7e213b939b7e8e49, 0x050d1d5d8a690a660b1b152058576274, 0x6861634d8c1173172c8e61746c4d5f9c, 0x28011d288c6b9e2d928e71933c8d7f80, 0x63696aff5f76737b809387867a737f7e, 0x3e3e0a1b203c46524d503a3305191e49),
    (0x403850058fa1893a904d475c82407d40, 0x0e10771c09621477590e07229b9f6f66, 0x8c4c77118f285f778d72147d239f9972, 0x681c8c4079428e2e7b2a917e562c7d85, 0x7983ff736d85805e7b72947d82567d7d, 0x203c414a4b23352d464447392d1d1c19),
    (0x4d5e484a8a9970a3891f93a4848c467f, 0x078920530f8d6b7018121e0971716184, 0x118a7c395f9025718ea0233528179799, 0x2d838f302e43707e1b7d7a947f6b361a, 0x5c5b5b776a99708789836f8a71709775, 0x434d4d53310d4a3d52211e512b414627),
    (0x4c33210b7f8e8c966f806f969aa49581, 0x136309220d5a7e7e561c0d5c94627755, 0x3838754c7a9c6f8c900f373b2b3d2478, 0x3164352d568e301a0b4390a07d6d7e81, 0x7b5eff91566272776f80939685886f81, 0x194c2f30223245484c2c4b2c4614241e),
    (0x1f240e2e8b909a8d8594a17f5c845a99, 0x708e10208020853785717f845e846d85, 0x708e258c8b9d618d399d3b362a739d28, 0x708e7c1c318d80308483948c0b089658, 0x7677889b5e6e7f71855a7a7f5c84846b, 0x3d3f44364e2048474a450e4e120d4c37),
    (0x21653f626f8c962e3093818196997083, 0x85908c8074855636101d61809699999c, 0x108d4c8224a1397f10904d9f4c124d2a, 0x7f8d6a828f9c7ea4089092895764066e, 0x5887788f797e5d6e9b5c929c6c717e83, 0x1e363b474f214d360a15504147335153),
    (0x45593e63888d92979a8388207d4b1f32, 0x8d59223590328b651f56160b7086a498, 0x768f86a0728a9b8723626c11120f2311, 0x8e9c77a36d9294199e717d90152e0584, 0x896d6979985e949b6e7f588489657098, 0x45534f54530534515136464b45504a40),
    (0x65535f4f978587353a789a80476c9986, 0x90538b648f8e6f7384253112a25d5894, 0x907a5f9b029f9d8f186da36a5e2c4b9d, 0x909d7f9595945e3a7d6d32a4090d8e86, 0x5b7c827f8b807a7f848969995e5b5b9b, 0x4c4e4a515250333850480d48532f310d),
    (0x684f0566839c8d9279778f888895942d, 0x414c905e856a905d8b2100366e828592, 0x8f879ba375628d1514299fa188153269, 0x949386a09e9d5f5506306e362d307749, 0x8a93865c975a5b89866a5a767f5a5e65, 0x4f4f4720504b184f2c24523e4d30503a),
    (0x640d55559b8a83a2469732a2698f8184, 0x7f7f146543178950070725108248757e, 0x839d87a18ea2117358a43f9d141e110f, 0x798491a1817357a3851888392326261e, 0x5f728794649879755d85889d63667770, 0x524b504c0a4e09302618171c2346533e),
    (0x530e07128c80998a9679a37c4f5d846f, 0x63065d81238213860e302e4a6a989297, 0x6c838280239b3186564660253d1f8e27, 0x9c9e8879228c16769672182f179a3f46, 0x86997384806c8a7c7f78956b70866993, 0x5350211d09454c092134065330273a14),
    (0x5236471b9583849c7a9d8a7e97a03d7c, 0x186d124c632479101a8f522e9a5b9395, 0x629c9c850e8e6d65489897897e2b934d, 0x9f9f949a6f5386488245247154104a2c, 0x5a75937c849a6b7282776c9775746d95, 0x4d5249401e062c12151f250933403d06),
    (0x552b4623948f82897f91766b45417a6a, 0x1f3955161955414b648948489d929c9b, 0x93a0968f356d7f2154335c2b53925d7e, 0x8f7e93892a5547675876764b42717175, 0x875a7dff756f82787981997a6e9294ff, 0x511b1b4d192527110c140b113c3a1710),
    (0x1e3f2c3586879591913f78672d7487a3, 0x5f4552365f3345555b5a287899796a93, 0x699b6f79223d4b306865906d58657b70, 0x9590757c8633566b5481504763508468, 0x6b7a6fff86918b9e9e9a6b949affffff, 0x50481c1e1c342dff16233e1e14314eff),
    (0xffffffff9082869b5dff69ff7f7affff, 0xff4461ff4a12ff52ffffffff9593949d, 0x7ba37992ff8c6b1fff6cffffffffffff, 0x8d756f80ffffff8a8834ffffffffffff, 0x737e79ffff72ffff99ffffffffffffff, 0x4930261926ffffffff0f2eff18ffffff),
    (0xffffffff986998ffffffffffffffffff, 0xffffffffffffffffffffffff92ff9aff, 0x4b9f5dffffffffffffffffffffffffff, 0xff616d4affffffffffffffffffffffff, 0xffffffffffffffffffffffffffffffff, 0x2d0f091affffffffffffffffffffffff),
)

LAG = 2
CHUNKS = 5
SLOTS = 33
UNITS = 65
UNIT = 16
CHUNK_UNITS = UNITS // CHUNKS
OPPOSITE = (1, 0, 3, 2, 5, 4)


def neighbour_position(p, d):
    x, y = divmod(p, 4)
    if d == 0:
        x = (x + 1) % 4
    if d == 1:
        x = (x + 3) % 4
    if d == 2:
        y = (y + 1) % 4
    if d == 3:
        y = (y + 3) % 4
    return 4 * x + y


def signed(word):
    return word - (1 << 32) if word >= 1 << 31 else word


def entries(step, d):
    return [(PLAN[step][d] >> (8 * p)) & 255 for p in range(16)]


def mask_of(flags):
    return sum(1 << p for p, flag in enumerate(flags) if flag)


def gather_kernel(re_ref, im_ref, held, part, part_in, send_sem, recv_sem, load_sem, pair_sem):
    bins = re_ref.shape[0]
    tiles = re_ref.shape[1]
    fr = lax.axis_index("fr")
    sr = lax.axis_index("sr")
    sc = lax.axis_index("sc")
    z, x, y = sr // 4, sr % 4, sc
    p = 4 * x + y
    steps = len(PLAN)

    loads = []
    for f in range(bins):
        for i, ref in enumerate((re_ref, im_ref)):
            unit = (2 * f + i) * tiles
            loads.append(
                pltpu.make_async_copy(ref.at[f], held.at[0, pl.ds(unit, tiles)], load_sem.at[2 * f + i])
            )
    for load in loads:
        load.start()

    xp, xm = (x + 1) % 4, (x + 3) % 4
    yp, ym = (y + 1) % 4, (y + 3) % 4
    zp, zm = (z + 1) % 4, (z + 3) % 4
    targets = (
        (fr, 4 * z + xp, y),
        (fr, 4 * z + xm, y),
        (fr, sr, yp),
        (fr, sr, ym),
        (fr, 4 * zp + x, y),
        (fr, 4 * zm + x, y),
    )
    ahead = (4 * (xp - x), 4 * (xm - x), yp - y, ym - y, 16, -16)
    twin = (1 - fr, sr, sc)

    barrier = pltpu.get_barrier_semaphore()
    for device in targets + (twin,):
        pl.semaphore_signal(barrier, inc=1, device_id=device, device_id_type=MESH)
    for load in loads:
        load.wait()
    pl.semaphore_wait(barrier, 7)

    def chosen(step, d):
        words = [signed((PLAN[step][d] >> (32 * i)) & 0xFFFFFFFF) for i in range(4)]
        word = jnp.where(
            x < 2,
            jnp.where(x == 0, jnp.int32(words[0]), jnp.int32(words[1])),
            jnp.where(x == 2, jnp.int32(words[2]), jnp.int32(words[3])),
        )
        return lax.shift_right_logical(word, 8 * y) & 255

    def guarded(mask, action):
        if mask == 0:
            return
        if mask == 0xFFFF:
            action()
            return
        pl.when((lax.shift_right_logical(jnp.int32(mask), p) & 1) == 1)(action)

    def transfer(step, d, slot, chunk):
        rows = pl.ds(chunk * CHUNK_UNITS, CHUNK_UNITS)
        return pltpu.make_async_remote_copy(
            src_ref=held.at[slot, rows],
            dst_ref=held.at[slot - ahead[d], rows],
            send_sem=send_sem.at[d, step],
            recv_sem=recv_sem.at[d, step],
            device_id=targets[d],
            device_id_type=MESH,
        )

    def send(step, d):
        def action():
            entry = chosen(step, d)
            transfer(step, d, entry // CHUNKS, entry % CHUNKS).start()

        guarded(mask_of(v != 255 for v in entries(step, d)), action)

    def waited(step, d, dest):
        rows = pl.ds(0, CHUNK_UNITS)
        return pltpu.make_async_remote_copy(
            src_ref=held.at[0, rows],
            dst_ref=held.at[1, rows],
            send_sem=send_sem.at[d, step],
            recv_sem=recv_sem.at[d, step],
            device_id=targets[d],
            device_id_type=MESH,
        )

    def receive(step, d):
        sent = entries(step, d)
        flags = [sent[neighbour_position(q, OPPOSITE[d])] != 255 for q in range(16)]
        guarded(mask_of(flags), lambda: waited(step, d, None).wait_recv())

    def finish(step, d):
        guarded(
            mask_of(v != 255 for v in entries(step, d)),
            lambda: waited(step, d, None).wait_send(),
        )

    exchange = pltpu.make_async_remote_copy(
        src_ref=part,
        dst_ref=part_in,
        send_sem=pair_sem.at[0],
        recv_sem=pair_sem.at[1],
        device_id=twin,
        device_id_type=MESH,
    )

    for step in range(steps + LAG):
        if step >= LAG:
            for d in range(6):
                receive(step - LAG, d)
        if step < steps:
            for d in range(6):
                send(step, d)
        if step == 0:
            total = jnp.zeros((tiles, UNIT, 256), jnp.float32)
            for i in range(2 * bins):
                piece = held[0, pl.ds(i * tiles, tiles)].astype(jnp.float32)
                total += piece * piece
            total = total.reshape(tiles * UNIT, 256)
            half = total[:, :128] + total[:, 128:]
            power = jnp.sum(half.T, axis=0, keepdims=True)
            part[...] = jnp.broadcast_to(power, part.shape)
            exchange.start()
        if step == 2:
            exchange.wait()
            power = part[...] + part_in[...]
            gain = 1.0 / jnp.sqrt(power * (1.0 / 2048.0))
            gain = jnp.concatenate([gain, gain], axis=0)
            gain = jnp.concatenate([gain, gain], axis=1)
            high = gain.astype(jnp.bfloat16).astype(jnp.float32)
            middle = (gain - high).astype(jnp.bfloat16).astype(jnp.float32)
            low = gain - high - middle
            row = lax.broadcasted_iota(jnp.int32, (UNIT, 256), 0)
            rest = jnp.where(row == 1, middle, low)
            held[0, UNITS - 1] = jnp.where(row == 0, high, rest).astype(jnp.bfloat16)
    for step in range(steps):
        for d in range(6):
            finish(step, d)


def gathered(re, im):
    bins, tiles = re.shape[:2]
    steps = len(PLAN)
    return pl.pallas_call(
        gather_kernel,
        out_shape=jax.ShapeDtypeStruct((SLOTS, UNITS, UNIT, 256), jnp.bfloat16),
        in_specs=[pl.BlockSpec(memory_space=pltpu.HBM)] * 2,
        out_specs=pl.BlockSpec(memory_space=pltpu.VMEM),
        scratch_shapes=[
            pltpu.VMEM((8, 128), jnp.float32),
            pltpu.VMEM((8, 128), jnp.float32),
            pltpu.SemaphoreType.DMA((6, steps)),
            pltpu.SemaphoreType.DMA((6, steps)),
            pltpu.SemaphoreType.DMA((2 * bins,)),
            pltpu.SemaphoreType.DMA((2,)),
        ],
        compiler_params=pltpu.CompilerParams(
            collective_id=0, has_side_effects=True, vmem_limit_bytes=24 << 20
        ),
        name="gather_blocks",
    )(re, im)


GROUP = 3


def gain_row(tile):
    wide = tile.astype(jnp.float32)
    return wide[0:1, :128] + wide[1:2, :128] + wide[2:3, :128]


def cross_kernel(order, held, out):
    step = pl.program_id(0)
    own_row = gain_row(held[0, UNITS - 1]) * (1.0 / 16.0)
    own_column = jnp.broadcast_to(own_row, (128, 128)).T
    for j in range(GROUP):
        slot = order[step * GROUP + j]
        weight = own_column * gain_row(held[slot, UNITS - 1])
        for f in range(out.shape[0]):
            mine = held[0, pl.ds(16 * f, 16)].reshape(256, 256)
            other = held[slot, pl.ds(16 * f, 16)].reshape(256, 256)
            full = lax.dot_general(
                mine, other, (((1,), (1,)), ((), ())), preferred_element_type=jnp.float32
            )
            out[f, j, :, :128] = (full[:128, :128] + full[128:, 128:]) * weight
            out[f, j, :, 128:] = (full[128:, :128] - full[:128, 128:]) * weight


def local(spec_re, spec_im, offsets):
    bins, rows, segs = spec_re.shape
    tiles = rows // UNIT
    re = spec_re.reshape(bins, tiles, UNIT, segs)
    im = spec_im.reshape(bins, tiles, UNIT, segs)
    held = gathered(re, im)
    cross = pl.pallas_call(
        cross_kernel,
        grid_spec=pltpu.PrefetchScalarGridSpec(
            num_scalar_prefetch=1,
            grid=(SLOTS // GROUP,),
            in_specs=[pl.BlockSpec(memory_space=pltpu.VMEM)],
            out_specs=pl.BlockSpec((bins, GROUP, rows, 256), lambda i, order: (0, i, 0, 0)),
        ),
        out_shape=jax.ShapeDtypeStruct((bins, SLOTS, rows, 256), jnp.float32),
        compiler_params=pltpu.CompilerParams(vmem_limit_bytes=30 << 20),
        name="cross_products",
    )(offsets[0], held)
    return cross[:, None]


def solution(mesh):
    placed = (P("fr", ("sr", "sc"), None), P("fr", ("sr", "sc"), None), P(("sr", "sc"), None))
    return jax.shard_map(
        local,
        mesh=mesh,
        in_specs=placed,
        out_specs=P("fr", ("sr", "sc"), None, None, None),
        check_vma=False,
    )
```

time: 500 us -> 101 us (0.20)
  waiting for transfers between devices: 355 us -> 0 us
  Pallas kernels: 0 us -> 97 us
  local copies, waits for them, and re-layouts: 52.3 us -> 1.92 us
  matrix products: 42.4 us -> 0 us
  other arithmetic: 28.1 us -> 0 us
  starting transfers between devices: 20.1 us -> 0 us
    ppermute x6 -> x0, waiting for transfers between devices: 179 us -> none  [passed_along(): lax.ppermute(array, axis, [(i, (i + by) % size) for i in range(size)])]
    all_to_all x1 -> x0, waiting for transfers between devices: 175 us -> none  [sent_to_all(): return lax.all_to_all(copies, axis, split_axis=0, concat_axis=0, tiled=True)]
    pallas_call x0 -> x2, Pallas kernels: none -> 97 us  [the longest x1 85.9 us: gathered(): pl.pallas_call(gather_kernel, out_shape=jax.ShapeDtypeStruct((SLOTS, UNIT...]
    dot_general x4 -> x0, matrix products: 42.4 us -> none  [multiply(): jnp.einsum('fis,mfjs->fmij', left_side, other, preferred_element_type=jnp...]
    select_n x1 -> x0, local copies, waits for them, and re-layouts: 18.1 us -> none  [local(): cross = jnp.take(joined, slot_order, axis=1)]
    gather x2 -> x0, local copies, waits for them, and re-layouts: 15.2 us -> none  [the longest x1 14.7 us: local(): cross = jnp.take(joined, slot_order, axis=1)]
    concatenate x4 -> x0, other arithmetic: 12.8 us -> none  [the longest x1 12.1 us: local(): joined = jnp.concatenate([real_part * weight, imag_part * weight], axis=-1)]
    select_n x4 -> x0, other arithmetic: 12.2 us -> none  [the longest x2 12.1 us: local(): cross = jnp.take(joined, slot_order, axis=1)]
  transfers between devices with their start and end apart: 7 -> 0, of which waited for: 5 -> 0; matrix products, arithmetic and copies ran while one was open for 3% -> 0% of each run, Pallas kernels for 0% -> 0%
where the time goes in v1:
time: 101 us; the launch traced here: 99 us
  Pallas kernels  97 us (96%)
  local copies, waits for them, and re-layouts  1.92 us (2%)
    pallas_call x1, Pallas kernels, gathered(): pl.pallas_call(gather_kernel, out_shape=jax.ShapeDtypeStruct((SLOTS, UNIT...  85.9 us
    pallas_call x1, Pallas kernels, local(): pl.pallas_call(cross_kernel, grid_spec=pltpu.PrefetchScalarGridSpec(num_s...  11.1 us

profile of v1, /device:TPU:30, one launch (start us, length us, event | category | flops | bytes accessed | tf_op | source)
XLA Modules:
  0.0 99.0 jit_solution(1684560992211987204)
XLA Ops:
  0.0 0.0 copy-start.2
  0.0 0.0 copy-start
  0.0 1.0 copy-done
  1.0 0.0 copy-start.1
  1.0 0.9 copy-done.1
  1.9 85.9 %gather_blocks.1.held = bf16[33,65,16,256]{3,2,1,0:T(8,128)(2,1)S(1)} custom-call(bf16[4,8,16,256]{3,2,1,0:T(8,128)(2,1)S(1)} %bitcast.6, bf16[4,8,16,256]{3,2,1,0:T(8,128)(2,1)S(1)} %bitcast.7), custom_call_target="tpu_custom_call" | custom-call | tf_op jit(solution)/shard_map/gather_blocks/pallas_call | solution.py:224
  87.9 0.0 copy-done.2
  87.9 11.1 %cross_products.1 = f32[4,33,128,256]{3,2,1,0:T(8,128)} custom-call(s32[33]{0:T(128)S(1)} %bitcast.8, bf16[33,65,16,256]{3,2,1,0:T(8,128)(2,1)S(1)} %gather_blocks.1.held), custom_call_target="tpu_custom_call" | custom-call | tf_op jit(solution)/shard_map/cross_products/pallas_call | solution.py:275
Async XLA Ops:
  0.0 87.9 %copy-start.2 = (s32[1,33]{1,0:T(1,128)S(1)}, s32[1,33]{1,0:T(1,128)}, u32[]{:S(2)}) copy-start(s32[1,33]{1,0:T(1,128)} %param.5) | copy-start | bytes 400
  0.0 1.0 copy-start
  1.0 0.9 copy-start.1

commit v2 on v1

v2 whole, which is shorter than its diff:
```python
import functools
import math

import jax
import jax.numpy as jnp
from jax import lax
from jax.experimental import pallas as pl
from jax.experimental.pallas import tpu as pltpu
from jax.sharding import PartitionSpec as P

MESH = pl.DeviceIdType.MESH

PLAN = (
    (
        0x0027000d000d0000ffffffffffffffffffffffffffffffffffffffffffffffff,
        0x000d0027001a0000000d000d000d0027001a000d00270027ffffffffffffffff,
        0x000dffffffffffff001affffffffffff0000ffffffffffff001affffffffffff,
        0x000d001a0027ffff001a000d0027ffff000d000d001affff0000001a0000ffff,
        0xffffffffffffffffffffffffffffffffffffffffffffffffffffffffffffffff,
        0x00270000000000270027000d0000000d000d0027001a001a00270027000d001a,
    ),
    (
        0x000000000027001affffffffffffffffffffffffffffffffffffffffffffffff,
        0x00000000000d001a0000001a0000001a00000000000d000dffffffffffffffff,
        0x0000ffffffffffff0027ffffffffffff0027ffffffffffff000dffffffffffff,
        0x00000027000dffff0000001a001affff00270000000dffff001a000d0027ffff,
        0xffffffffffffffffffffffffffffffffffffffffffffffffffffffffffffffff,
        0x001a000d0027001a001a0000001a001a0027001a0000000d000d001a0027000d,
    ),
    (
        0x04370410041004370437041d0410041d041d0437042a042a04370319041d042a,
        0x04370410041004370437041d0410041d041d0437042a042a04370437041d042a,
        0x04370410041004370437041d0410041d041d0437042a042a04370437041d042a,
        0x04370410041004370437041d0410041d041d0437042a042a04370437041d042a,
        0xffffffffffffffffffffffffffffffffffffffffffffffffffffffffffffffff,
        0x000d001a001a000d000d002700270000001a000000270027001a000000000027,
    ),
    (
        0x042a041d0437042a042a0410042a042a0437042a0410041d033304370437041d,
        0x042a041d0437042a042a0410042a042a0437042a0410041d041d042a0437041d,
        0x042a041d0437042a042a0410042a042a0437042a0410041d041d042a0437041d,
        0x042a041d0437042a042a0410042a042a0437042a0410041d041d042a0437041d,
        0xffffffffffffffffffffffffffffffffffffffffffffffffffffffffffffffff,
        0x003400340034003400340034000d002700340034003400340034003400340034,
    ),
    (
        0x041d042a042a041d041d043704370410042a0410043704370743071c071c0743,
        0x041d042a03f6041d041d0437043704100367045e03e9046b042a041004100437,
        0x03cf042a042a04fa041d0514051404fa042a0521051405210521053b071c04fa,
        0x041d042a042a041d041d04370514053b042a045e043705210743041004780743,
        0xffff0478045104fa053b04780514053b053bffff047805210521053b071c0743,
        0x00000027000d00000000001a003400340000000d000d00000000000d001a0000,
    ),
    (
        0x044404440444044404440444041d043704440444044404440736041007430736,
        0x044404440444044404440444045e045104440444044404440444044404440444,
        0x04440444044404ed04440521053b04ed04440514052e04fa0444071c052e0743,
        0x044404440444044404440444041d052e044404440444052e0444044404440736,
        0xffff046b045e04ed052e0521053b0451052e0514052e04e00736052e052e052e,
        0x012b012b0111011e03190333032603260333033303190326036703dc03e90437,
    ),
    (
        0x0326030c0326031903330326030c0319035a03cf046b0451042a044404440437,
        0x01110478045104ed0111046b03e904fa053b03cf046b04fa03e9053b03dc04e0,
        0x041d030c012b044403cf04370437052e052e04100437043703e9052e07430521,
        0x0111011e045e0111052e0521045e0437053b0514046b0437053b045e05140521,
        0xffffffffffff0451ffffffff0451ffffffffffff046b0451053b045e051404fa,
        0x0111011e012b011103330326030c03190104011e03330319035a03f603dc0444,
    ),
    (
        0x03dc0437006800d00410042a044404440410041d041d04100680073607360729,
        0x035a03e9046b046b04d3045e0444044404e0046b051404100410041d042a0410,
        0x041004370104041d0410052e04fa0521063f053b053b0514041006db04100729,
        0x0410045e046b04100521045e044405550410046b053b05140736053b042a0729,
        0xffffffff04b9046b0478052e04780521045e053b053b05140729073607360729,
        0x011e01040104004e0326030c03330333036703e9004e04440104041004440410,
    ),
    (
        0x031900410319004e07290743073607360743074307290736077707ec07500444,
        0x0403048504b90478054805480478045e0104011e0111012b077707ec07f90847,
        0x0403053b041d050705210743054807360104054804e00507011e041d042a0444,
        0x053b053b0521030c0729048504850548054806180111055501040319012b0410,
        0xffff04850485050705480548054805480548054804e004ed0750075007500750,
        0x013801380068030c0340034003400444035a03cf0111041003e90444042a030c,
    ),
    (
        0x034003400333030c07430736071c03330367048507430485076a041d042a0410,
        0x0410052e048504850374012b005b0507046b03f605620485076a080607ec0854,
        0x053b052e0138012b054807360736072903cf04ed041d04100548054805480548,
        0x0521052e053b0138046b074304780736022f030c048506320673054804850548,
        0xffffffff04ac0485046b048504850507046b04ed048505070548054805480548,
        0x03400340013803330367012b011104370326030c0041004e030c041d004e00dd,
    ),
    (
        0x0381004e00a900c30736071c0743049f037403f6049f03330410080607f90507,
        0x034d04510104013804e0056205620104004e0111004e011e0548056204ed04b9,
        0x052e0514051404d3030c071c074304440111052e054805480326041008540410,
        0x052e05140514012b0743030c0111074305140451045e0410035a030c03740437,
        0xffffffff049f049f0492045e049f04e005d705620548054805e4070206320625,
        0x0104033303190319030c0319031901040374034003f600c3041003cf03190041,
    ),
    (
        0x034d0333049f04ac07020750075004c60673034004ac072903e9048504b90750,
        0x054800ea040304d304ed04ed011105e403cf049f03f6057c0514056f083a0820,
        0x03f6054804ed071c07360750034004d3074307430340033306250702062504d3,
        0x0548054806320562037407500743056f03260340054805480666048506320485,
        0x046b04e0063204ac04ed04ed05bd056f057c04fa06590702069a056f06180514,
        0x030c011103400326035a03f6005b030c03cf03f603400333034d01110111022f,
    ),
    (
        0x007500750075005b077706f506e804b90736071c04b904c6034d03cf07ec04e0,
        0x03f6056204780104021506320485005b049200dd00410152048503e904b905e4,
        0x0548075006180548021506f506e803400326034005210854034002220403022f,
        0x045e0562054807430485063f0319085406660743015f0340034d01450340046b,
        0x04fa057c04c604c60485063204e0057c0492048504d305fe066606b406e80618,
        0x0326032603330410021503cf03e9034003e903dc0326034003dc03e90403016c,
    ),
    (
        0x040303dc04c604c60680072907290485034d0319034d049f069a034d046b04b9,
        0x004e04d30548055505140555058905890374050704ed049f05070813058904c6,
        0x063f07430729074307500319040305140632071c03cf01c703dc034007500847,
        0x051406320618057c04510632063f0485030c031907290854056f06180451035a,
        0x04d3056f063f05620507050706250589056f056f04ed060b063f061806660589,
        0x02cb030c00ea034003cf03e903dc0410030c031903cf030c0374004103cf01e1,
    ),
    (
        0x03f603e9009c006806db07020784071c0702038103cf040303dc06a7037403b5,
        0x0507056f009c008f064c0589049f015f0485015201380138075d05a30492046b,
        0x051405210750051406db07020729023c030c022f04d3020801d405e403260340,
        0x07500618064c055506800381046b057c047806320326020803740326034d0680,
        0x0632061806db0555064c04b906e8060b05e405f105070589068d064c063f0680,
        0x031903190326044403dc02ff04030381034d0381015f040302080145037403b5,
    ),
    (
        0x050704ac049203c2067307df07f90750030c02ff073603e9025602f2081307b8,
        0x006800dd058905f104ac02ff050705d702ff0555050705fe0596038e04c6060b,
        0x071c0736050705f106f503f602ff084703f6070202150632051403f6020804ed,
        0x0673052107290589026307290367045e016c057c075004850659064c0521022f,
        0x050704ac064c05f106b404ac0680078405f106a7057c05f1063205e404c606e8,
        0x033303dc030c042a03f603b503a802d8027d02ff03b503dc038103c201ee035a,
    ),
    (
        0x0249002703e9008f079106a7049207f9079106a70492080606c107f903cf0451,
        0x049f0555008f01ba007504c600d0016c034d00ea018601fb0784057c04fa049f,
        0x0750062504fa0702072906320521020805d702cb081301fb01e101e10111030c,
        0x071c074306250729071c02150673058907770249034d068d022f022201450208,
        0x070f05f104920589056f04920507068004fa0507068d06f5064c05b0070207b8,
        0x0179040303f6043702d8038103b5035a024902cb034d020801e1038e01450367,
    ),
    (
        0x02cb005b02cb03b506f507f904ac04ac02490492080602b10784045e07d20297,
        0x00c3016c04fa015200f700f705bd060b04fa038e04c6058904ed055505070492,
        0x0736070f06db061800dd021501fb082005e403dc03f606f50618020804fa0514,
        0x0736062507430618036705890249035a035a04b9068d01520548063f06590381,
        0x05fe06250625067305fe06c1078405d704d304b90673076a0589063f065905a3,
        0x023c03f603dc039b03c2021502ff03cf0319022f035a02b1029701e103b50256,
    ),
    (
        0x0492009c008f004106c103c204b90784068d05a303b5079103a803b504c6076a,
        0x04c606e8018605d7070f04920208015201e1056f00d005f105bd0507065905a3,
        0x072905d70625082005fe070f07ec02d802e507df050703cf0222023c04ed01e1,
        0x056f07500736068d056f027d063208200743015f016c0791058902560208045e,
        0x0492070f0702061806c1067304b9079e06c1068d05f106e8050705a3068d06ce,
        0x020803cf0410015f016c01e101fb015202d801d403dc036703a802560410038e,
    ),
    (
        0x049f00f700b600ea06b406c104c603a8028a038e06e804b90297079e07ab06ce,
        0x028a008200d0019303c2009c04fa055503c201ad01ba04c605a3069a060b05d7,
        0x00dd05a30743075000f702cb021505d706c100ea02cb07ec04fa060b02ff0702,
        0x05890736027d076a016c067303b50152027d01ad0555076a023c0270056f0562,
        0x056f05a306c1070205a305a3049206b4079107d205bd068d04fa069a050704b9,
        0x028a03e901ee041d039b042a01c70208028a04030186034d016c00d0026302a4,
    ),
    (
        0x04fa006803a800b607ec03b507b8079e06c1050706f50702028a036702ff0403,
        0x070f070f00b6049206e8056f010402be00ea04b9049f004e03a8049205ca0702,
        0x074306f50403072906b407f903a802e500c303f6061803e9011102e5050705fe,
        0x023c072906800666073603190326046b06730215035a049f014500410104016c,
        0x05d706b4066606f504b904c60562070205bd049206f50791045e049205ca06c1,
        0x03cf0263018602d802970444039b028a02ff041d038103cf02be043702cb02ff,
    ),
    (
        0x008204b900ea049f04ac0478049f045104ed034d034003670507035a018602be,
        0x06f5009c0041017902a403a8019301c70145039b007500ea06c106660485069a,
        0x06db080607ec07ec020801e100d001c701c707f900f700ea00f70111010400ea,
        0x07290249071c045e0104023c01040673005b01380068045101790000023c0555,
        0x059605e40659065905ca04d3063204c605ca05a3049f04c6046b04b904ed0492,
        0x035a044403e902ff03b5027002be02be03f602b1038e03a8015201c701860186,
    ),
    (
        0x054803190082039b02b104b903a8027003c2069a076a057c039b03a808200179,
        0x01fb04c605d7011e015f004106b406f501ee004e005b005b069a0659057c057c,
        0x01ee081308060319070f01040813081304e000f70319060b00ea04ed013802e5,
        0x03670256023c04850410075d076a0270001a07b8076a026302080034005b0179,
        0x05ca06e80507049204ac07ec04c604d3045105ca04ac04ac05ca04ed04e005b0,
        0x03f6043703b502be028a028a02b102970193038e03c2042a01a002b102be03e9,
    ),
    (
        0x052e03c2045e04780297075d07ab0743048501ee02e501520659072901ee0186,
        0x0249015202f202ff071c071c027001a001d40068060b015f047804b903e90562,
        0x0618021507df0854011100f70111011e01d40806020800f7003400d000f70625,
        0x0625058907840340025602b1005b01040784035a004e057c00270777001a012b,
        0x06b4070207df0777045e056204d304b904ac0451063f0478048506db05bd04c6,
        0x03dc03c202be03a8038e038e042a02ff041d043703670270041d01ee0437012b,
    ),
    (
        0x04d3052e046b0521070f02a4045e04ed06db07df063206b4016c019306b406db,
        0x07360729071c04c6011e02700736069a005b015f00dd055507b803c20451052e,
        0x030c07df03c20326077707c506f5069a076a030c011106c1056f011e023c00d0,
        0x024901930333083a0806081307ec071c03670806078403b50555008207d20104,
        0x04b90777057c04b9058906180589048504ed04d306b4055504d304ac0478049f,
        0x03e9042a042a0381044403a80437034d042a039b041002630437027d038103cf,
    ),
    (
        0x04c60485052104fa014507c5070f06e802e502cb033302f20729078403dc0333,
        0x02ff007500ea01ad0750075001380270015f019300f7018605f1079e068d04d3,
        0x050700d007f9079e01520111039b02a401520813079e0444000001d4034000dd,
        0x064c07ec07910333011e00a9004e034007f9015201e107b8003402a400340145,
        0x04c605ca04d3060b0632057c079104920507070206ce0806062504fa0680045e,
        0x04370410043701a0041d0410041d03f604370367044403c203b5039b029703dc,
    ),
    (
        0x03a8020802560485075d01ad06f5072905a3075006a706c1035a03260729063f,
        0x074304fa05a3053b023c013805fe04ac016c0659065901c7079105f1045e04fa,
        0x05e407f900d007f9058905d706ce07b804fa011101ad06db010401ee07ab057c,
        0x01ad081305620854057c071c0784062501c707ec052e0333063f065902b1015f,
        0x056207ab0673069a04fa07ab057c07ec048506f5070f06ce06db049f057c060b,
        0x04100374038e02a4041002be028a0193039b035a01d4043700d0005b01a0034d,
    ),
    (
        0x0222032603400340035a07ab047806c103f603e904d3028a068d06b4032606e8,
        0x012b027001e100dd04fa050701ad0138008201d400c30736052107f9049f0666,
        0x031901e1070f03a80186030c031905f100a9064c05fe071cffff073601ee01d4,
        0x07ec018601fb020801ee011e062503a8068d011102080777013800a9ffff06ce,
        0x06ce064c05b00813060b075d04ac07f9064c05960555ffff06c1ffffffffffff,
        0x0444018603c20186020801d40208ffff008f01ee01c7ffff00a9ffffffffffff,
    ),
    (
        0xffffffffffffffff07c5027d079effff06e8070fffffffff03c2027dffffffff,
        0x0562ffffffffffff045e0222ffffffffffffffffffffffff03dc0451ffffffff,
        0xffff0854030c05feffff0596ffffffffffff0249ffffffffffffffffffffffff,
        0x05ca064cffff0847ffffffffffffffffffffffffffffffffffffffffffffffff,
        0x06e805d7ffffffffffffffffffffffffffffffffffffffffffffffffffffffff,
        0x042a0270ffffffffffffffffffffffffffffffffffffffffffffffffffffffff,
    ),
    (
        0xffffffffffffffff0367ffffffffffffffffffffffffffffffffffffffffffff,
        0xffffffffffffffffffffffffffffffffffffffffffffffff05feffffffffffff,
        0xffff07ecffffffffffffffffffffffffffffffffffffffffffffffffffffffff,
        0xffffffffffff0820ffffffffffffffffffffffffffffffffffffffffffffffff,
        0xffffffffffffffffffffffffffffffffffffffffffffffffffffffffffffffff,
        0x041dffffffffffffffffffffffffffffffffffffffffffffffffffffffffffff,
    ),
)

FIRST_LAG, LATER_LAG, FIRST_STEPS = 2, 3, 4
GAIN_STEP = 2
SLOTS = 33
UNITS = 65
UNIT = 16
STARTS = (0, 13, 26, 39, 52)
OPPOSITE = (1, 0, 3, 2, 5, 4)
NOTHING = 0xFFFF


def lag(step):
    return FIRST_LAG if step < FIRST_STEPS else LATER_LAG


SIZES = dict(zip(STARTS, (b - a for a, b in zip(STARTS, STARTS[1:] + (UNITS,)))))


def size_of(entry):
    return 0 if entry == NOTHING else SIZES[entry % UNITS]


def neighbour_position(p, d):
    x, y = divmod(p, 4)
    if d == 0:
        x = (x + 1) % 4
    if d == 1:
        x = (x + 3) % 4
    if d == 2:
        y = (y + 1) % 4
    if d == 3:
        y = (y + 3) % 4
    return 4 * x + y


def signed(word):
    return word - (1 << 32) if word >= 1 << 31 else word


def entries(step, d):
    return [(PLAN[step][d] >> (16 * p)) & 0xFFFF for p in range(16)]


def mask_of(flags):
    return sum(1 << p for p, flag in enumerate(flags) if flag)


def gather_kernel(re_ref, im_ref, held, part, part_in, send_sem, recv_sem, load_sem, pair_sem):
    bins = re_ref.shape[0]
    tiles = re_ref.shape[1]
    fr = lax.axis_index("fr")
    sr = lax.axis_index("sr")
    sc = lax.axis_index("sc")
    z, x, y = sr // 4, sr % 4, sc
    p = 4 * x + y
    steps = len(PLAN)

    loads = []
    for f in range(bins):
        for i, ref in enumerate((re_ref, im_ref)):
            unit = (2 * f + i) * tiles
            loads.append(
                pltpu.make_async_copy(ref.at[f], held.at[pl.ds(unit, tiles)], load_sem.at[2 * f + i])
            )
    for load in loads:
        load.start()

    xp, xm = (x + 1) % 4, (x + 3) % 4
    yp, ym = (y + 1) % 4, (y + 3) % 4
    zp, zm = (z + 1) % 4, (z + 3) % 4
    targets = (
        (fr, 4 * z + xp, y),
        (fr, 4 * z + xm, y),
        (fr, sr, yp),
        (fr, sr, ym),
        (fr, 4 * zp + x, y),
        (fr, 4 * zm + x, y),
    )
    ahead = (4 * (xp - x), 4 * (xm - x), yp - y, ym - y, 16, -16)
    twin = (1 - fr, sr, sc)
    shift = 16 * (y % 2)

    barrier = pltpu.get_barrier_semaphore()
    for device in targets + (twin,):
        pl.semaphore_signal(barrier, inc=1, device_id=device, device_id_type=MESH)
    for load in loads:
        load.wait()
    pl.semaphore_wait(barrier, 7)

    def chosen(step, d):
        words = [jnp.int32(signed((PLAN[step][d] >> (32 * i)) & 0xFFFFFFFF)) for i in range(8)]
        words = [jnp.where(y < 2, words[i], words[i + 1]) for i in range(0, 8, 2)]
        word = jnp.where(
            x < 2,
            jnp.where(x == 0, words[0], words[1]),
            jnp.where(x == 2, words[2], words[3]),
        )
        return lax.shift_right_logical(word, shift) & 0xFFFF

    def guarded(mask, action):
        if mask == 0:
            return
        if mask == 0xFFFF:
            action()
            return
        pl.when((lax.shift_right_logical(jnp.int32(mask), p) & 1) == 1)(action)

    def transfer(step, d, source, target, size):
        return pltpu.make_async_remote_copy(
            src_ref=held.at[pl.ds(source, size)],
            dst_ref=held.at[pl.ds(target, size)],
            send_sem=send_sem.at[d, step],
            recv_sem=recv_sem.at[d, step],
            device_id=targets[d],
            device_id_type=MESH,
        )

    def for_each_size(sizes, action):
        for size in sorted(set(sizes) - {0}):
            guarded(mask_of(v == size for v in sizes), functools.partial(action, size))

    def send(step, d):
        def action(size):
            source = chosen(step, d)
            transfer(step, d, source, source - UNITS * ahead[d], size).start()

        for_each_size([size_of(v) for v in entries(step, d)], action)

    def receive(step, d):
        sent = [size_of(v) for v in entries(step, d)]
        coming = [sent[neighbour_position(q, OPPOSITE[d])] for q in range(16)]
        for_each_size(coming, lambda size: transfer(step, d, 0, UNITS, size).wait_recv())

    def finish(step, d):
        sent = [size_of(v) for v in entries(step, d)]
        for_each_size(sent, lambda size: transfer(step, d, 0, UNITS, size).wait_send())

    exchange = pltpu.make_async_remote_copy(
        src_ref=part,
        dst_ref=part_in,
        send_sem=pair_sem.at[0],
        recv_sem=pair_sem.at[1],
        device_id=twin,
        device_id_type=MESH,
    )

    for step in range(steps + LATER_LAG):
        for earlier in range(steps):
            if earlier + lag(earlier) == step:
                for d in range(6):
                    receive(earlier, d)
        if step < steps:
            for d in range(6):
                send(step, d)
        if step == 0:
            total = jnp.zeros((tiles, UNIT, 256), jnp.float32)
            for i in range(2 * bins):
                piece = held[pl.ds(i * tiles, tiles)].astype(jnp.float32)
                total += piece * piece
            total = total.reshape(tiles * UNIT, 256)
            half = total[:, :128] + total[:, 128:]
            power = jnp.sum(half.T, axis=0, keepdims=True)
            part[...] = jnp.broadcast_to(power, part.shape)
            exchange.start()
        if step == GAIN_STEP:
            exchange.wait()
            power = part[...] + part_in[...]
            gain = 1.0 / jnp.sqrt(power * (1.0 / 2048.0))
            gain = jnp.concatenate([gain, gain], axis=0)
            gain = jnp.concatenate([gain, gain], axis=1)
            high = gain.astype(jnp.bfloat16).astype(jnp.float32)
            middle = (gain - high).astype(jnp.bfloat16).astype(jnp.float32)
            low = gain - high - middle
            row = lax.broadcasted_iota(jnp.int32, (UNIT, 256), 0)
            rest = jnp.where(row == 1, middle, low)
            held[UNITS - 1] = jnp.where(row == 0, high, rest).astype(jnp.bfloat16)
    for step in range(steps):
        for d in range(6):
            finish(step, d)


def gathered(re, im):
    bins, tiles = re.shape[:2]
    steps = len(PLAN)
    return pl.pallas_call(
        gather_kernel,
        out_shape=jax.ShapeDtypeStruct((SLOTS * UNITS, UNIT, 256), jnp.bfloat16),
        in_specs=[pl.BlockSpec(memory_space=pltpu.HBM)] * 2,
        out_specs=pl.BlockSpec(memory_space=pltpu.VMEM),
        scratch_shapes=[
            pltpu.VMEM((8, 128), jnp.float32),
            pltpu.VMEM((8, 128), jnp.float32),
            pltpu.SemaphoreType.DMA((6, steps)),
            pltpu.SemaphoreType.DMA((6, steps)),
            pltpu.SemaphoreType.DMA((2 * bins,)),
            pltpu.SemaphoreType.DMA((2,)),
        ],
        compiler_params=pltpu.CompilerParams(
            collective_id=0, has_side_effects=True, vmem_limit_bytes=24 << 20
        ),
        name="gather_blocks",
    )(re, im)


GROUP = 11
RING = 3


def gain_row(tile):
    wide = tile.astype(jnp.float32)
    return wide[0:1, :128] + wide[1:2, :128] + wide[2:3, :128]


def cross_kernel(order, held, out, staged, own_column, sems):
    bins = out.shape[0]
    own_row = gain_row(held[UNITS - 1]) * (1.0 / 16.0)
    own_column[...] = jnp.broadcast_to(own_row, (128, 128)).T

    def store(buffer, slot):
        return pltpu.make_async_copy(staged.at[buffer], out.at[:, slot], sems.at[buffer])

    def group(i, carry):
        for j in range(GROUP):
            buffer = (i % RING) * GROUP + j

            @pl.when(i >= RING)
            def _():
                store(buffer, 0).wait()

        for j in range(GROUP):
            buffer = (i % RING) * GROUP + j
            first = order[i * GROUP + j] * UNITS
            weight = own_column[...] * gain_row(held[first + UNITS - 1])
            for f in range(bins):
                mine = held[pl.ds(16 * f, 16)].reshape(256, 256)
                other = held[pl.ds(first + 16 * f, 16)].reshape(256, 256)
                full = lax.dot_general(
                    mine, other, (((1,), (1,)), ((), ())), preferred_element_type=jnp.float32
                )
                staged[buffer, f, :, :128] = (full[:128, :128] + full[128:, 128:]) * weight
                staged[buffer, f, :, 128:] = (full[128:, :128] - full[:128, 128:]) * weight
            store(buffer, i * GROUP + j).start()
        return carry

    groups = SLOTS // GROUP
    lax.fori_loop(0, groups, group, 0)
    for i in range(groups - RING, groups):
        for j in range(GROUP):
            store((i % RING) * GROUP + j, 0).wait()


def local(spec_re, spec_im, offsets):
    bins, rows, segs = spec_re.shape
    tiles = rows // UNIT
    re = spec_re.reshape(bins, tiles, UNIT, segs)
    im = spec_im.reshape(bins, tiles, UNIT, segs)
    re = pltpu.with_memory_space_constraint(re, pltpu.HBM)
    im = pltpu.with_memory_space_constraint(im, pltpu.HBM)
    held = gathered(re, im)
    cross = pl.pallas_call(
        cross_kernel,
        in_specs=[pl.BlockSpec(memory_space=pltpu.SMEM), pl.BlockSpec(memory_space=pltpu.VMEM)],
        out_specs=pl.BlockSpec(memory_space=pltpu.HBM),
        out_shape=jax.ShapeDtypeStruct((bins, SLOTS, rows, 256), jnp.float32),
        scratch_shapes=[
            pltpu.VMEM((RING * GROUP, bins, rows, 256), jnp.float32),
            pltpu.VMEM((rows, rows), jnp.float32),
            pltpu.SemaphoreType.DMA((RING * GROUP,)),
        ],
        compiler_params=pltpu.CompilerParams(vmem_limit_bytes=30 << 20),
        name="cross_products",
    )(offsets[0], held)
    return cross[:, None]


def solution(mesh):
    placed = (P("fr", ("sr", "sc"), None), P("fr", ("sr", "sc"), None), P(("sr", "sc"), None))
    return jax.shard_map(
        local,
        mesh=mesh,
        in_specs=placed,
        out_specs=P("fr", ("sr", "sc"), None, None, None),
        check_vma=False,
    )
```

time: 101 us -> 85.9 us (0.85); the launches traced: 99 us -> 85.7 us
  Pallas kernels: 97 us -> 85.7 us
  local copies, waits for them, and re-layouts: 1.92 us -> 0.01 us
    pallas_call x2, Pallas kernels: 97 us -> 85.7 us  [the longest x1 78.5 us: gathered(): pl.pallas_call(gather_kernel, out_shape=jax.ShapeDtypeStruct((SLOTS * UNI...]
    unnamed x6 -> x2, local copies, waits for them, and re-layouts: 1.92 us -> 0.01 us
where the time goes in v2:
time: 85.9 us; the launch traced here: 85.7 us
  Pallas kernels  85.7 us (100%)
    pallas_call x1, Pallas kernels, gathered(): pl.pallas_call(gather_kernel, out_shape=jax.ShapeDtypeStruct((SLOTS * UNI...  78.5 us
    pallas_call x1, Pallas kernels, local(): pl.pallas_call(cross_kernel, in_specs=[pl.BlockSpec(memory_space=pltpu.SM...  7.24 us

profile of v2, /device:TPU:30, one launch (start us, length us, event | category | flops | bytes accessed | tf_op | source)
XLA Modules:
  0.0 85.7 jit_solution(11975513638983748348)
XLA Ops:
  0.0 0.0 copy-start
  0.0 78.5 %gather_blocks.1.held = bf16[2145,16,256]{2,1,0:T(8,128)(2,1)S(1)} custom-call(bf16[4,8,16,256]{3,2,1,0:T(8,128)(2,1)} %bitcast.7, bf16[4,8,16,256]{3,2,1,0:T(8,128)(2,1)} %bitcast.8), custom_call_target="tpu_custom_call" | custom-call | tf_op jit(solution)/shard_map/gather_blocks/pallas_call | solution.py:439
  78.5 0.0 copy-done
  78.5 7.2 %cross_products.1 = f32[4,33,128,256]{3,2,1,0:T(8,128)} custom-call(s32[33]{0:T(128)S(1)} %bitcast.6, bf16[2145,16,256]{2,1,0:T(8,128)(2,1)S(1)} %gather_blocks.1.held), custom_call_target="tpu_custom_call" | custom-call | tf_op jit(solution)/shard_map/cross_products/pallas_call | solution.py:514
Async XLA Ops:
  0.0 78.5 %copy-start = (s32[1,33]{1,0:T(1,128)S(1)}, s32[1,33]{1,0:T(1,128)}, u32[]{:S(2)}) copy-start(s32[1,33]{1,0:T(1,128)} %param.5) | copy-start | bytes 400

commit v3 on v1

v3 whole, which is shorter than its diff:
```python
import functools
import math

import jax
import jax.numpy as jnp
from jax import lax
from jax.experimental import pallas as pl
from jax.experimental.pallas import tpu as pltpu
from jax.sharding import PartitionSpec as P

MESH = pl.DeviceIdType.MESH

PLAN = (
    (
        0x0020004000200000ffffffffffffffffffffffffffffffffffffffffffffffff,
        0x000000400020000000000040000000400040000000400040ffffffffffffffff,
        0x0040ffffffffffff0000ffffffffffff0020ffffffffffff0040ffffffffffff,
        0x004000400000ffff000000200040ffff002000200040ffff000000200040ffff,
        0xffffffffffffffffffffffffffffffffffffffffffffffffffffffffffffffff,
        0x0000002000000020004000200040002000200040002000200020004000200040,
    ),
    (
        0x0000000000400040ffffffffffffffffffffffffffffffffffffffffffffffff,
        0x002000000040004000200000002000000000004000000000ffffffffffffffff,
        0x0020ffffffffffff0020ffffffffffff0000ffffffffffff0000ffffffffffff,
        0x002000000040ffff002000000020ffff000000400000ffff004000000000ffff,
        0xffffffffffffffffffffffffffffffffffffffffffffffffffffffffffffffff,
        0x0020000000400040002000000020000000000000000000000040000000000000,
    ),
    (
        0x0060083008100830085008300850083008300850083008300830085008300850,
        0x0060083008100830085008300850083008300060083008300830085008300850,
        0x08100830081001c3085002440224020400600244020402440830020402440244,
        0x0810083000600830085000600060020400600060083002440830085008300244,
        0xffffffffffffffffffffffffffffffffffffffffffffffffffffffffffffffff,
        0x0810083008100830085008300850083008300850083008300830085008300850,
    ),
    (
        0x0040006000600060083008100830081008100810081008100850064c062c0810,
        0x0040006000600060006000600060006000600020006000600850081008100810,
        0x0060081008500850006002040244018300400204022402040060064c062c01c3,
        0x0060006000200850006000400000024400400810006002040060006000600204,
        0xffffffffffffffffffffffffffffffffffffffffffffffffffffffffffffffff,
        0x0830081008500850083008100830081008100810081008100850081008100810,
    ),
    (
        0x06ad089108b1099310601040106010401040106010401040060c0e3c0e1c0e3c,
        0x07af089108b109930224081000a109d30a540a340a5408b11040106010401060,
        0x07af062c102010400204104010600a3408100a340a5410400a34106010400e3c,
        0x0830089100c11040020408d10a1410400a540a340a540a340a3408b108d10a34,
        0xffff089108b10993ffff0a340a1409d30a540a340a540a340a340e3c0a340a34,
        0x004000c10060000000600040022400400040002000a100600000002000400060,
    ),
    (
        0x07af078f085008501040064c062c1020062c064c062c10201040106010201060,
        0x06ad078f08500850083000a1083008100810085008100a340a34102008d108b1,
        0x078f10400224024408301020104010400830106010400a34085010200a341060,
        0x022408100850024408300810083010200830085008101040085002040e1c1060,
        0xffffffffffffffffffff08d1ffff0a34ffffffff089108b1ffff08b108d108b1,
        0x00600040002000e1000000600060006002040060006000c1066c0264062c0020,
    ),
    (
        0x078f07cf07cf060c0ebd0fdf10400e3c102010201020060c1060102010401020,
        0x0830081007cf0a5400810081018300e101c30810089102640fdf0fbf10201020,
        0x08300f9f0fbf10600e3c02640e3c102001c31020102010200264022410201020,
        0x0e5c0e3c0e5c10600e3c0e5c0a34026400c100e10891102000c100e100a11020,
        0xffffffff0912093209b30fdf09b30a9508b109d30c180c3808b10c380e1c09b3,
        0x0850006008700810087008500000085008500830020408700810083008500870,
    ),
    (
        0x062c08d100e100e1060c060c060c0850085008300fbf09930fdf08300ebd0f9f,
        0x0a3408b10204093200c10a9509520a9508b101a30ab509930810083009320870,
        0x0e5c0204062c0e3c01c30fdf02640b9709b301830fbf09930c580fbf08500a34,
        0x062c08b1062c08100244060c0e3c0e3c04280a1408b10c380c580ab50c580870,
        0xffffffff0fbf09120fbf09930952ffff09b30ad50fbf0ad50c580ab50dbb0e3c,
        0x0870085008300060081008700870087000600870087000400060006000e10830,
    ),
    (
        0x06cd08b1089109320f9f087008910e1c0fdf0870087008700f9f0fbf08500870,
        0x00c10204089108f101830993026409b30a1409d3026408d108b10a7408500830,
        0x0a34085004280e1c0428099309b30e1c0e3c0fbf0e1c08700e7c08300fdf0870,
        0x02440a1400e10e1c0ebd08b10a54060c08b1024408d10e5c02640a740e3c0ab5,
        0x09d30f3e0ebd0edd0f9f0fbf0fbf0c580ebd0fbf0e1c0bd70f9f09b30fdf0bb7,
        0x0244087000c100a1026402640810026400c10183004001c3026400810060060c,
    ),
    (
        0x05ab00e1062c01c31080106008700fbf0e5c0f9f08b108d10e7c08d10ddb0830,
        0x09d309b300e1091200e102640a5402640264024408b100e10e9d0f9f0f9f0952,
        0x09d309b30fdf0c3802440fbf09d310600183087008700e1c03c70f9f0a140830,
        0x0cb90edd0ebd0edd0e9d02440e1c10600e5c0e1c0e3c02640a1402240a14066c,
        0x0cb90ddb0dbb0c380e9d0ebd0ab50ab50fdf0f9f0f9f09120fdf0ddb0ddb0f9f,
        0x00c1044800e101e3024401a300c100e1028500c1038700e103c7022401c300e1,
    ),
    (
        0x068d0850087008f110200ebd0edd10800f9f1080108008500e9d087008f11040,
        0x02040224093201a309b3087000e101e300c102850a140932087007cf08f11080,
        0x0e3c044810400264064c1080108010800a14104002641080087008700ddb1080,
        0x020402240a1402640c380ebd08100ab50264062c00e108d106ed0edd08f11040,
        0x0f1e0edd09320fdf08b10ab50edd0b360f9f0e1c09b309320e9d0f9f0f9f0952,
        0x020402240142087001e301e3010201e30870062c0850085008700870087000c1,
    ),
    (
        0x0850066c068d064c048910800d9b0ebd10600d9b0850066c10200ddb08701080,
        0x07cf02c508d1022401e30a14093200810850099307ef09d30a740f5e10600b97,
        0x0a541080108010200a740dbb10200a740e5c0f9f07ef09d30c180bd70870066c,
        0x0c99066c0a950c180e1c066c0891066c0e9d0e5c0a1410800a7408910e5c0ad5,
        0x0d9b0e5c0a950c1809120dbb0d9b0ad50d9b0d9b0a950bb70c180f5e09b30ad5,
        0x01830468068d02240081024400e1066c02640142016201e300c1014202640264,
    ),
    (
        0x00c1087008f1016208700d9b0fdf0870087008d1064c0ebd0870089109d308f1,
        0x089100e1087001e3078f02c50870087000e107ef01c302e507af0870087008f1,
        0x0e7c0e5c066c081008100d9b066c066c07ef0264064c062c0244099307af1040,
        0x068d06ad0244087000e100e108d1087000e104a9060c062c04e900810af50830,
        0x0891099309930f3e0f3e0f1e09320e9d0c780c990e9d09520f1e0a950af50fff,
        0x040805ab066c016200e10081018306cd00e10468064c02e504e907cf01620468,
    ),
    (
        0x083001a3093209b30fff09f30e7c066c074e066c0fff106007ef076e0fff0972,
        0x026408d102a50a74093209f30a950b160102026402e501620ebd108009d30ad5,
        0x02640a34040810800a54062c0fff08700c78062c1080106007af104010800264,
        0x02640a3402e50e7c04890e7c0e7c0ad5074e0e3c06ad10600870060c0c1808d1,
        0x0e1c0d3a0d9b0a950d9b0fff0a950b160fbf0dbb09120fbf0c380d5a0c180972,
        0x0264028502e501c30408062c06ad07cf07ef066c018303e707ef06ed00a1066c,
    ),
    (
        0x058b05ab06ed01420e5c0f9f0fff0e7c10800952066c0e3c08d107ef10800ebd,
        0x099301c301c30a95040807af09f308b108d1076e095209f30a540b9710800bd7,
        0x0204064c09930224040810600fdf04280e1c0bd70972066c078f0c78066c0d9b,
        0x0e7c0e5c0a54064c04e90e9d08f1064c0e1c0edd046808f10ebd0af50a7408f1,
        0x0c990fbf0cd90dbb0fff0e9d0f9f0af50efd0f1e09520c990c990b970c990b97,
        0x046801c30326058b048904c9068d0346074e076e01c3046806ed076e05eb054a,
    ),
    (
        0x066c064c00c100a10d3a0fff064c064c064c068d0edd08f110800d5a097207cf,
        0x00e102a5099302c501c3070e01620af507ef02e5085001420f1e095209720b76,
        0x0e1c0fff0b9701e30d9b0b9709930edd066c01a30d9b0a740c380e7c04680c58,
        0x066c04080cd902e50e5c044806cd0edd0a7404c90e5c0af5068d06ed064c04e9,
        0x09320d1a0b970fff0d1a093209d30ebd0cd90bd70b360ebd09120bd70f5e0c18,
        0x00e1040801c302e506ed0408016200c10081016202e506ed02e5048904680244,
    ),
    (
        0x070e070e078f097205ab05eb091208910fff0e3c097209720fbf08f105eb0fbf,
        0x08b10a54018302e50a340ab50ad502040b360a14078f03060fff0af50c180b36,
        0x09b305eb0bb7064c01e305eb0e7c062c03870e7c0fdf0264062c09f301e3060c,
        0x0c180a95066c0366008104080efd0efd0468044802e50e7c08b102e50c380efd,
        0x08b10cb90c780bb70a95095209f30fbf0b360f3e0c580fdf0ab50ebd09320a95,
        0x078f02c506ed06ad046802e502e503a702c507cf052a076e074e05ab01420204,
    ),
    (
        0x03c7008100a10122058b0e3c0efd09720efd07cf0dfb03460bd70f3e0efd0952,
        0x081009520af5072e09d308910b160b5601e302a5018301220bf70f3e0b760bf7,
        0x0a7409d30ddb0bd70e7c0f9f03a70e5c0204064c0bf70f9f042805ab05ab054a,
        0x04480cb90edd02c504c90cd90ebd0c780e3c0489064c06ed02440489068d06ed,
        0x0d5a09520dfb0cb90fdf0f7e0b160cb90b560b970edd0b3609520d9b0cb90912,
        0x04c902e501e305cb02c503c703c7058b010205eb05ab0346076e056a008107cf,
    ),
    (
        0x012206ad010200810d5a0edd0dfb0efd05eb0e7c07cf076e070e0efd076e0e5c,
        0x01a309120a740b56072e012208d10ad50183097201a30102095209720ab50e9d,
        0x0d9b0b970448058b046801e30a540fdf0bb701c304680428044803a70dbb0387,
        0x06ed0efd0a340c780e7c06cd04a908f104c9068d0e9d0efd0e9d04e904e906cd,
        0x0b3609120f5e0fbf0b160b970f1e0c9909720b560bd70dfb09320edd0b560c38,
        0x06ed07cf03c7044801830162042804c902e504c9076e07ef018304e9076e074e,
    ),
    (
        0x07cf052a072e07ef0d7a0f7e0e5c0f1e07cf0f3e0ebd0efd0f5e0dbb0b3606ad,
        0x02a5058b09520b1609f309320912036601a3016208d10af509120fff0fbf09d3,
        0x0c780d9b0c7809f30c58066c04680bf7058b0dbb0b970dfb0b97062c02040c78,
        0x08f10c1808d1068d0c780cb9099308910972087004c9081004890c580cb90264,
        0x0f7e0b360edd0f9f0d3a0bb70f3e09720ab50d1a0f5e0ab50b560c180b360cd9,
        0x03a704e9060c068d04c9048903a7078f076e056a03660366030603e706cd0183,
    ),
    (
        0x0285050a05ab09120dfb0dbb0ebd0e9d0346056a06ed07cf064c08b106ad0fdf,
        0x01420b1603260bf702e5054a028508500081070e00c103870f7e0efd0b560932,
        0x0a140fbf0f9f0fbf0c38074e0dfb08500ddb05ab01a307af0468060c0bd705ab,
        0x0e1c0b970af50ebd0af5048904c904e9038700a10cf906cd00810cd902240346,
        0x091209320d3a0b1609320f3e0bf70f3e0c9909120b560d9b0cd909f30c380c58,
        0x056a060c0366052a05ab05cb00a10366040802a50428072e060c060c03870346,
    ),
    (
        0x048903c70122076e056a076e0f1e068d058b0d3a0f7e03060d7a0e5c0e7c064c,
        0x054a02e5036605eb09120224010203a706ed01420d1a09120d3a0c9909120d5a,
        0x0cd90fdf050a07ef0a950bb705ab0c99034609d30f7e0e5c0326052a01a30204,
        0x01620cd904890c58050a04c9068d04a908100ebd070e04e90a540cf904a9076e,
        0x0af50d5a0bf70d5a0ab50b160b3609320bb70d3a0cf90d3a09720cd90c580c99,
        0x07cf076e056a076e0162054a076e074e050a024406ed068d032605eb03060081,
    ),
    (
        0x056affffffffffff05eb095205ab0f7e0d7a0af50f1e070e0e5c0f5e07cf0d1a,
        0x09f3014201420b36050a01a309b30a140b56010201e3ffff08d1076e0af50d1a,
        0x0b560b360bf70f9fffff0bd70c780cd9ffff0c180e5c060cffff0a3403a705cb,
        0x03a7076e0e7c08d1066c0c180cf90a5402850cd9ffff0489ffffffffffff068d,
        0x0fff0b160b560cf90ebdffff0b76ffff0f3e0b76ffffffff09f3ffffffffffff,
        0x03c7034602c5ffff03a7ffffffffffff01e3ffffffffffffffffffffffffffff,
    ),
    (
        0xffffffffffffffff0fbf0cb90e3cffff05cbffffffffffff0ebdffffffffffff,
        0x0d7affffffffffffffffffffffffffffffffffffffffffff0af5ffffffffffff,
        0xffff0f1e0c58ffffffffffffffffffffffffffffffffffffffffffffffffffff,
        0x0e3cffffffff0dbbffffffffffffffffffffffffffffffffffffffffffffffff,
        0x0d3affffffffffffffffffffffffffffffffffffffffffffffffffffffffffff,
        0x0387ffffffffffffffffffffffffffffffffffffffffffffffffffffffffffff,
    ),
)
SEMAPHORES = (
    (0, 6, 12, 18, 24, 30),
    (1, 7, 13, 19, 24, 31),
    (2, 8, 14, 20, 24, 32),
    (3, 9, 15, 21, 24, 33),
    (4, 10, 16, 22, 24, 34),
    (5, 11, 17, 23, 25, 35),
    (0, 6, 12, 18, 26, 36),
    (1, 7, 13, 19, 27, 37),
    (2, 8, 14, 20, 28, 38),
    (3, 9, 15, 21, 29, 39),
    (4, 10, 16, 22, 24, 30),
    (5, 11, 17, 23, 25, 31),
    (0, 6, 12, 18, 26, 32),
    (1, 7, 13, 19, 27, 33),
    (2, 8, 14, 20, 28, 34),
    (3, 9, 15, 21, 29, 35),
    (4, 10, 16, 22, 24, 36),
    (5, 11, 17, 23, 25, 37),
    (0, 6, 12, 18, 26, 38),
    (1, 7, 13, 19, 27, 39),
    (2, 8, 14, 20, 28, 30),
    (3, 9, 15, 21, 29, 31),
    (4, 10, 16, 22, 24, 32),
    (5, 11, 17, 23, 25, 33),
)
NEEDS = (
    (
        0xffffffffffffffffffffffffffffffff,
        0xffffffffffffffffffffffffffffffff,
        0xffffffffffffffffffffffffffffffff,
        0xffffffffffffffffffffffffffffffff,
        0xffffffffffffffffffffffffffffffff,
        0xffffffffffffffffffffffffffffffff,
    ),
    (
        0xffffffffffffffffffffffffffffffff,
        0xffffffffffffffffffffffffffffffff,
        0xffffffffffffffffffffffffffffffff,
        0xffffffffffffffffffffffffffffffff,
        0xffffffffffffffffffffffffffffffff,
        0xffffffffffffffffffffffffffffffff,
    ),
    (
        0xffffffffffffffffffffffffffffffff,
        0xffffffffffffffffffffffffffffffff,
        0xffffff0cff0606ffff0606ffff0606ff,
        0xffffffffffffff06ffffff06ffffff06,
        0xffffffffffffffffffffffffffffffff,
        0x1e1e1e1e1e1e1e1e1e1e1e1e1e1e1e1e,
    ),
    (
        0xffffffffffffffffffffffffffffffff,
        0xffffffffffffffffffffffffffffffff,
        0xffffffffff0707ffff0707ffffffffff,
        0xffffffffffffff07ffffff07ffffff07,
        0xffffffffffffffffffffffffffffffff,
        0x1f1f1f1f1f1f1f1f1f1f1f1f1f1f1f1f,
    ),
    (
        0x14ffffff20ffffff202020ffff0202ff,
        0x0eff140effffff0effffff1420202020,
        0xff0220ffff202008ffffff20ffffff02,
        0xff14ff20ff1408200808080808141408,
        0xffffffffff08ffffffffffffffff08ff,
        0xffffffffffffffffffffffffffffffff,
    ),
    (
        0xffffffff21ffffffffffff21ffff21ff,
        0xffffffffffffffffffffffffff21ffff,
        0x0fffffffff2121ffffffffffffffffff,
        0xffffffffffffff21ffffffffffffffff,
        0xffffffffffffffffffff15ffffffffff,
        0xffffffffffffffffffffffffffffffff,
    ),
    (
        0xffffffff1610ff04ffffffffffffffff,
        0xffffff0affffffffffffffff1010ffff,
        0xff1010ffffff04ffffffffffffffffff,
        0x040404ff040422ffffffffffffffffff,
        0xffff16100aff101616100404160affff,
        0x22ff22222222ff222222ff2222222222,
    ),
    (
        0xffffffffffffffffffffffffffffffff,
        0xffffffffffffffffffffffffffffffff,
        0xffffffffffffffffffffffffffffffff,
        0xffffffffffffffffffffffffffffffff,
        0xffffff11ff0bffffffffffffffffffff,
        0x232323ff23232323ff2323ffffffff23,
    ),
    (
        0xffffffffffffffffffffffffffffffff,
        0xffffffffffffffffffffffffffffffff,
        0xffffffffffffffffffffffffffffffff,
        0xffffffffffffffffffffffffffffffff,
        0x060c1212ffffff06ffffffffffffffff,
        0xff24ffffffff24ffffffffffffffffff,
    ),
    (
        0xffffffffffffffffffffffffffffffff,
        0xffffffffffffffffffffffffffffffff,
        0xffffffffffffffffffffffffffffffff,
        0xffffffffffffffffffffffffffffffff,
        0xffff0dffffffffffffffffffffffffff,
        0xffffffffffffffffffffffffffffffff,
    ),
    (
        0xffffffffffffffffffffffffffffffff,
        0xffffffffffffffffffffffffffffffff,
        0xffffffffffffffffffffffffffffffff,
        0xffffffffffffffffffffffffffffffff,
        0xffffffffffffffffffffffffffffffff,
        0xffffffffffffffffffff26ffffff26ff,
    ),
    (
        0xffffffffffffffffffffffffffffffff,
        0xffffffffffffffffffffffffffffffff,
        0xffffffffffffffffffffffffffffffff,
        0xffffffffffffffffffffffffffffffff,
        0xff03ffffffffffffffffffffffffffff,
        0xffffffffffffffffffffffffffffffff,
    ),
    (
        0xffffffffffffffffffffffffffffffff,
        0xffffffffffffffffffffffffffffffff,
        0xffffffffffffffffffffffffffffffff,
        0xffffffffffffffffffffffffffffffff,
        0xffffffffffffffffffffffffffffffff,
        0xffffffffffffffffffffffffffffffff,
    ),
    (
        0xffffffffffffffffffffffffffffffff,
        0xffffffffffffffffffffffffffffffff,
        0xffffffffffffffffffffffffffffffff,
        0xffffffffffffffffffffffffffffffff,
        0xffffffffffffffffffffffffffffffff,
        0xffffffffffffffffffffffffffffffff,
    ),
    (
        0xffffffffffffffffffffffffffffffff,
        0xffffffffffffffffffffffffffffffff,
        0xffffffffffffffffffffffffffffffff,
        0xffffffffffffffffffffffffffffffff,
        0xffffffffffffffffffffffffffffffff,
        0xffffffffffffffffffffffffffffffff,
    ),
    (
        0xffffffffffffffffffffffffffffffff,
        0xffffffffffffffffffffffffffffffff,
        0xffffffffffffffffffffffffffffffff,
        0xffffffffffffffffffffffffffffffff,
        0xffffffffffffffffffffffffffffffff,
        0xffffffffffffffffffffffffffffffff,
    ),
    (
        0xffffffffffffffffffffffffffffffff,
        0xffffffffffffffffffffffffffffffff,
        0xffffffffffffffffffffffffffffffff,
        0xffffffffffffffffffffffffffffffff,
        0xffffffffffffffffffffffffffffffff,
        0xffffffffffffffffffffffffffffffff,
    ),
    (
        0xffffffffffffffffffffffffffffffff,
        0xffffffffffffffffffffffffffffffff,
        0xffffffffffffffffffffffffffffffff,
        0xffffffffffffffffffffffffffffffff,
        0xffffffffffffffffffffffffffffffff,
        0xffffffffffffffffffffffffffffffff,
    ),
    (
        0xffffffffffffffffffffffffffffffff,
        0xffffffffffffffffffffffffffffffff,
        0xffffffffffffffffffffffffffffffff,
        0xffffffffffffffffffffffffffffffff,
        0xffffffffffffffffffffffffffffffff,
        0xffffffffffffffffffffffffffffffff,
    ),
    (
        0xffffffffffffffffffffffffffffffff,
        0xffffffffffffffffffffffffffffffff,
        0xffffffffffffffffffffffffffffffff,
        0xffffffffffffffffffffffffffffffff,
        0xffffffffffffffffffffffffffffffff,
        0xffffffffffffffffffffffffffffffff,
    ),
    (
        0xffffffffffffffffffffffffffffffff,
        0xffffffffffffffffffffffffffffffff,
        0xffffffffffffffffffffffffffffffff,
        0xffffffffffffffffffffffffffffffff,
        0xffffffffffffffffffffffffffffffff,
        0xffffffffffffffffffffffffffffffff,
    ),
    (
        0xffffffffffffffffffffffffffffffff,
        0xffffffffffffffffffffffffffffffff,
        0xffffffffffffffffffffffffffffffff,
        0xffffffffffffffffffffffffffffffff,
        0xffffffffffffffffffffffffffffffff,
        0xffffffffffffffffffffffffffffffff,
    ),
    (
        0xffffffffffffffffffffffffffffffff,
        0xffffffffffffffffff1cffffffffffff,
        0xffffffffffffffffffffffffffffffff,
        0xffffffffffffffffffffffffffffffff,
        0xffffffffffffffffffffffffffffffff,
        0xffffffffffffffffffffffffffffffff,
    ),
    (
        0xffffffffffffffffffffffffffffffff,
        0xffffffffffffffffffffffffffffffff,
        0xffffffffffffffffffffffffffffffff,
        0xffffffffffffffffffffffffffffffff,
        0xffffffffffffffffffffffffffffffff,
        0xffffffffffffffffffffffffffffffff,
    ),
)
LATE = (
    (0x000f, 0x0888, 0x0111, 0x7777, 0x0000, 0x0000),
    (0x000f, 0x088e, 0x1111, 0x7777, 0x0000, 0x0000),
    (0xbff8, 0xf804, 0x6eff, 0x1be9, 0x0000, 0xc000),
    (0xffff, 0xffff, 0x7fff, 0xffdf, 0x0000, 0xf0e9),
    (0x10cf, 0xe7fb, 0x89b3, 0xd677, 0x77ff, 0x4020),
    (0xffff, 0xfbff, 0xefff, 0xffff, 0x0537, 0x109e),
    (0xffff, 0x7eff, 0xbfff, 0xcfff, 0x3fff, 0xbdff),
    (0xffff, 0xffff, 0xdfff, 0xffff, 0x3eff, 0xffff),
    (0xffff, 0xffff, 0xffff, 0xffff, 0xffff, 0xffdd),
    (0xbfff, 0xffff, 0xffff, 0xffff, 0xffff, 0xffff),
    (0xffff, 0xffff, 0xffff, 0xffff, 0xffff, 0xffff),
    (0xffff, 0xffff, 0xffff, 0xffff, 0xffff, 0xffff),
    (0xffff, 0xffff, 0xffff, 0xffff, 0xffff, 0xffff),
    (0xffff, 0xffff, 0xffff, 0xffff, 0xffff, 0xffff),
    (0xffff, 0xffff, 0xffff, 0xffff, 0xffff, 0xffff),
    (0xffff, 0xffff, 0xffff, 0xffff, 0xffff, 0xffff),
    (0xffff, 0xffff, 0xffff, 0xffff, 0xffff, 0xffff),
    (0xffff, 0xffff, 0xffff, 0xffff, 0xffff, 0xffff),
    (0xffff, 0xffff, 0xffff, 0xffff, 0xffff, 0xffff),
    (0xffff, 0xffff, 0xffff, 0xffff, 0xffff, 0xffff),
    (0xffff, 0xffff, 0xffff, 0xffff, 0xffbf, 0xffff),
    (0xffff, 0xffff, 0xffff, 0xffff, 0xffff, 0xffff),
    (0xfff8, 0xfffe, 0xfeee, 0xffe8, 0xfac8, 0xe880),
    (0xe880, 0x8800, 0xc000, 0xc000, 0x8000, 0x8000),
)
LATE_BY = 3
NO_WAIT = 0xFF
GAIN_STEP = 1
SLOTS = 33
UNITS = 129
UNIT = 16
LANES = 128
STARTS = (0, 32, 64, 96)
OPPOSITE = (1, 0, 3, 2, 5, 4)
ORDER = (5, 3, 1, 2, 0, 4)
SENDS = 3
NOTHING = 0xFFFF


SIZES = dict(zip(STARTS, (b - a for a, b in zip(STARTS, STARTS[1:] + (UNITS,)))))


def size_of(entry):
    return 0 if entry == NOTHING else SIZES[entry % UNITS]


def neighbour_position(p, d):
    x, y = divmod(p, 4)
    if d == 0:
        x = (x + 1) % 4
    if d == 1:
        x = (x + 3) % 4
    if d == 2:
        y = (y + 1) % 4
    if d == 3:
        y = (y + 3) % 4
    return 4 * x + y


def signed(word):
    return word - (1 << 32) if word >= 1 << 31 else word


def entries(step, d):
    return [(PLAN[step][d] >> (16 * p)) & 0xFFFF for p in range(16)]


def mask_of(flags):
    return sum(1 << p for p, flag in enumerate(flags) if flag)


def gather_kernel(re_ref, im_ref, held, part, part_in, send_sem, recv_sem, load_sem, pair_sem):
    bins = re_ref.shape[0]
    tiles = re_ref.shape[1]
    fr = lax.axis_index("fr")
    sr = lax.axis_index("sr")
    sc = lax.axis_index("sc")
    z, x, y = sr // 4, sr % 4, sc
    p = 4 * x + y
    steps = len(PLAN)

    loads = []
    for f in range(bins):
        for half in range(2):
            for i, ref in enumerate((re_ref, im_ref)):
                place = 4 * f + 2 * half + i
                source = ref.at[f, :, :, pl.ds(half * LANES, LANES)]
                target = held.at[pl.ds(place * tiles, tiles)]
                loads.append(pltpu.make_async_copy(source, target, load_sem.at[0]))
    for load in loads:
        load.start()

    xp, xm = (x + 1) % 4, (x + 3) % 4
    yp, ym = (y + 1) % 4, (y + 3) % 4
    zp, zm = (z + 1) % 4, (z + 3) % 4
    targets = (
        (fr, 4 * z + xp, y),
        (fr, 4 * z + xm, y),
        (fr, sr, yp),
        (fr, sr, ym),
        (fr, 4 * zp + x, y),
        (fr, 4 * zm + x, y),
    )
    ahead = (4 * (xp - x), 4 * (xm - x), yp - y, ym - y, 16, -16)
    twin = (1 - fr, sr, sc)
    shift = 16 * (y % 2)

    barrier = pltpu.get_barrier_semaphore()
    for device in targets + (twin,):
        pl.semaphore_signal(barrier, inc=1, device_id=device, device_id_type=MESH)
    everything = held.at[pl.ds(0, UNITS - 1)]
    pltpu.make_async_copy(everything, everything, load_sem.at[0]).wait()
    pl.semaphore_wait(barrier, 7)

    def chosen(step, d):
        words = [jnp.int32(signed((PLAN[step][d] >> (32 * i)) & 0xFFFFFFFF)) for i in range(8)]
        words = [jnp.where(y < 2, words[i], words[i + 1]) for i in range(0, 8, 2)]
        word = jnp.where(
            x < 2,
            jnp.where(x == 0, words[0], words[1]),
            jnp.where(x == 2, words[2], words[3]),
        )
        return lax.shift_right_logical(word, shift) & 0xFFFF

    def needed(step, d):
        words = [jnp.int32(signed((NEEDS[step][d] >> (32 * i)) & 0xFFFFFFFF)) for i in range(4)]
        word = jnp.where(
            x < 2,
            jnp.where(x == 0, words[0], words[1]),
            jnp.where(x == 2, words[2], words[3]),
        )
        return lax.shift_right_logical(word, 8 * y) & 0xFF

    def guarded(mask, action):
        if mask == 0:
            return
        if mask == 0xFFFF:
            action()
            return
        pl.when((lax.shift_right_logical(jnp.int32(mask), p) & 1) == 1)(action)

    def transfer(step, d, source, target, size, arrival):
        return pltpu.make_async_remote_copy(
            src_ref=held.at[pl.ds(source, size)],
            dst_ref=held.at[pl.ds(target, size)],
            send_sem=send_sem.at[SENDS * d + step % SENDS],
            recv_sem=recv_sem.at[arrival],
            device_id=targets[d],
            device_id_type=MESH,
        )

    def for_each_size(sizes, action, among=0xFFFF):
        for size in sorted(set(sizes) - {0}):
            guarded(mask_of(v == size for v in sizes) & among, functools.partial(action, size))

    def send(step, d):
        waits = mask_of((NEEDS[step][d] >> (8 * q)) & 255 != NO_WAIT for q in range(16))

        def arrived(size):
            transfer(step, d, 0, UNITS, size, needed(step, d)).wait_recv()

        def action(size):
            source = chosen(step, d)
            transfer(step, d, source, source - UNITS * ahead[d], size, SEMAPHORES[step][d]).start()

        sizes = [size_of(v) for v in entries(step, d)]
        for_each_size(sizes, arrived, waits)
        for_each_size(sizes, action)

    def receive(step, d):
        sent = [size_of(v) for v in entries(step, d)]
        coming = [sent[neighbour_position(q, OPPOSITE[d])] for q in range(16)]
        for_each_size(coming, lambda size: transfer(step, d, 0, UNITS, size, SEMAPHORES[step][d]).wait_recv(), LATE[step][d])

    def finish(step, d):
        sent = [size_of(v) for v in entries(step, d)]
        for_each_size(sent, lambda size: transfer(step, d, 0, UNITS, size, SEMAPHORES[step][d]).wait_send())

    exchange = pltpu.make_async_remote_copy(
        src_ref=part,
        dst_ref=part_in,
        send_sem=pair_sem.at[0],
        recv_sem=pair_sem.at[1],
        device_id=twin,
        device_id_type=MESH,
    )

    for step in range(steps):
        if step >= LATE_BY:
            for d in range(6):
                receive(step - LATE_BY, d)
        for d in ORDER:
            if step >= SENDS:
                finish(step - SENDS, d)
            send(step, d)
        if step == 0:
            total = jnp.zeros((tiles, UNIT, LANES), jnp.float32)
            for i in range(4 * bins):
                piece = held[pl.ds(i * tiles, tiles)].astype(jnp.float32)
                total += piece * piece
            total = total.reshape(tiles * UNIT, LANES)
            power = jnp.sum(total.T, axis=0, keepdims=True)
            part[...] = jnp.broadcast_to(power, part.shape)
            exchange.start()
        if step == GAIN_STEP:
            exchange.wait()
            power = part[...] + part_in[...]
            gain = 1.0 / jnp.sqrt(power * (1.0 / 2048.0))
            gain = jnp.concatenate([gain, gain], axis=0)
            high = gain.astype(jnp.bfloat16).astype(jnp.float32)
            middle = (gain - high).astype(jnp.bfloat16).astype(jnp.float32)
            low = gain - high - middle
            row = lax.broadcasted_iota(jnp.int32, (UNIT, LANES), 0)
            rest = jnp.where(row == 1, middle, low)
            held[UNITS - 1] = jnp.where(row == 0, high, rest).astype(jnp.bfloat16)
    for step in range(steps - LATE_BY, steps):
        for d in range(6):
            receive(step, d)
    for step in range(steps - SENDS, steps):
        for d in range(6):
            finish(step, d)


def gathered(re, im):
    bins, tiles = re.shape[:2]
    steps = len(PLAN)
    return pl.pallas_call(
        gather_kernel,
        out_shape=jax.ShapeDtypeStruct((SLOTS * UNITS, UNIT, LANES), jnp.bfloat16),
        in_specs=[pl.BlockSpec(memory_space=pltpu.HBM)] * 2,
        out_specs=pl.BlockSpec(memory_space=pltpu.VMEM),
        scratch_shapes=[
            pltpu.VMEM((8, 128), jnp.float32),
            pltpu.VMEM((8, 128), jnp.float32),
            pltpu.SemaphoreType.DMA((6 * SENDS,)),
            pltpu.SemaphoreType.DMA((max(map(max, SEMAPHORES)) + 1,)),
            pltpu.SemaphoreType.DMA((1,)),
            pltpu.SemaphoreType.DMA((2,)),
        ],
        compiler_params=pltpu.CompilerParams(
            collective_id=0, has_side_effects=True, vmem_limit_bytes=24 << 20
        ),
        name="gather_blocks",
    )(re, im)


GROUP = 11


def gain_row(tile):
    wide = tile.astype(jnp.float32)
    return wide[0:1] + wide[1:2] + wide[2:3]


def spectra(held, f, first):
    halves = [held[pl.ds(first + 32 * f + 16 * h, 16)].reshape(256, LANES) for h in range(2)]
    return jnp.concatenate(halves, axis=1)


def cross_kernel(order, held, out, staged, own_column, sem):
    bins = out.shape[0]
    own_row = gain_row(held[UNITS - 1]) * (1.0 / 16.0)
    own_column[...] = jnp.broadcast_to(own_row, (128, 128)).T

    def group(i, carry):
        for j in range(GROUP):
            place = i * GROUP + j
            first = order[place] * UNITS
            weight = own_column[...] * gain_row(held[first + UNITS - 1])
            for f in range(bins):
                mine, other = spectra(held, f, 0), spectra(held, f, first)
                full = lax.dot_general(
                    mine, other, (((1,), (1,)), ((), ())), preferred_element_type=jnp.float32
                )
                staged[place, f, :, :128] = (full[:128, :128] + full[128:, 128:]) * weight
                staged[place, f, :, 128:] = (full[128:, :128] - full[:128, 128:]) * weight
            pltpu.make_async_copy(staged.at[place], out.at[:, place], sem).start()
        return carry

    lax.fori_loop(0, SLOTS // GROUP, group, 0)
    pltpu.make_async_copy(staged, staged, sem).wait()


def local(spec_re, spec_im, offsets):
    bins, rows, segs = spec_re.shape
    tiles = rows // UNIT
    re = spec_re.reshape(bins, tiles, UNIT, segs)
    im = spec_im.reshape(bins, tiles, UNIT, segs)
    re = pltpu.with_memory_space_constraint(re, pltpu.HBM)
    im = pltpu.with_memory_space_constraint(im, pltpu.HBM)
    held = gathered(re, im)
    cross = pl.pallas_call(
        cross_kernel,
        in_specs=[pl.BlockSpec(memory_space=pltpu.SMEM), pl.BlockSpec(memory_space=pltpu.VMEM)],
        out_specs=pl.BlockSpec(memory_space=pltpu.HBM),
        out_shape=jax.ShapeDtypeStruct((bins, SLOTS, rows, 256), jnp.float32),
        scratch_shapes=[
            pltpu.VMEM((SLOTS, bins, rows, 256), jnp.float32),
            pltpu.VMEM((rows, rows), jnp.float32),
            pltpu.SemaphoreType.DMA,
        ],
        compiler_params=pltpu.CompilerParams(vmem_limit_bytes=30 << 20),
        name="cross_products",
    )(offsets[0], held)
    return cross[:, None]


def solution(mesh):
    placed = (P("fr", ("sr", "sc"), None), P("fr", ("sr", "sc"), None), P(("sr", "sc"), None))
    return jax.shard_map(
        local,
        mesh=mesh,
        in_specs=placed,
        out_specs=P("fr", ("sr", "sc"), None, None, None),
        check_vma=False,
    )
```

time: 101 us -> 81.5 us (0.81)
  Pallas kernels: 97 us -> 79.9 us
  local copies, waits for them, and re-layouts: 1.92 us -> 0.01 us
    pallas_call x2, Pallas kernels: 97 us -> 79.9 us  [the longest x1 73 us: gathered(): pl.pallas_call(gather_kernel, out_shape=jax.ShapeDtypeStruct((SLOTS * UNI...]
    unnamed x6 -> x2, local copies, waits for them, and re-layouts: 1.92 us -> 0.01 us
where the time goes in v3:
time: 81.5 us; the launch traced here: 79.9 us
  Pallas kernels  79.9 us (98%)
    pallas_call x1, Pallas kernels, gathered(): pl.pallas_call(gather_kernel, out_shape=jax.ShapeDtypeStruct((SLOTS * UNI...  73 us
    pallas_call x1, Pallas kernels, local(): pl.pallas_call(cross_kernel, in_specs=[pl.BlockSpec(memory_space=pltpu.SM...  6.95 us

profile of v3, /device:TPU:30, one launch (start us, length us, event | category | flops | bytes accessed | tf_op | source)
XLA Modules:
  0.0 79.9 jit_solution(16711909653174962110)
XLA Ops:
  0.0 0.0 copy-start
  0.0 73.0 %gather_blocks.1.held = bf16[4257,16,128]{2,1,0:T(8,128)(2,1)S(1)} custom-call(bf16[4,8,16,256]{3,2,1,0:T(8,128)(2,1)} %bitcast.7, bf16[4,8,16,256]{3,2,1,0:T(8,128)(2,1)} %bitcast.8), custom_call_target="tpu_custom_call" | custom-call | tf_op jit(solution)/shard_map/gather_blocks/pallas_call | solution.py:654
  73.0 0.0 copy-done
  73.0 7.0 %cross_products.1 = f32[4,33,128,256]{3,2,1,0:T(8,128)} custom-call(s32[33]{0:T(128)S(1)} %bitcast.6, bf16[4257,16,128]{2,1,0:T(8,128)(2,1)S(1)} %gather_blocks.1.held), custom_call_target="tpu_custom_call" | custom-call | tf_op jit(solution)/shard_map/cross_products/pallas_call | solution.py:719
Async XLA Ops:
  0.0 73.0 %copy-start = (s32[1,33]{1,0:T(1,128)S(1)}, s32[1,33]{1,0:T(1,128)}, u32[]{:S(2)}) copy-start(s32[1,33]{1,0:T(1,128)} %param.5) | copy-start | bytes 400

commit v4 on v3

v4 whole, which is shorter than its diff:
```python
import functools
import math

import jax
import jax.numpy as jnp
from jax import lax
from jax.experimental import pallas as pl
from jax.experimental.pallas import tpu as pltpu
from jax.sharding import PartitionSpec as P

MESH = pl.DeviceIdType.MESH

PLAN = (
    (
        0x00270068000d0000ffffffffffffffffffffffffffffffffffffffffffffffff,
        0x004e005b000d0041004e002700340000000000270068005bffffffffffffffff,
        0x0034ffffffffffff0027ffffffffffff000dffffffffffff001affffffffffff,
        0x001a004e000dffff0034001a004effff001a0068001affff004e0027000dffff,
        0xffffffffffffffffffffffffffffffffffffffffffffffffffffffffffffffff,
        0x0027005b005b002700270034001a00680034000000270034000d005b001a0000,
    ),
    (
        0x0068000d001a000dffffffffffffffffffffffffffffffffffffffffffffffff,
        0x004100270027000d0041004e0027005b0041001a00000041ffffffffffffffff,
        0x0041ffffffffffff0068ffffffffffff004effffffffffff0041ffffffffffff,
        0x0041001a001affff000d0041005bffff0068005b0041ffff0041004e0034ffff,
        0xffffffffffffffffffffffffffffffffffffffffffffffffffffffffffffffff,
        0x0041000d004e000d005b004e0041000d005b001a0000004e00680068004e0068,
    ),
    (
        0x0000000000340034ffffffffffffffffffffffffffffffffffffffffffffffff,
        0x000000410000005b001a005b0068004100270041000d0027ffffffffffffffff,
        0x000dffffffffffff0000ffffffffffff0027ffffffffffff0027ffffffffffff,
        0x000000000068ffff0000005b000dffff00270041004effff00000000005bffff,
        0xffffffffffffffffffffffffffffffffffffffffffffffffffffffffffffffff,
        0x005b00000000005b00000068000d0034002700410034000000270000005b001a,
    ),
    (
        0x005b00340041004effffffffffffffffffffffffffffffffffffffffffffffff,
        0x001a003400410068000d000d00000027004e000d005b001affffffffffffffff,
        0x005bffffffffffff001affffffffffff0034ffffffffffff005bffffffffffff,
        0x000d00340041ffff0068000d0000ffff000d004e005bffff005b00410041ffff,
        0xffffffffffffffffffffffffffffffffffffffffffffffffffffffffffffffff,
        0x003400340041001a004e000d0000001a001a0034005b0068005b001a0027004e,
    ),
    (
        0x0075086b086b083708370844082a0878084408100837084406330674082a060c,
        0x08370075086b083708370844082a08780844081008370844081d086b082a0810,
        0x0837086b086b01b70075025f021102450075022b02380204081d022b026c019d,
        0x0837086b086b083708370844082a02450844081008370204081d086b082a025f,
        0xffffffffffffffffffffffffffffffffffffffffffffffffffffffffffffffff,
        0x0837086b086b083708370844082a08780844081008370844081d086b082a0810,
    ),
    (
        0x08510075085e0075086b085e0851081d086b082a0810085e081d086b06190810,
        0x0068081d00750075086b000000750075086b00750075000d08780878085e0878,
        0x0068081d085e083700410844082a01aa0000081008370190007506740619025f,
        0x0075081d0075081d086b0000007508780041007500750844007500340000060c,
        0xffffffffffffffffffffffffffffffffffffffffffffffffffffffffffffffff,
        0x0851081d085e081d086b085e0851081d086b082a0810085e08780878085e0878,
    ),
    (
        0x0837081d0810081d08100878081d084408370851084408100674087806260878,
        0x086b001a085e001a003400750851081d007500680034085e08370810086b082a,
        0x004e0810081001c4086b022b022b01eb086b0252022b025f0878021e02040245,
        0x086b0027085e086b0075085e08510211086b082a0810025f08780878085e0245,
        0xffffffffffffffffffffffffffffffffffffffffffffffffffffffffffffffff,
        0x086b08100810086b08100878081d0844083708510844081008370810086b082a,
    ),
    (
        0x084408100068086b085e081d0810082a082a0844086b0878060c060c06400640,
        0x007508100068003408100878081d08440068003400410810086b082a0837085e,
        0x001a084408510190004e02450204025f0068025f026c0245003402450211022b,
        0x004e00410810082a004108780068025f004e0034084402450837000d0068022b,
        0xffffffffffffffffffffffffffffffffffffffffffffffffffffffffffffffff,
        0x084408440851082a085e081d0810082a082a0844086b0878086b082a0837085e,
    ),
    (
        0x06b407ea0626082a10471054103a1088105404701047040808370e770e770e43,
        0x084408b808ec08ec0075004108c5082a082a0a48089108780a48089e08ec1020,
        0x07ea025f021e09ba0a3b02790a6f1088082a0a480a2e10540a48107b103a1020,
        0x0844007500cf0204085e002708c50a3b0a3b08c508910a7c0a48082a08371020,
        0xffff08b808ec08ec0a3b08b808c508ab0a3b08c508910a7c0a48089e08ec08ab,
        0x001a004e00cf0068000d0075005b004e0211005b004e0075003400750075005b,
    ),
    (
        0x079c065a064d0041107b06260633065a107b103a0626106e1088082a106e065a,
        0x079c07dd089e004e00680a21009b08ab0a6f07b6001a009b10881088106e0a48,
        0x079c026c0252102d0034106e1061102d0a6f103a1020106e004e1088106e1088,
        0x006800680027026c001a08ec009b102d0a6f000d00cf106e0a6f089e00751088,
        0xffffffff089e09baffff08ec0a6f0a3b0a6f0a480a2e08b80a6f0a140a3b0a48,
        0x000d001a009b004e0034001a004e00cf0000004e00cf022b004e02110000065a,
    ),
    (
        0x060c06740619064010201088060c102d10471061042210200e5d1020107b103a,
        0x078f08ec07b608df0a6f02450a6208d206c1005b08ab089110471020107b103a,
        0x078f0204025f107b0a6f1088102d10540a3b1061105410200e5d1020107b103a,
        0x003408ec0034021e0252007508df1054007508ec08ab10200e5d08f90e6a103a,
        0xffff08ecffff08df0a6f0a210a6208d2ffff08ec0a5508910e5d08f90e6a09a0,
        0x004e002700750075025200000279026c004101b7023802790000004e0068000d,
    ),
    (
        0x001a001a007500e90633064d0640060c06c1067410540674107b06810e1c085e,
        0x06a707d000cf0891021e00f608df00dc00dc00c2022b0075102d107b08f91088,
        0x07c306740619103a026c102d1020103a02111054107b1088020401eb02790211,
        0x022b00f600a8061900c20a1408f9103a0a1400c2000d10880034022b00b50211,
        0xffffffffffff0891ffff0a1408df09ee0a140a7c08ab0a210e5008b80e1c0a62,
        0x0000008e002700e900410041002700dc008101aa0075001a00410027000d0041,
    ),
    (
        0x065a0619060c0626106e06401007103a103a086b0fd308850e500fb910470e77,
        0x07c3085e09390a1401aa08df005b004e0a21008e027900c2107b103a0f9f086b,
        0x0e430e500e360252081d09ee1007027901de0a7c0a55022b0000103a1047106e,
        0x0e430e500e360e840a4808df0e43026c0a21022b00f60a480a2e008100c2106e,
        0xffffffff0939096d0a4808df08f90af008f909ad0a2108c50a2e0e7708ab0a14,
        0x082a085e00340878081d0885086b085e0068086b085e0885084408850885086b,
    ),
    (
        0x004e0041002708780e770fe00fac085e0e840f9f0e6a1088084408850885086b,
        0x081d00f608ab096d027900c2004e085e01de020400e902790844088510070a7c,
        0x0a7c085e0fac08780a4808850e43085e040801eb085e0279068108850245021e,
        0x0a7c008108ab087808b800c20aa20279021e002700e90279027900f6008e021e,
        0xffffffff0fac091f08b809ee100709460eeb0c730fd30a2e0cc00fb90f9f0e36,
        0x081d082a00f6085e0844082a085e00410810085e0041043c085e000d08100027,
    ),
    (
        0x082a07d008df009b0fed08850fd308df0810085e085e0a3b04890fed08100e36,
        0x000d009b00340a2e00c2082a00c208df000d085e085e0a3b085e0a210810081d,
        0x0e77021e0ffa0a2e0e77026c026c0238085102450a210a3b026c0a21081001c4,
        0x0e1c0a140a62085e0844026c0a890238081000e90a480a3b001a088500a8029f,
        0xffffffff0ffa09120eaa0fac0fac09600e840e1c0e6a09ad0ffa0fed100708b8,
        0x085e0837088508850068081000a801f8085100e9008e00270810085e0878081d,
    ),
    (
        0x07c300e908ab01eb0ed10f9f0fb90e1c0eeb0fd30f9f0a891007085e0fb9081d,
        0x0a3b089e0a6f00b50a6200e90a8900e9008100cf01de02450810085e087808b8,
        0x0a3b06190fb901eb01f80e5d0a890a7c01aa09c7043c0a4801aa027901c4081d,
        0x0e770e840a6f08850ed10e5d00c20e1c00810e1c02790a2e00dc02790878086b,
        0xffffffff096d09460ed10f9f0fd30ae30fe00fd30e770e360eb70ffa08f90a7c,
        0x0810004108370000085108510837019d004e00cf0885082a08510837081d0851,
    ),
    (
        0x081d083700c20946102d0f8608370ec40fd30ffa0885082a085e0837081d0851,
        0x025f008100c208f9084401900081019d021e025f088509120eeb0fc608850851,
        0x08100db5099308f901c40810021e019d027909ba027908850a2e0190081d0851,
        0x0a6f08370ed10e36085100f6021e020400dc00f600680885008e083708ab0851,
        0x0d010ec40fb90fc60fac09d40fb90a950fd30ffa100709120e9d0ede0a950a95,
        0x00750068001a009b007500f6006800e9007500f6000d000d008e004100410034,
    ),
    (
        0x069a085e083700a80e360667107b08ec0891107b0a48036108510a210878107b,
        0x082a00e90837025f01f8014300f6024500c2086b01c4017708510837081d107b,
        0x0a6f103a08370fc60e430667107b106e026c107b01c4082a0851026c1095107b,
        0x042f0a2e0906025f0e43066700a8106e0891025f00dc043c00a80a21026c107b,
        0x0dcf0db509930eb709c70a62096009a00e770aa20e430c730eeb0c250fed0e77,
        0x00680075000d003400c2005b0075005b000d0068001a0041001a0034003400b5,
    ),
    (
        0x06f500f6084400b51054103a106e0681085107dd0851109508100fc610950fe0,
        0x0238027908440885080409d407dd0a7c00f607dd01f8008e106e081d10200837,
        0x0a210ddc09fb106e0804082a106e06810e7706810fed10950804081d021e0837,
        0x0e6a0afd00e90ae300f60885008106810f0506810e4304560844081d00cf0837,
        0x0c730f2b09fb092c08ab0d9b0aaf0bf20f050a950fed092c0c180fc60c180e84,
        0x02380279084400b500f60027009b011c064007dd00a8005b007500f600c20075,
    ),
    (
        0x06db089e00e908f9060c102008b80ffa102009c70e4308371020078f10880837,
        0x0252041509060211087808c5016a01b708b80891010f08371020106e10880c3f,
        0x0de9104702040211060c065a083709a001c4106e01aa08370211106e047d102d,
        0x025204150a950211087808c50837083708b8089100a80837085e085e02ed102d,
        0x0de90e9d0da80ae309930ac90dcf0b0a08b808910c180ac909a00a620a620c3f,
        0x06db041500e902110878009b016a00f600dc002700680190016a009b00b500c2,
    ),
    (
        0x081000cf0102081010611061066708510e0308df0681103a0eeb081d102d1061,
        0x07dd0252026c008e01c402fa014301c4085e08df085101f810611047102d1061,
        0x02040d9b026c08100a62106107dd020408780ffa0851103a025208371088060c,
        0x02040252026c0af000b5064006670b0a028508df0885103a048902d3081d02c6,
        0x0ccd0d9b0db50bbe0c3f0a080c730c3209460a2e0c8d09d40fb90ddc0eeb0c32,
        0x019d085100c208100279014301430204085e00750851008e00dc014301770136,
    ),
    (
        0x0598068108b806db088509060d9b08f9088508f9081d081d089e085108510844,
        0x08df0a6f02040245078f01eb087808f9016a08f90a4809d4089e085108510844,
        0x0885043c02791095079c019d08780885089101f8081d081d0e36085108510e6a,
        0x08df0af00f0502450dcf0906068108f900f608f906190ae3089e0c250a890844,
        0x08df0f380a9509930dcf0df60ede0afd093909a00e9d0ae30e290e4309060f52,
        0x0598043c082a06db00b5019008780000016a01eb00f6009b011c085108510844,
    ),
    (
        0x087807b6081d06e80eeb086b0fed086b064d0878082a0851082a08440e430f52,
        0x00dc022b081d00a808d2086b09fb0afd01aa0878081d0851082a0844084408c5,
        0x024509ba0e77024508d20ffa0885086b0c660878082a0c4c082a084408440844,
        0x0245022b02790cc00eeb065a0a3b086b064d0aa2089e085102e002fa03e208c5,
        0x0c320ddc0e7709870eeb0ffa09fb0fc60c660db50f9f0c320ca610140ffa0bb1,
        0x087807b6027906e8001a086b00dc086b08850878082a0851082a0844084401f8,
    ),
    (
        0x0702009b043c00c2068d0851065a0fc6081d0f8610070ac906b40e4307b60885,
        0x0a62021108b80ba407a9078f08b801020939091208b8086b0885090608d20885,
        0x0a4802110633022b0a2e05d906810fc60e5007dd1095086b079c09e103c80885,
        0x0a4802110a14022b043c0aa20e5008510e50091208b8086b06b408c508d20885,
        0x0e500e360fed0ba40ce70dcf0a9509870a080bd809e10ffa0f0509e1091f0987,
        0x070202110633022b064d05d9064d0851081d008e010f086b06b4015d07b60885,
    ),
    (
        0x07dd0878082a092c064d08ab0885063306b408370878086b097a08ab084408c5,
        0x0a1402d3021108ab01eb0837011c090606b4029f08780150097a08ab08c508d2,
        0x0a620e1c0211047d01eb08370a4806330e1c083708780a89097a0408102d0a3b,
        0x008e0e1c020408ab064d08ab064d09060e1c065a0878082a097a08ab047d08d2,
        0x0fb90e1c0aaf0cc00ddc09e10b0a0c180fed0ac909460ddc0eaa0eaa0eb7092c,
        0x008e02d30177047d01eb065a0885063306b401f80878017701f8027902fa037b,
    ),
    (
        0x0496059806b409870fe00d9b08440e360f790db50fb9089e08850906098708d2,
        0x0d1a0a6202e008440987013601b703470a7c0245016a0a890fed095309870946,
        0x0e5d0a3b0da80a550bff01eb0470062608850db507a9085107ea095303fc1061,
        0x0e5d0e5d08d208440c3f045604700e360eb706330e91089e009b0a6f0c251061,
        0x0e5d0eeb0e6a0b160fe00fed09460be50f790ae309600c3f0fed10070c250b16,
        0x049601eb02e0004101c407c300c2088508780633081d081d010f019001c4021e,
    ),
    (
        0x06810702079c064d108809a00dcf0a08069a064d064d08ab07d010140ffa1054,
        0x06db071b0a1402380885090609870a89027902fa080408ab092c07d00ffa089e,
        0x029202450fed02380c8009a00dcf08510422058b064d0c730e1c01f810201054,
        0x02920a89081d023806810e3604080702069a0bd80c18064006c10c8d06191054,
        0x0d5b0f7910140a0809870aa2091f091f0fb90f9f09120ad608c50afd0de90bd8,
        0x02920245024502380885029f0681029200c2064d00e9016a07d007d0021e03fc,
    ),
    (
        0x096d0728016a089107a90dcf064d092c062607d008b809a0074207c310540946,
        0x08780238023802b909e10a620b0a092c0ad607d002e0036107c31054105409ad,
        0x0e500e36023804560dcf061909fb08100626064010610d0109a010540e500f52,
        0x08780e36049602b90e5002ed047d0afd0e77061908510d010e840a7c0a550f05,
        0x0d1a097a09ad0af00c990af00d9b0bcb0e9d0f6c0db5091f0abc0e6a0aa20bcb,
        0x021e0463016a02b907a902ed06e803ef06260640029f0361074207c301de032d,
    ),
    (
        0x05d905b206330a3b08040df60ede08b8106e08850e9d068107020ede08040a08,
        0x027902fa0b7e0a3b011c0ac90abc08b80a0807ea09930de90702073508040a6f,
        0x02790a89105403c80e36041507ea0be507d0061910140e5d0b3d0a6208041095,
        0x0a550e9d02ac0eeb0e360ac90ede06740c6604fe00c2107b0eeb0a620ec40a7c,
        0x0fc609600b7e0dc20ae30ec40f4508b80e030f860bff0de90b3d0c8d0c4c0fb9,
        0x00a802fa02920279044904150422078f064d061907ea06810702081d01430463,
    ),
    (
        0x0449097a096d065a082a0953097a064d07b61020091f09fb069a0fac0fac06ce,
        0x089e010f0102092c06db08f90a95091f078f022b0143092c0a080a890abc0b16,
        0x0d1a07d00db50bbe0c1809d4080404150a7c0bd80c660f9f04220ddc0fac0bd8,
        0x0f120ae3085110200c1806ce02450a95065a0a950a210ec40e1c08b80ca606ce,
        0x09600df60e9d0be50c18093909ba0da808ab0e9d0b230f9f0dcf0df60ca60e43,
        0x088507d001020387068106f50804047007f708850143058b02fa04a303fc03ef,
    ),
    (
        0x064006db07a9085106190fd309460d820946062609600ddc0ffa069a0f9f0f93,
        0x06e803470b710bf20a210aa20b230b71094609390bcb09ee08d20a7c07ea092c,
        0x0e6a0b9710950df60a210c7301de0d820e030c730c3f0ffa0e290dc202380e77,
        0x0e500c4c0aaf0c8d08ab0fd304e402ac08c50ae306b40c730ede0a950cc00e36,
        0x09ba0af00f050df610070f520af008c50ffa0ed10c3f0a4810070af00af00c4c,
        0x04080190043c084402e001aa01de02110245047d0347054b02c60292031303d5,
    ),
    (
        0x072808b8098708ec0d7506000e9106a70d340e10102d0e500e9d07420fd306a7,
        0x096d0a140b0a02c609fb0a080aa20aaf0d3409fb0ae30a14080409a00a2e0b0a,
        0x0d9b019d103a0f6c068109c706260bf203ef03bb102d09ad0285101406260ce7,
        0x07280ef80b0a0a9509fb07020eb7043c08f90e5d062608ab0e9d02380e3606c1,
        0x09e10d270b0a09530f790bb10b3d0bbe0d340e100ae30bf20aa20aaf0c590b0a,
        0x072801f801b706f5068d019d06260810071b03bb043c06ce03e202fa037b00f6,
    ),
    (
        0x078f078f03d500cf0ce70d4e091f107b07f70de90fed0d4e0dcf10070ed10e29,
        0x0a21097a07dd029209930cc001c400810702099307c303470960096d0afd0a95,
        0x0e1c09fb09ad0ba40993021e0c3f0da80a1409930fd30c8d0c2509ba0e6a03bb,
        0x0e2902ac0ede04560ce70ed10c660ae3061902850e6a069a0c250ede04080a95,
        0x09390f6c0bcb0fe009a0097a0c3f0ed10c5909930d0e0c800d010ba40fb90e9d,
        0x078f00c2045606330783008106b4012907b6083701de034701aa012903c804fe,
    ),
    (
        0x063304b0015d06740e6a0e6a0eb70f9f0fb907f71088091206ce0df60da80f38,
        0x00f60afd09d40a55096d091f07350af008ab09d4078f08b809e10a6209460fb9,
        0x036e0df609d4102005d90e6a0d9b0bb107c309d410880e910e50025207d00fb9,
        0x0e84009b0cda08100ae3029f0ef804490ef803060c8d0e5d0f1206a706ce0a14,
        0x0d680d820e030f860eb7091f0abc0bb10ce70c3f0ddc0fd30de909ee0ae30f45,
        0x036e03470619064d0081013606db047d02850306025f0408048906a7058b0354,
    ),
    (
        0x0885074f0804088506b40d820e0309ad10880f930df607a906e80e9d08d21047,
        0x09ba01290b640be5091f075c092c09870878077601d1030608f90fe00d0e0b8b,
        0x09e1066709ee0a3b0a890681040808370be510950df607a90da8078f0a080c66,
        0x00dc031306b4089e04b00f050c990c3f0ec403ef068d09870d0e08df0d0e069a,
        0x096d0f930b640bff091f0dc20e030c3f09930abc0df60d010f790d340d0e0c66,
        0x06260129087802c604fe02fa05b2083704b00347028503060387042f036e01d1,
    ),
    (
        0x05f3082a077606f509fb0e1c0b640f520ef8089e0d9b08040f050f860de9092c,
        0x0d6809120aaf0bbe0912018309460bcb0a5502ed036e08c509a00aaf0ca60bb1,
        0x0e840c25065a0fed0e6a107b0fac0c8009fb0f9f0bcb0d5b0c73025f0fb90633,
        0x0c1806670456095308df0e1c065a0ed108d206ce0b640aaf0c800ce702e00ca6,
        0x0b1610140ede0fd308df0eb70b4a097a0c730af00ac90aaf0c730ce70c32096d,
        0x03bb059802c6046305980674075c008e00f6062606b40456066706810354036e,
    ),
    (
        0x054b03fc05a5015d07830769108809060f2b0e50079c0fd30fed0d340db508f9,
        0x09e109a00a21033a078309390d820e0307690a080b570bbe0fd309d40b230ad6,
        0x0b7109a0068104490e5d0c1810950ffa07690e430619074207f70e7704490c4c,
        0x0c730bf2046302ed0e1c0c660e5d04f10e840e500e8408d20d010e77025f089e,
        0x0b710bf20eeb0bf20d750ed10d750b710bf209d4096d0d750cb309ba0ce70b30,
        0x02c603130449044906e8076907ea064d05bf015d0279074201430361047d0150,
    ),
    (
        0x09600517059801500e910ed10f52109505cc0cda0ccd0ec406a70f6c0fed091f,
        0x009b092c0aa202ac076907ea0b3d0bbe0b8b0c0c0d0e09530f930b0a0f5f0c18,
        0x0da80fd3019d0dc20b710be505a50bd80e5d02110db50ddc0633062607dd0fed,
        0x085e00cf0af00c320c590cc00f5204ca08ab0c660e770e360292024506a706db,
        0x091209ba0cda0f520b710bbe0d0e0b4a0df60ec40ca60eeb0ba40c4c0f5f0fe0,
        0x0489044906b403c807c304fe07830804059807020783024505f3064006f501aa,
    ),
    (
        0x06c10769074207d005b20d1a10140f790fc60fac0ffa0d9b0d010f93070e06db,
        0x0b1602920912048908c502e0025f0bf202b90ccd01aa0c4c0cda0f93092c0b3d,
        0x0e290c730c6610540204060c0d27018305cc10140bff0d9b096005e609930fd3,
        0x06c1074f0c4c0c18097a08910abc10950c730ed10c3f0ede049606190f790667,
        0x0b0a0bcb0c8d0f9f096d0d1a0eb70f5209ad0ccd0d9b0bbe0cda0b3d0dcf0ef8,
        0x06c1074f04f108510422028501c40702040806a703c807a9074f0347070e0565,
    ),
    (
        0x09ba064d008107a904bd0f520dc210540600060c0da810540ed10f9f1007102d,
        0x0912078f08d2032d082a012907f70c0c00e901b70102070e0b4a0c3f0b570bd8,
        0x09ba101409c70d9b0bbe0dc20d0e0f9f0ec40e1c0da8026c0d9b081009c70e43,
        0x0b3d06a706400f05049602fa0e840e4309600f45060c02380cc00abc00810e9d,
        0x0ddc0dcf0dcf0b7e0aa20f860c990d1a0b97097a09c70f860d9b0f2b0f930f93,
        0x0320010f02ed041501f806ce071b0489050a06740702018303ae064d01900211,
    ),
    (
        0x05a505d906f508040db506f50f860f380e501095092c091f0ca60f1e06a70eeb,
        0x09ad0af002c6057f019d02ed036e0bff096002e00aaf0b300a7c0ca60a210b30,
        0x011c0da80de90e5d09e1062607d00d9b0df60bbe01d103e2047d020409e10d01,
        0x064d0ede0ad606b40cf40e840cb30c180667026c0c4c0aa20c73069a06f50279,
        0x0c660fd30b710d4e09460c0c0e9d0f380c990b230f1e0c250b230c800da80ca6,
        0x071b0361081d016a061907b6078f079c053e07a9020406a7053e019d02b90489,
    ),
    (
        0x07b605e606ce07c30ffa109505a50fed0d0108ec0bb108f90be50d8f0bb10735,
        0x0b7e0d340804019000f6088509060960092c02b90a6f0aaf0d820af00a7c0b7e,
        0x06000bcb05a50fd3083707a90abc043c0a480c25025f021e0be506330c320dc2,
        0x0de906b4068d0626090608b802ac06260af00abc0cc00b710c3f0e2904220cf4,
        0x0d750b7e0e840f6c0ffa092c0b230b230be50c250cc00b8b0d0e0d8f0e100d8f,
        0x042f066706e8012901aa07a9060c015d03ae025202e001aa0885011c04e400dc,
    ),
    (
        0x05bf075c071b00f60d270d680ef8069a09530939089e071b05580640096009ba,
        0x013609d401d10b71069a09600d27094603c806ce092c02c60d410b160a950bcb,
        0x054b0fc610880e4304560456101402520de90be50d410a210d8f0e91068103a1,
        0x0c9909600aa20ad600cf0cda0ca60e5d02d306b406db0f050d820d820ba40252,
        0x0b3d0afd0d4e0fed09120fe00d820ce70b8b0ce70f860fe00d8f0b16097a0d27,
        0x0354078f03d5073505580837044904f104fe081d074f071b028506db033a0361,
    ),
    (
        0x0939096d0129078f05f30d8f0df6088505170d8f0e9107c30fb9095308ab0906,
        0x0d9b015d0252032008b80252008e0da807c302c6030603ef0b0a0fd30b0a0be5,
        0x023803610e100bcb09530c0c05bf0dcf0b23060005e60572090601b707ea01b7,
        0x02fa03610a890d5b02fa04bd0d0e04fe042f0e3604150f1204080408004e0456,
        0x09870b4a0e100ccd09530d8f0ac90cf40bcb0f930f520dcf0f9309870d5b0fd3,
        0x0415079c03fc053103c804bd060004fe0728069a057f06c1017702c602c601b7,
    ),
    (
        0x05cc0285072805b2109507f7098710140939068d07280c7304a30e360eb7096d,
        0x0b30094609ba09530d410c7304e409ad021109600b8b02d30c250fb90bd80c0c,
        0x05cc04fe07f70e770b300d0e0f930e5d0a2107b60cda06400c660abc07f70a7c,
        0x0d820d9b071b0e5d0c320d0e09600c4c0ccd00a8070202d3022b04a3042f054b,
        0x0d820b970d410e9d0d410b7e0bff0d9b0f1e0d820bf20d3409390d750c660da8,
        0x02ed05b2037b0804077607f707d0037b0681029f02c603fc0422074206ce054b,
    ),
    (
        0x012900dc036106c10cc00eb7075c0fac10140e430906065a06190f5f0f790d41,
        0x09390953015d0b570da80d1a03200ba408100a2e096d094608b80b3d0b160bff,
        0x0d2706330bbe06330dc209ad0c7303d50b970fe00e770f860d411007067401de,
        0x0c6604f10d8208910e6a0eb70f050ede04ca0b3d02b90ef80e770cf402b9068d,
        0x0a950f050d750d7509600b160d010dc20b160bbe0ce709ee0c8009120d010d41,
        0x07f7009b0415057f036e051704700783042204fe00b5069a065a023806740387,
    ),
    (
        0x015006ce00dc08d2057f0ede0e9d0fe00bf20c8d0ba409390f6c03130ef809e1,
        0x06f5086b097a05cc00e906ce0d680de906a7094601eb0d750993092c0f520b64,
        0x05980c18107b0f2b03c80c4c0e910d4103fc0fed04630b230bff066703d50674,
        0x0aaf0456097a0e7704d704d70ce70f120cc00463085e090602ed0c4c02520c4c,
        0x0aaf0be50eb70c320d270ba40b570b1609fb0b7e0d410cf409600f1e0e770dcf,
        0x0449088507f7050a058b04d7065a06db019002110572015d05650183077607f7,
    ),
    (
        0x050a060c068d097a096005f310540b640d4e0b160db506a70d4e0fd3065a075c,
        0x011c01b701f801f80c3f09ad0c590b23025207c3036109a00f520aa2091f106e,
        0x0df60b4a0f9f0b970c32078f0e360a140912041506000c18019006190640026c,
        0x0b300d1a0bcb104700810a7c0e360e840bcb0eb70f1208c50c990640043c0489,
        0x0d9b0ccd0f6c0ffa0b160b300f050b6409c70d680b640be508f909460db50f2b,
        0x07dd07dd0496029f0742069a059804ca06000681079c07b60804070203e2075c,
    ),
    (
        0x057f0449040809ba05cc06330f930be50c590e840ede07d0029206ce0f6c0bcb,
        0x02e00b5703c80bd8012908d20313008e07d0021e009b03c80c800b570d5b0fac,
        0x09c704630ddc0c59064005cc0aaf051706190da802520953086b04ca0fc6064d,
        0x0b7e04a30d010e430d820c4c0df6089e04960ccd030602e00aaf0d5b02c60b7e,
        0x0b230ed10cf40d5b0cda0ad609ad0f5f091f0dc20bb10ec40c4c0be50d4e0d34,
        0x03ef0600010f05bf03940735069a053e06ce074f07d0074f079c021e064d074f,
    ),
    (
        0x06e8079c00f601020e8407830ce7106e06740fe0058b052402d3106e0e290742,
        0x0081050a02ac0a6f03d5015d01aa0d4108df0b23019d0b4a0e9d096009930fd3,
        0x0d5b0f2b07b6104703d5042f05720211038706330c800cb3070e0f9f042f0667,
        0x07760a3b0e43107b08ec09ad0e2905650b230d9b0d9b042f04bd02e008b8065a,
        0x0ce70d680de90d9b0d1a0c730bf20e0309530d1a0f2b10070d340cc00f5209fb,
        0x077603c8064d0456074f0387026c01eb0320040806db068d00cf0489068d069a,
    ),
    (
        0x016a0081015001830d5b05310e430fb90cda04b005cc102d06f506a7079c0b64,
        0x04560517032d0cf403610aaf0bbe0bb100b5019d025f02e00d8f0ffa0d750ec4,
        0x0a2e10950b3d0de90c8d0ba402380ad6096d0fd3065a021102ed0fac04d7043c,
        0x10070b230b8b06a70abc0b8b0eeb04d7089e0a7c02d306f506a7031302380c80,
        0x0b4a0d4e0df610070abc0b570d1a0df60db50df60f050cc00b300bf20cc00c25,
        0x027906330702042f080405310667036e042f07b604f1057202e0022b010202e0,
    ),
    (
        0x07d000b5028501d10b970e9107830cc007760c590de90e29074f0d9b0600106e,
        0x095303610810078f0a890851017702fa019d0292029f01aa1007078310470ffa,
        0x0e360ffa0d82053e078f04080fe0066703060f5207c3065a036e01830306054b,
        0x0e360cb30885106102d30b0a09ad059807830449057f0d5b050a043c00e904fe,
        0x0bb10b160fd30da80bff0bd80d5b0ffa0d9b0b8b0d750df60b4a0d680d410d82,
        0x07d000f60470070204bd023807b6045603a105cc0252070e05a500dc06810804,
    ),
    (
        0x011c00a805f301900ac905a50ac90e84072806a705a50a95049607f70c3f06c1,
        0x019d0a2e029f07c30bd8032003ef00a8009b01eb0354033a0f0507420fac0fe0,
        0x0b300fed0b160d410d1a036e07a90d750470081d0a080eb70456023801eb0598,
        0x0a2e0bb10c250a2e0bd80b4a0a480f7903540e77049604ca03060306056506b4,
        0x0f520ef80bff0b570f120da8096d0f790912092c0ba40b7e0b640de909e10dc2,
        0x074f03940320060c073506330524071b065a06db036107280558037b050a05f3,
    ),
    (
        0x071b074200a8070e06e80e100d5b0f120e7706b4096d097a0e100c18032008ec,
        0x0a0809c7050a0ac908df050a0d41010f01eb00b5012901de0f120e9d103a091f,
        0x091f05980cb3101408df0d2705650598085e0eaa050a07ea0b57068105f30600,
        0x04080a480e50108804490ede0f860b9700b504bd09ee06db00cf00a8022b057f,
        0x0cda0bbe0cb30b8b0bcb0be50f860fed0b7e0b300be509460be50d5b09930d68,
        0x037b056501f8078307b606e807020496029f06ce069a0449019d03bb03ae0183,
    ),
    (
        0x04150572046301de0e100f120db50d010b3d0f380ce709ad0bbe05a5074f0ddc,
        0x0e36091f01aa07d00d9b021e01360394022b03ae0d41089e0ef8074f0f380ca6,
        0x0b7e0b710dc20fac0d9b0f450eaa060002fa0d7507ea04ca0408043c0e360a2e,
        0x0c250c660eb70dcf0af0021103471088037b043c029f0e290bf201770e5002e0,
        0x09530c180ed10b7109e10bf20f520d8f0d410d410c990dc20b710d410c80ffff,
        0x03d5042f0517055806ce070e01b70143070200a801770804027904bd071bffff,
    ),
    (
        0x03e2ffffffffffff0f52102d0e1c0eeb0cb308910a9508b80e8408f90af00ede,
        0x0d34069a02b9036e09060afd07d00c800143ffffffffffff0fe00fed0e9d0d75,
        0x0b16102d0d010ddcffff05bf05f3091fffff10070fac03aeffff05f303a10238,
        0x0d680e100c590f450a620e50ffff0f86082a0afdffff102d02b900cfffff0d01,
        0x0b570f1e0bbe0b640f6c0b4a0de9ffff092c0f450d68ffff0891ffffffffffff,
        0x057f070207760517019d03ef043cffff025204700524ffff0136ffffffffffff,
    ),
    (
        0xffffffffffffffff0ad60ec4078fffff0d0effffffffffff0517ffffffffffff,
        0x05d9ffffffffffff015dffffffffffffffffffffffffffff0ffa0ae30912ffff,
        0xffff0f9f0fd30d8fffff0facffffffffffff0361ffffffffffffffffffffffff,
        0x0a210eb7ffff0d41ffffffffffff04b0ffffffffffff0b57ffffffffffffffff,
        0x0f790cda0f1effff0e84ffffffffffff0c4cffffffffffffffffffffffffffff,
        0x011c018307d0ffff008effffffffffffffffffffffffffffffffffffffffffff,
    ),
    (
        0xffffffffffffffff101404bdffffffffffffffffffffffffffffffffffffffff,
        0xffffffffffffffffffffffffffffffffffffffffffffffff0fac070effffffff,
        0xffff10541007ffffffffffffffffffffffffffffffffffffffffffffffffffff,
        0x0ec4ffffffff103affffffffffffffffffffffffffffffffffffffffffffffff,
        0x1014ffffffffffffffffffffffffffffffffffffffffffffffffffffffffffff,
        0x07eaffffffffffffffffffffffffffffffffffffffffffffffffffffffffffff,
    ),
    (
        0xffffffffffffffff0f45ffffffffffffffffffffffffffffffffffffffffffff,
        0xffffffffffffffffffffffffffffffffffffffffffffffff071bffffffffffff,
        0xffff0e84ffffffffffffffffffffffffffffffffffffffffffffffffffffffff,
        0xffffffffffff0e91ffffffffffffffffffffffffffffffffffffffffffffffff,
        0xffffffffffffffffffffffffffffffffffffffffffffffffffffffffffffffff,
        0xffffffffffffffffffffffffffffffffffffffffffffffffffffffffffffffff,
    ),
)
SEMAPHORES = (
    (0, 10, 20, 30, 40, 50),
    (1, 11, 21, 31, 40, 51),
    (2, 12, 22, 32, 40, 52),
    (3, 13, 23, 33, 40, 53),
    (4, 14, 24, 34, 40, 54),
    (5, 15, 25, 35, 40, 55),
    (6, 16, 26, 36, 40, 56),
    (7, 17, 27, 37, 40, 57),
    (8, 18, 28, 38, 40, 58),
    (9, 19, 29, 39, 41, 59),
    (0, 10, 20, 30, 42, 60),
    (1, 11, 21, 31, 43, 61),
    (2, 12, 22, 32, 44, 62),
    (3, 13, 23, 33, 45, 63),
    (4, 14, 24, 34, 46, 64),
    (5, 15, 25, 35, 47, 65),
    (6, 16, 26, 36, 48, 66),
    (7, 17, 27, 37, 49, 67),
    (8, 18, 28, 38, 40, 50),
    (9, 19, 29, 39, 41, 51),
    (0, 10, 20, 30, 42, 52),
    (1, 11, 21, 31, 43, 53),
    (2, 12, 22, 32, 44, 54),
    (3, 13, 23, 33, 45, 55),
    (4, 14, 24, 34, 46, 56),
    (5, 15, 25, 35, 47, 57),
    (6, 16, 26, 36, 48, 58),
    (7, 17, 27, 37, 49, 59),
    (8, 18, 28, 38, 40, 60),
    (9, 19, 29, 39, 41, 61),
    (0, 10, 20, 30, 42, 62),
    (1, 11, 21, 31, 43, 63),
    (2, 12, 22, 32, 44, 64),
    (3, 13, 23, 33, 45, 65),
    (4, 14, 24, 34, 46, 66),
    (5, 15, 25, 35, 47, 67),
    (6, 16, 26, 36, 48, 50),
    (7, 17, 27, 37, 49, 51),
    (8, 18, 28, 38, 40, 52),
    (9, 19, 29, 39, 41, 53),
    (0, 10, 20, 30, 42, 54),
    (1, 11, 21, 31, 43, 55),
    (2, 12, 22, 32, 44, 56),
    (3, 13, 23, 33, 45, 57),
    (4, 14, 24, 34, 46, 58),
    (5, 15, 25, 35, 47, 59),
    (6, 16, 26, 36, 48, 60),
    (7, 17, 27, 37, 49, 61),
    (8, 18, 28, 38, 40, 62),
    (9, 19, 29, 39, 41, 63),
    (0, 10, 20, 30, 42, 64),
    (1, 11, 21, 31, 43, 65),
    (2, 12, 22, 32, 44, 66),
    (3, 13, 23, 33, 45, 67),
    (4, 14, 24, 34, 46, 50),
    (5, 15, 25, 35, 47, 51),
    (6, 16, 26, 36, 48, 52),
    (7, 17, 27, 37, 49, 53),
    (8, 18, 28, 38, 40, 54),
)
NEEDS = (
    (
        0xffffffffffffffffffffffffffffffff,
        0xffffffffffffffffffffffffffffffff,
        0xffffffffffffffffffffffffffffffff,
        0xffffffffffffffffffffffffffffffff,
        0xffffffffffffffffffffffffffffffff,
        0xffffffffffffffffffffffffffffffff,
    ),
    (
        0xffffffffffffffffffffffffffffffff,
        0xffffffffffffffffffffffffffffffff,
        0xffffffffffffffffffffffffffffffff,
        0xffffffffffffffffffffffffffffffff,
        0xffffffffffffffffffffffffffffffff,
        0xffffffffffffffffffffffffffffffff,
    ),
    (
        0xffffffffffffffffffffffffffffffff,
        0xffffffffffffffffffffffffffffffff,
        0xffffffffffffffffffffffffffffffff,
        0xffffffffffffffffffffffffffffffff,
        0xffffffffffffffffffffffffffffffff,
        0xffffffffffffffffffffffffffffffff,
    ),
    (
        0xffffffffffffffffffffffffffffffff,
        0xffffffffffffffffffffffffffffffff,
        0xffffffffffffffffffffffffffffffff,
        0xffffffffffffffffffffffffffffffff,
        0xffffffffffffffffffffffffffffffff,
        0xffffffffffffffffffffffffffffffff,
    ),
    (
        0xffffffffffffffffffffffff0000ff00,
        0xffffffffffffffffffffffffffffffff,
        0xffffff14ff0a0affff0a0affff0a0a14,
        0xffffffffffffff0affffff0affffff0a,
        0xffffffffffffffffffffffffffffffff,
        0x32323232323232323232323232323232,
    ),
    (
        0xffffffffffffffffffffffffffffffff,
        0xffffffffffffffffffffffffffffffff,
        0xffffffffffffffffffffffffffffffff,
        0xffffffffffffffffffffffffffffffff,
        0xffffffffffffffffffffffffffffffff,
        0x33333333333333333333333333333333,
    ),
    (
        0xffffffffffffffffffffffffffffffff,
        0xffffffffffffffffffffffffffffffff,
        0xffffffffffffffffffffffffffffffff,
        0xffffffffffffffffffffffffffffffff,
        0xffffffffffffffffffffffffffffffff,
        0x34343434343434343434343434343434,
    ),
    (
        0xffffffffffffffffffffffffffffffff,
        0xffffffffffffffffffffffffffffffff,
        0xffffffffffffffffffffffffffffffff,
        0xffffffffffffffffffffffffffffffff,
        0xffffffffffffffffffffffffffffffff,
        0x35353535353535353535353535353535,
    ),
    (
        0x221804ff363636ff36043604ff040404,
        0xff222222ffffffffff0effffff2222ff,
        0x180e0e180e0e0e36ffff0e36ff3636ff,
        0xffffff0effff220e0e22220e0effff36,
        0xffffffffff22ff22ffffffffffffff22,
        0xffffffffffffffffffffffffffffffff,
    ),
    (
        0xff0505ff3705ff0537ffffffffffffff,
        0x191923ffff0fffffff19ffff373737ff,
        0xff0f0f37ff3737ffff3737ffffffffff,
        0xffffff0fff23ff370fffff370fffff37,
        0xffffffffffffffffffffffffffffffff,
        0xffffffffffffffffffffffffffffffff,
    ),
    (
        0x0606060638ffffff38ff06ffffffffff,
        0x1affff2410ff1024ffffff24383838ff,
        0xff101038ff3838ffff3838ffffffffff,
        0xff24ff10ffff2438ff242438ff24ff38,
        0xffffffffffffffffffff10ffffffffff,
        0xffffffffffffffffffffffffffffffff,
    ),
    (
        0xffffffffffffffffffffffff39ffffff,
        0x251bff25ffffffffffffffffffffffff,
        0x1bffff39ff3939ffff3939ffffffffff,
        0xffffffffff11253911ffff39ffffffff,
        0xffffffffffffffffff11ffff0725ffff,
        0xffffffffffffffffffffffffffffffff,
    ),
    (
        0xffffffffffffffffffff1cffff1cffff,
        0xffff1c12ffffffffffffffffffff1cff,
        0xffffffffff1c1cffffffffffffffffff,
        0x08080808122608ff3affffff12ffffff,
        0xffffff1cffffff12261cffffffff26ff,
        0x3a3aff3a3a3a3a3aff3a3a3a3a3a3a3a,
    ),
    (
        0xffffffff091d1dff091d09ffffffffff,
        0xffffffffffffffffffffffffffff1dff,
        0xffff1dffffffffffffffffffffffffff,
        0x13ff3bffffff13ffffffffffffffffff,
        0xffffff1dffffffff27ffffffffffffff,
        0x3b3bff3b3b3b3bff3b3bffff3bff3bff,
    ),
    (
        0xffffffffffff14ffffffffffffffffff,
        0xffffff0affffffffffffffffffffffff,
        0xffff14ffffffffffffffffffffffffff,
        0x000affffffff3cffffff3cffffffffff,
        0xffffff14ff14ff1eff00ffffffffffff,
        0x3c3c3c3cff3cffff3cffffff3c3c3c3c,
    ),
    (
        0xffffffffff1515ffffffffffffffffff,
        0xff3dffffffffffffffffffffffffffff,
        0xffff15ffffffffffffffffffffffffff,
        0xffffffffffffffffffffffffffffffff,
        0xffffff15ffffffffffffffffffffffff,
        0x3dff3dff3d3d3dffffff3d3d3d3d3d3d,
    ),
    (
        0xffffffff3e16ff20ffffffffffffffff,
        0xffffffffffffffffffffffff2016ffff,
        0xff160cffffffffffffffffffffffffff,
        0x0cff2002ffffffffffffffffffffffff,
        0x2020ff16ffffffffffffffffffffffff,
        0xffffffffffffffffffffffffffffffff,
    ),
    (
        0xffffffffffffffffffffffffffffffff,
        0xffffffffffffffffffffffffffffffff,
        0xff3fffffffffffffffffffffffffffff,
        0xffff3fffffffffffffffffffffffffff,
        0xffffffffffffffffffffffffffffffff,
        0xffffffffffffffffffffffffffffffff,
    ),
    (
        0xffffffffffffffffffffffffffffffff,
        0xffffffffffffffffffffffffffffffff,
        0xffffffffffffffffffffffffffffffff,
        0xffffff22ffffffffffffffffffffffff,
        0xffffffffffffffffffffffffffffffff,
        0xffffffffffffffffffffffffffffffff,
    ),
    (
        0xffffffffffffffffffffffffffffffff,
        0xffffffffffffffffffffffffffffffff,
        0xffffffffffffffffffffffffffffffff,
        0xffffffffffffffffffffffffffffffff,
        0xffffffffffffffffffffffffffffffff,
        0xffffffffffffffffffffffffffffffff,
    ),
    (
        0xffffffffffffffffffffffffffffffff,
        0xffffffffffffffffffffffffffffffff,
        0xffffffffffffffffffffffffffffffff,
        0xffffffffffffffffffffffffffffffff,
        0xffffffffffffffffffffffffffffffff,
        0xffffffffffffffffffffffffffffffff,
    ),
    (
        0xffffffffffffffffffffffffffffffff,
        0xffffffffffffffffffffffffffffffff,
        0xffffffffffffffffffffffffffffffff,
        0xffffffffffffffffffffffffffffffff,
        0xffffffffffffffffffffffffffffffff,
        0xffffffffffffffffffffffffffffffff,
    ),
    (
        0xffffffffffffffffffffffffffffffff,
        0xffffffffffffffffffffffffffffffff,
        0xffffffffffffffffffffffffffffffff,
        0xffffffffffffffffffffffffffffffff,
        0xffffffffffffffffffffffffffffffff,
        0xffffffffffffffffffffffffffffffff,
    ),
    (
        0xffffffffffffffffffffffffffffffff,
        0xffffffffffffffffffffffffffffffff,
        0xffffffffffffffffffffffffffffffff,
        0xffffffffffffffffffffffffffffffff,
        0xffffffffffffffffffffffffffffffff,
        0xffffffffffffffffffffffffffffffff,
    ),
    (
        0xffffffffffffffffffffffffffffffff,
        0xffffffffffffffffffffffffffffffff,
        0xffffffffffffffffffffffffffffffff,
        0xffffffffffffffffffffffffffffffff,
        0xffffffffffffffffffffffffffffffff,
        0xffffffffffffffffffffffffffffffff,
    ),
    (
        0xffffffffffffffffffffffffffffffff,
        0xffffffffffffffffffffffffffffffff,
        0xffffffffffffffffffffffffffffffff,
        0xffffffffffffffffffffffffffffffff,
        0xffffffffffffffffffffffffffffffff,
        0xffffffffffffffffffffffffffffffff,
    ),
    (
        0xffffffffffffffffffffffffffffffff,
        0xffffffffffffffffffffffffffffffff,
        0xffffffffffffffffffffffffffffffff,
        0xffffffffffffffffffffffffffffffff,
        0xffffffffffffffffffffffffffffffff,
        0xffffffffffffffffffffffffffffffff,
    ),
    (
        0xffffffffffffffffffffffffffffffff,
        0xffffffffffffffffffffffffffffffff,
        0xffffffffffffffffffffffffffffffff,
        0xffffffffffffffffffffffffffffffff,
        0xffffffffffffffffffffffffffffffff,
        0xffffffffffffffffffffffffffffffff,
    ),
    (
        0xffffffffffffffffffffffffffffffff,
        0xffffffffffffffffffffffffffffffff,
        0xffffffffffffffffffffffffffffffff,
        0xffffffffffffffffffffffffffffffff,
        0xffffffffffffffffffffffffffffffff,
        0xffffffffffffffffffffffffffffffff,
    ),
    (
        0xffffffffffffffffffffffffffffffff,
        0xffffffffffffffffffffffffffffffff,
        0xffffffffffffffffffffffffffffffff,
        0xffffffffffffffffffffffffffffffff,
        0xffffffffffffffffffffffffffffffff,
        0xffffffffffffffffffffffffffffffff,
    ),
    (
        0xffffffffffffffffffffffffffffffff,
        0xffffffffffffffffffffffffffffffff,
        0xffffffffffffffffffffffffffffffff,
        0xffffffffffffffffffffffffffffffff,
        0xffffffffffffffffffffffffffffffff,
        0xffffffffffffffffffffffffffffffff,
    ),
    (
        0xffffffffffffffffffffffffffffffff,
        0xffffffffffffffffffffffffffffffff,
        0xffffffffffffffffffffffffffffffff,
        0xffffffffffffffffffffffffffffffff,
        0xffffffffffffffffffffffffffffffff,
        0xffffffffffffffffffffffffffffffff,
    ),
    (
        0xffffffffffffffffffffffffffffffff,
        0xffffffffffffffffffffffffffffffff,
        0xffffffffffffffffffffffffffffffff,
        0xffffffffffffffffffffffffffffffff,
        0xffffffffffffffffffffffffffffffff,
        0xffffffffffffffffffffffffffffffff,
    ),
    (
        0xffffffffffffffffffffffffffffffff,
        0xffffffffffffffffffffffffffffffff,
        0xffffffffffffffffffffffffffffffff,
        0xffffffffffffffffffffffffffffffff,
        0xffffffffffffffffffffffffffffffff,
        0xffffffffffffffffffffffffffffffff,
    ),
    (
        0xffffffffffffffffffffffffffffffff,
        0xffffffffffffffffffffffffffffffff,
        0xffffffffffffffffffffffffffffffff,
        0xffffffffffffffffffffffffffffffff,
        0xffffffffffffffffffffffffffffffff,
        0xffffffffffffffffffffffffffffffff,
    ),
    (
        0xffffffffffffffffffffffffffffffff,
        0xffffffffffffffffffffffffffffffff,
        0xffffffffffffffffffffffffffffffff,
        0xffffffffffffffffffffffffffffffff,
        0xffffffffffffffffffffffffffffffff,
        0xffffffffffffffffffffffffffffffff,
    ),
    (
        0xffffffffffffffffffffffffffffffff,
        0xffffffffffffffffffffffffffffffff,
        0xffffffffffffffffffffffffffffffff,
        0xffffffffffffffffffffffffffffffff,
        0xffffffffffffffffffffffffffffffff,
        0xffffffffffffffffffffffffffffffff,
    ),
    (
        0xffffffffffffffffffffffffffffffff,
        0xffffffffffffffffffffffffffffffff,
        0xffffffffffffffffffffffffffffffff,
        0xffffffffffffffffffffffffffffffff,
        0xffffffffffffffffffffffffffffffff,
        0xffffffffffffffffffffffffffffffff,
    ),
    (
        0xffffffffffffffffffffffffffffffff,
        0xffffffffffffffffffffffffffffffff,
        0xffffffffffffffffffffffffffffffff,
        0xffffffffffffffffffffffffffffffff,
        0xffffffffffffffffffffffffffffffff,
        0xffffffffffffffffffffffffffffffff,
    ),
    (
        0xffffffffffffffffffffffffffffffff,
        0xffffffffffffffffffffffffffffffff,
        0xffffffffffffffffffffffffffffffff,
        0xffffffffffffffffffffffffffffffff,
        0xffffffffffffffffffffffffffffffff,
        0xffffffffffffffffffffffffffffffff,
    ),
    (
        0xffffffffffffffffffffffffffffffff,
        0xffffffffffffffffffffffffffffffff,
        0xffffffffffffffffffffffffffffffff,
        0xffffffffffffffffffffffffffffffff,
        0xffffffffffffffffffffffffffffffff,
        0xffffffffffffffffffffffffffffffff,
    ),
    (
        0xffffffffffffffffffffffffffffffff,
        0xffffffffffffffffffffffffffffffff,
        0xffffffffffffffffffffffffffffffff,
        0xffffffffffffffffffffffffffffffff,
        0xffffffffffffffffffffffffffffffff,
        0xffffffffffffffffffffffffffffffff,
    ),
    (
        0xffffffffffffffffffffffffffffffff,
        0xffffffffffffffffffffffffffffffff,
        0xffffffffffffffffffffffffffffffff,
        0xffffffffffffffffffffffffffffffff,
        0xffffffffffffffffffffffffffffffff,
        0xffffffffffffffffffffffffffffffff,
    ),
    (
        0xffffffffffffffffffffffffffffffff,
        0xffffffffffffffffffffffffffffffff,
        0xffffffffffffffffffffffffffffffff,
        0xffffffffffffffffffffffffffffffff,
        0xffffffffffffffffffffffffffffffff,
        0xffffffffffffffffffffffffffffffff,
    ),
    (
        0xffffffffffffffffffffffffffffffff,
        0xffffffffffffffffffffffffffffffff,
        0xffffffffffffffffffffffffffffffff,
        0xffffffffffffffffffffffffffffffff,
        0xffffffffffffffffffffffffffffffff,
        0xffffffffffffffffffffffffffffffff,
    ),
    (
        0xffffffffffffffffffffffffffffffff,
        0xffffffffffffffffffffffffffffffff,
        0xffffffffffffffffffffffffffffffff,
        0xffffffffffffffffffffffffffffffff,
        0xffffffffffffffffffffffffffffffff,
        0xffffffffffffffffffffffffffffffff,
    ),
    (
        0xffffffffffffffffffffffffffffffff,
        0xffffffffffffffffffffffffffffffff,
        0xffffffffffffffffffffffffffffffff,
        0xffffffffffffffffffffffffffffffff,
        0xffffffffffffffffffffffffffffffff,
        0xffffffffffffffffffffffffffffffff,
    ),
    (
        0xffffffffffffffffffffffffffffffff,
        0xffffffffffffffffffffffffffffffff,
        0xffffffffffffffffffffffffffffffff,
        0xffffffffffffffffffffffffffffffff,
        0xffffffffffffffffffffffffffffffff,
        0xffffffffffffffffffffffffffffffff,
    ),
    (
        0xffffffffffffffffffffffffffffffff,
        0xffffffffffffffffffffffffffffffff,
        0xffffffffffffffffffffffffffffffff,
        0xffffffffffffffffffffffffffffffff,
        0xffffffffffffffffffffffffffffffff,
        0xffffffffffffffffffffffffffffffff,
    ),
    (
        0xffffffffffffffffffffffffffffffff,
        0xffffffffffffffffffffffffffffffff,
        0xffffffffffffffffffffffffffffffff,
        0xffffffffffffffffffffffffffffffff,
        0xffffffffffffffffffffffffffffffff,
        0xffffffffffffffffffffffffffffffff,
    ),
    (
        0xffffffffffffffffffffffffffffffff,
        0xffffffffffffffffffffffffffffffff,
        0xff3cffffffffffffffffffffffffffff,
        0xffffffffffffffffffffffffffffffff,
        0xffffffffffffffffffffffffffffffff,
        0xffffffffffffffffffffffffffffffff,
    ),
    (
        0xffffffffffffffffffffffffffffffff,
        0xffffffffffffffffffffffffffffffff,
        0xffffffffffffffffffffffffffffffff,
        0xffffffffffffffffffffffffffffffff,
        0xffffffffffffffffffffffffffffffff,
        0xffffffffffffffffffffffffffffffff,
    ),
    (
        0xffffffffffffffffffffffffffffffff,
        0xffffffffffffffffffffffffffffffff,
        0xffffffffffffffffffffffffffffffff,
        0xffffffffffffffffffffffffffffffff,
        0xffffffffffffffffffffffffffffffff,
        0xffffffffffffffffffffffffffffffff,
    ),
    (
        0xffffffffffffffffffffffffffffffff,
        0xffffffffffffffffffffffffffffffff,
        0xffffffffffffffffffffffffffffffff,
        0xffffffffffffffffffffffffffffffff,
        0xffffffffffffffffffffffffffffffff,
        0xffffffffffffffffffffffffffffffff,
    ),
    (
        0xffffffffffffffffffffffffffffffff,
        0xffffffffffffffffffffffffffffffff,
        0xffffffffffffffffffffffffffffffff,
        0xffffffffffffffffffffffffffffffff,
        0xffffffffffffffffffffffffffffffff,
        0xffffffffffffffffffffffffffffffff,
    ),
    (
        0xffffffffffffffffffffffffffffffff,
        0xffffffffffffffffffffffffffffffff,
        0xffffffffffffffffffffffffffffffff,
        0xffffffffffffffffffffffffffffffff,
        0xffffffffffffffffffffffffffffffff,
        0xffffffffffffffffffffffffffffffff,
    ),
    (
        0xffffffffffffffffffffffffffffffff,
        0xffffffffffffffffffffffffffffffff,
        0xffffffffffffffffffffffffffffffff,
        0xffffffffffffffffffffffffffffffff,
        0xffffffffffffffffffffffffffffffff,
        0xffffffffffffffffffffffffffffffff,
    ),
    (
        0xffffffffffffffffffffffffffffffff,
        0xffffffffffffffffffffffffffffffff,
        0xffffffffffffffffffffffffffffffff,
        0xffffffffffffffffffffffffffffffff,
        0xffffffffffffffffffffffffffffffff,
        0xffffffffffffffffffffffffffffffff,
    ),
    (
        0xffffffffffffffffffffffffffffffff,
        0xffffffffffffffffffffffffffffffff,
        0xffffffffffffffffffffffffffffffff,
        0xffffffffffffffffffffffffffffffff,
        0xffffffffffffffffffffffffffffffff,
        0xffffffffffffffffffffffffffffffff,
    ),
)
LATE = (
    (0x0002, 0x0888, 0x0110, 0x7777, 0x0000, 0x0000),
    (0x000f, 0x0fff, 0x1111, 0x7777, 0x0000, 0x0000),
    (0x000f, 0x0fff, 0x1111, 0x7777, 0x0000, 0x0000),
    (0x000f, 0x0fff, 0x1111, 0x7777, 0x0000, 0x0000),
    (0xdfa8, 0x8007, 0x2fff, 0x0898, 0x0000, 0xf048),
    (0x9aff, 0x8b77, 0x3fbf, 0xdbff, 0x0000, 0xe000),
    (0x0fdf, 0x85df, 0x7fff, 0xac8b, 0x0000, 0xe000),
    (0xfff7, 0xfb3f, 0x3fff, 0x6dfb, 0x0000, 0xe887),
    (0x0dff, 0xe6f7, 0xc999, 0xfb7d, 0x7fff, 0x2000),
    (0xf75f, 0x7dff, 0xc9bd, 0xff7f, 0x37ff, 0x0135),
    (0x7fbf, 0xafff, 0xc9ff, 0xfeff, 0x5f7f, 0x0950),
    (0xffff, 0xffff, 0xc9ff, 0xffff, 0x17ff, 0x11c0),
    (0xefff, 0x5fff, 0xabfb, 0x1ef7, 0x3fff, 0xf7ff),
    (0xffff, 0xffff, 0xffff, 0xffff, 0x3fff, 0x9fff),
    (0xffff, 0xffff, 0xffff, 0xefff, 0x3fff, 0xffff),
    (0xffff, 0xffff, 0xffff, 0xffff, 0x3fff, 0xffff),
    (0xffff, 0xffff, 0xffff, 0xffff, 0xffff, 0xffff),
    (0xffff, 0xffff, 0xffff, 0xffff, 0xffff, 0xffff),
    (0xffff, 0xffff, 0xffff, 0xffff, 0xffff, 0xffff),
    (0xffff, 0xffff, 0xffff, 0xffff, 0xffff, 0xffff),
    (0xffff, 0xffff, 0xffff, 0xffff, 0xffff, 0xffff),
    (0xffff, 0xffff, 0xffff, 0xffff, 0xffff, 0xffff),
    (0xffff, 0xffff, 0xffff, 0xffff, 0xffff, 0xffff),
    (0xffff, 0xffff, 0xffff, 0xffff, 0xffff, 0xffff),
    (0xffff, 0xffff, 0xffff, 0xffff, 0xffff, 0xffff),
    (0xffff, 0xffff, 0xffff, 0xffff, 0xffff, 0xffff),
    (0xffff, 0xffff, 0xffff, 0xffff, 0xffff, 0xffff),
    (0xffff, 0xffff, 0xffff, 0xffff, 0xffff, 0xffff),
    (0xffff, 0xffff, 0xffff, 0xffff, 0xffff, 0xffff),
    (0xffff, 0xffff, 0xffff, 0xffff, 0xffff, 0xffff),
    (0xffff, 0xffff, 0xffff, 0xffff, 0xffff, 0xffff),
    (0xffff, 0xffff, 0xffff, 0xffff, 0xffff, 0xffff),
    (0xffff, 0xffff, 0xffff, 0xffff, 0xffff, 0xffff),
    (0xffff, 0xffff, 0xffff, 0xffff, 0xffff, 0xffff),
    (0xffff, 0xffff, 0xffff, 0xffff, 0xffff, 0xffff),
    (0xffff, 0xffff, 0xffff, 0xffff, 0xffff, 0xffff),
    (0xffff, 0xffff, 0xffff, 0xffff, 0xffff, 0xffff),
    (0xffff, 0xffff, 0xffff, 0xffff, 0xffff, 0xffff),
    (0xffff, 0xffff, 0xffff, 0xffff, 0xffff, 0xffff),
    (0xffff, 0xffff, 0xffff, 0xffff, 0xffff, 0xffff),
    (0xffff, 0xffff, 0xffff, 0xffff, 0xffff, 0xffff),
    (0xffff, 0xffff, 0xffff, 0xffff, 0xffff, 0xffff),
    (0xffff, 0xffff, 0xffff, 0xffff, 0xffff, 0xffff),
    (0xffff, 0xffff, 0xffff, 0xffff, 0xffff, 0xffff),
    (0xffff, 0xffff, 0xffff, 0xffff, 0xffff, 0xffff),
    (0xffff, 0xffff, 0xffff, 0xffff, 0xffff, 0xffff),
    (0xffff, 0xffff, 0xffff, 0xffff, 0xffff, 0xbfff),
    (0xffff, 0xffff, 0xffff, 0xffff, 0xffff, 0xffff),
    (0xffff, 0xffff, 0xffff, 0xffff, 0xffff, 0xffff),
    (0xffff, 0xffff, 0xffff, 0xffff, 0xffff, 0xffff),
    (0xffff, 0xffff, 0xffff, 0xffff, 0xffff, 0xffff),
    (0xffff, 0xffff, 0xffff, 0xffff, 0xffff, 0xffff),
    (0xffff, 0xffff, 0xffff, 0xffff, 0xffff, 0xffff),
    (0xffff, 0xffff, 0xffff, 0xffff, 0xffff, 0xffff),
    (0xffff, 0xffff, 0xffff, 0xffff, 0xfffe, 0xfffe),
    (0xfff8, 0xfff8, 0xfeee, 0xfeee, 0xfee8, 0xfee8),
    (0xe880, 0xe880, 0xe880, 0xe880, 0xe880, 0xe800),
    (0xc000, 0xc000, 0xc000, 0xc000, 0x8000, 0x8000),
    (0x8000, 0x8000, 0x8000, 0x8000, 0x0000, 0x0000),
)
LATE_BY = 5
NO_WAIT = 0xFF
GAIN_STEP = 2
SLOTS = 33
UNITS = 129
UNIT = 16
LANES = 128
STARTS = (0, 13, 26, 39, 52, 65, 78, 91, 104, 117)
OPPOSITE = (1, 0, 3, 2, 5, 4)
ORDER = (5, 3, 1, 2, 0, 4)
SENDS = 3
NOTHING = 0xFFFF


SIZES = dict(zip(STARTS, (b - a for a, b in zip(STARTS, STARTS[1:] + (UNITS,)))))


def size_of(entry):
    return 0 if entry == NOTHING else SIZES[entry % UNITS]


def neighbour_position(p, d):
    x, y = divmod(p, 4)
    if d == 0:
        x = (x + 1) % 4
    if d == 1:
        x = (x + 3) % 4
    if d == 2:
        y = (y + 1) % 4
    if d == 3:
        y = (y + 3) % 4
    return 4 * x + y


def signed(word):
    return word - (1 << 32) if word >= 1 << 31 else word


def entries(step, d):
    return [(PLAN[step][d] >> (16 * p)) & 0xFFFF for p in range(16)]


def mask_of(flags):
    return sum(1 << p for p, flag in enumerate(flags) if flag)


def gather_kernel(re_ref, im_ref, held, part, part_in, send_sem, recv_sem, load_sem, pair_sem):
    bins = re_ref.shape[0]
    tiles = re_ref.shape[1]
    fr = lax.axis_index("fr")
    sr = lax.axis_index("sr")
    sc = lax.axis_index("sc")
    z, x, y = sr // 4, sr % 4, sc
    p = 4 * x + y
    steps = len(PLAN)

    xp, xm = (x + 1) % 4, (x + 3) % 4
    yp, ym = (y + 1) % 4, (y + 3) % 4
    zp, zm = (z + 1) % 4, (z + 3) % 4
    targets = (
        (fr, 4 * z + xp, y),
        (fr, 4 * z + xm, y),
        (fr, sr, yp),
        (fr, sr, ym),
        (fr, 4 * zp + x, y),
        (fr, 4 * zm + x, y),
    )
    ahead = (4 * (xp - x), 4 * (xm - x), yp - y, ym - y, 16, -16)
    twin = (1 - fr, sr, sc)
    shift = 16 * (y % 2)

    barrier = pltpu.get_barrier_semaphore()
    for device in targets + (twin,):
        pl.semaphore_signal(barrier, inc=1, device_id=device, device_id_type=MESH)
    loads = []
    for f in range(bins):
        for half in range(2):
            for i, ref in enumerate((re_ref, im_ref)):
                place = 4 * f + 2 * half + i
                source = ref.at[f, :, :, pl.ds(half * LANES, LANES)]
                target = held.at[pl.ds(place * tiles, tiles)]
                loads.append(pltpu.make_async_copy(source, target, load_sem.at[0]))
    for load in loads:
        load.start()

    everything = held.at[pl.ds(0, UNITS - 1)]
    pltpu.make_async_copy(everything, everything, load_sem.at[0]).wait()
    pl.semaphore_wait(barrier, 7)

    def chosen(step, d):
        words = [jnp.int32(signed((PLAN[step][d] >> (32 * i)) & 0xFFFFFFFF)) for i in range(8)]
        words = [jnp.where(y < 2, words[i], words[i + 1]) for i in range(0, 8, 2)]
        word = jnp.where(
            x < 2,
            jnp.where(x == 0, words[0], words[1]),
            jnp.where(x == 2, words[2], words[3]),
        )
        return lax.shift_right_logical(word, shift) & 0xFFFF

    def needed(step, d):
        words = [jnp.int32(signed((NEEDS[step][d] >> (32 * i)) & 0xFFFFFFFF)) for i in range(4)]
        word = jnp.where(
            x < 2,
            jnp.where(x == 0, words[0], words[1]),
            jnp.where(x == 2, words[2], words[3]),
        )
        return lax.shift_right_logical(word, 8 * y) & 0xFF

    def guarded(mask, action):
        if mask == 0:
            return
        if mask == 0xFFFF:
            action()
            return
        pl.when((lax.shift_right_logical(jnp.int32(mask), p) & 1) == 1)(action)

    def transfer(step, d, source, target, size, arrival):
        return pltpu.make_async_remote_copy(
            src_ref=held.at[pl.ds(source, size)],
            dst_ref=held.at[pl.ds(target, size)],
            send_sem=send_sem.at[SENDS * d + step % SENDS],
            recv_sem=recv_sem.at[arrival],
            device_id=targets[d],
            device_id_type=MESH,
        )

    def for_each_size(sizes, action, among=0xFFFF):
        for size in sorted(set(sizes) - {0}):
            guarded(mask_of(v == size for v in sizes) & among, functools.partial(action, size))

    def send(step, d):
        waits = mask_of((NEEDS[step][d] >> (8 * q)) & 255 != NO_WAIT for q in range(16))

        def arrived(size):
            transfer(step, d, 0, UNITS, size, needed(step, d)).wait_recv()

        def action(size):
            source = chosen(step, d)
            transfer(step, d, source, source - UNITS * ahead[d], size, SEMAPHORES[step][d]).start()

        sizes = [size_of(v) for v in entries(step, d)]
        for_each_size(sizes, arrived, waits)
        for_each_size(sizes, action)

    def receive(step, d):
        sent = [size_of(v) for v in entries(step, d)]
        coming = [sent[neighbour_position(q, OPPOSITE[d])] for q in range(16)]
        for_each_size(coming, lambda size: transfer(step, d, 0, UNITS, size, SEMAPHORES[step][d]).wait_recv(), LATE[step][d])

    def finish(step, d):
        sent = [size_of(v) for v in entries(step, d)]
        for_each_size(sent, lambda size: transfer(step, d, 0, UNITS, size, SEMAPHORES[step][d]).wait_send())

    exchange = pltpu.make_async_remote_copy(
        src_ref=part,
        dst_ref=part_in,
        send_sem=pair_sem.at[0],
        recv_sem=pair_sem.at[1],
        device_id=twin,
        device_id_type=MESH,
    )

    for step in range(steps):
        if step >= LATE_BY:
            for d in range(6):
                receive(step - LATE_BY, d)
        for d in ORDER:
            if step >= SENDS:
                finish(step - SENDS, d)
            send(step, d)
        if step == 0:
            total = jnp.zeros((tiles, UNIT, LANES), jnp.float32)
            for i in range(4 * bins):
                piece = held[pl.ds(i * tiles, tiles)].astype(jnp.float32)
                total += piece * piece
            total = total.reshape(tiles * UNIT, LANES)
            power = jnp.sum(total.T, axis=0, keepdims=True)
            part[...] = jnp.broadcast_to(power, part.shape)
            exchange.start()
        if step == GAIN_STEP:
            exchange.wait()
            power = part[...] + part_in[...]
            gain = 1.0 / jnp.sqrt(power * (1.0 / 2048.0))
            gain = jnp.concatenate([gain, gain], axis=0)
            high = gain.astype(jnp.bfloat16).astype(jnp.float32)
            middle = (gain - high).astype(jnp.bfloat16).astype(jnp.float32)
            low = gain - high - middle
            row = lax.broadcasted_iota(jnp.int32, (UNIT, LANES), 0)
            rest = jnp.where(row == 1, middle, low)
            held[UNITS - 1] = jnp.where(row == 0, high, rest).astype(jnp.bfloat16)
    for step in range(steps - LATE_BY, steps):
        for d in range(6):
            receive(step, d)
    for step in range(steps - SENDS, steps):
        for d in range(6):
            finish(step, d)


def gathered(re, im):
    bins, tiles = re.shape[:2]
    steps = len(PLAN)
    return pl.pallas_call(
        gather_kernel,
        out_shape=jax.ShapeDtypeStruct((SLOTS * UNITS, UNIT, LANES), jnp.bfloat16),
        in_specs=[pl.BlockSpec(memory_space=pltpu.HBM)] * 2,
        out_specs=pl.BlockSpec(memory_space=pltpu.VMEM),
        scratch_shapes=[
            pltpu.VMEM((8, 128), jnp.float32),
            pltpu.VMEM((8, 128), jnp.float32),
            pltpu.SemaphoreType.DMA((6 * SENDS,)),
            pltpu.SemaphoreType.DMA((max(map(max, SEMAPHORES)) + 1,)),
            pltpu.SemaphoreType.DMA((1,)),
            pltpu.SemaphoreType.DMA((2,)),
        ],
        compiler_params=pltpu.CompilerParams(
            collective_id=0, has_side_effects=True, vmem_limit_bytes=24 << 20
        ),
        name="gather_blocks",
    )(re, im)


GROUP = 11


def gain_row(tile):
    wide = tile.astype(jnp.float32)
    return wide[0:1] + wide[1:2] + wide[2:3]


def spectra(held, f, first):
    halves = [held[pl.ds(first + 32 * f + 16 * h, 16)].reshape(256, LANES) for h in range(2)]
    return jnp.concatenate(halves, axis=1)


def cross_kernel(plan, held, out, order, staged, own_column, sem, order_sem):
    bins = out.shape[0]
    fetch = pltpu.make_async_copy(plan, order, order_sem)
    fetch.start()
    own_row = gain_row(held[UNITS - 1]) * (1.0 / 16.0)
    own_column[...] = jnp.broadcast_to(own_row, (128, 128)).T
    fetch.wait()

    def group(i, carry):
        for j in range(GROUP):
            place = i * GROUP + j
            first = order[0, place] * UNITS
            weight = own_column[...] * gain_row(held[first + UNITS - 1])
            for f in range(bins):
                mine, other = spectra(held, f, 0), spectra(held, f, first)
                full = lax.dot_general(
                    mine, other, (((1,), (1,)), ((), ())), preferred_element_type=jnp.float32
                )
                staged[place, f, :, :128] = (full[:128, :128] + full[128:, 128:]) * weight
                staged[place, f, :, 128:] = (full[128:, :128] - full[:128, 128:]) * weight
            pltpu.make_async_copy(staged.at[place], out.at[:, place], sem).start()
        return carry

    lax.fori_loop(0, SLOTS // GROUP, group, 0)
    pltpu.make_async_copy(staged, staged, sem).wait()


def local(spec_re, spec_im, offsets):
    bins, rows, segs = spec_re.shape
    tiles = rows // UNIT
    re = spec_re.reshape(bins, tiles, UNIT, segs)
    im = spec_im.reshape(bins, tiles, UNIT, segs)
    re = pltpu.with_memory_space_constraint(re, pltpu.HBM)
    im = pltpu.with_memory_space_constraint(im, pltpu.HBM)
    held = gathered(re, im)
    cross = pl.pallas_call(
        cross_kernel,
        in_specs=[pl.BlockSpec(memory_space=pl.ANY), pl.BlockSpec(memory_space=pltpu.VMEM)],
        out_specs=pl.BlockSpec(memory_space=pltpu.HBM),
        out_shape=jax.ShapeDtypeStruct((bins, SLOTS, rows, 256), jnp.float32),
        scratch_shapes=[
            pltpu.SMEM((1, SLOTS), jnp.int32),
            pltpu.VMEM((SLOTS, bins, rows, 256), jnp.float32),
            pltpu.VMEM((rows, rows), jnp.float32),
            pltpu.SemaphoreType.DMA,
            pltpu.SemaphoreType.DMA,
        ],
        compiler_params=pltpu.CompilerParams(vmem_limit_bytes=30 << 20),
        name="cross_products",
    )(offsets, held)
    return cross[:, None]


def solution(mesh):
    placed = (P("fr", ("sr", "sc"), None), P("fr", ("sr", "sc"), None), P(("sr", "sc"), None))
    return jax.shard_map(
        local,
        mesh=mesh,
        in_specs=placed,
        out_specs=P("fr", ("sr", "sc"), None, None, None),
        check_vma=False,
    )
```

time: 81.5 us -> 80.1 us (0.983); the launches traced: 79.9 us -> 79.9 us
  no operation moved by 1% of the time
where the time goes in v4:
time: 80.1 us; the launch traced here: 79.9 us
  Pallas kernels  79.9 us (100%)
    pallas_call x1, Pallas kernels, gathered(): pl.pallas_call(gather_kernel, out_shape=jax.ShapeDtypeStruct((SLOTS * UNI...  73 us
    pallas_call x1, Pallas kernels, local(): pl.pallas_call(cross_kernel, in_specs=[pl.BlockSpec(memory_space=pl.ANY),...  6.85 us

profile of v4, /device:TPU:30, one launch (start us, length us, event | category | flops | bytes accessed | tf_op | source)
XLA Modules:
  0.0 79.9 jit_solution(2491171024294220005)
XLA Ops:
  0.0 0.0 copy-start
  0.0 73.0 %gather_blocks.1.held = bf16[4257,16,128]{2,1,0:T(8,128)(2,1)S(1)} custom-call(bf16[4,8,16,256]{3,2,1,0:T(8,128)(2,1)} %bitcast.5, bf16[4,8,16,256]{3,2,1,0:T(8,128)(2,1)} %bitcast.6), custom_call_target="tpu_custom_call" | custom-call | tf_op jit(solution)/shard_map/gather_blocks/pallas_call | solution.py:1284
  73.1 0.0 copy-done
  73.1 6.9 %cross_products.1 = f32[4,33,128,256]{3,2,1,0:T(8,128)} custom-call(s32[1,33]{1,0:T(1,128)S(1)} %copy-done, bf16[4257,16,128]{2,1,0:T(8,128)(2,1)S(1)} %gather_blocks.1.held), custom_call_target="tpu_custom_call" | custom-call | tf_op jit(solution)/shard_map/cross_products/pallas_call | solution.py:1352
Async XLA Ops:
  0.0 73.1 %copy-start = (s32[1,33]{1,0:T(1,128)S(1)}, s32[1,33]{1,0:T(1,128)}, u32[]{:S(2)}) copy-start(s32[1,33]{1,0:T(1,128)} %plan.1) | copy-start | bytes 400

commit v5 on v3

v5 whole, which is shorter than its diff:
```python
import functools
import math

import jax
import jax.numpy as jnp
from jax import lax
from jax.experimental import pallas as pl
from jax.experimental.pallas import tpu as pltpu
from jax.sharding import PartitionSpec as P

MESH = pl.DeviceIdType.MESH

PLAN = (
    (
        0x0010000800500000ffffffffffffffffffffffffffffffffffffffffffffffff,
        0x001800400040006800000010005800480058004800280030ffffffffffffffff,
        0x0060ffffffffffff0028ffffffffffff0038ffffffffffff0038ffffffffffff,
        0x002800300000ffff004800380008ffff007000180048ffff005000480040ffff,
        0xffffffffffffffffffffffffffffffffffffffffffffffffffffffffffffffff,
        0x0060005000700038003800300038002000580020003800080030004800000068,
    ),
    (
        0x0050001000580070ffffffffffffffffffffffffffffffffffffffffffffffff,
        0x007000300010001000100040002000680030001000500028ffffffffffffffff,
        0x0068ffffffffffff0020ffffffffffff0010ffffffffffff0068ffffffffffff,
        0x006800200020ffff001000400038ffff005000500030ffff004000400050ffff,
        0xffffffffffffffffffffffffffffffffffffffffffffffffffffffffffffffff,
        0x0030002800480018006000700020002800280008005000480070003000180028,
    ),
    (
        0x0048003800400050ffffffffffffffffffffffffffffffffffffffffffffffff,
        0x004000680008002000500028001000100048006800100000ffffffffffffffff,
        0x0008ffffffffffff0038ffffffffffff0018ffffffffffff0048ffffffffffff,
        0x004800600068ffff005800580048ffff001800700068ffff002800700030ffff,
        0xffffffffffffffffffffffffffffffffffffffffffffffffffffffffffffffff,
        0x0050005800500020003000180050005000380040001800680000002800280030,
    ),
    (
        0x0058006800600060ffffffffffffffffffffffffffffffffffffffffffffffff,
        0x005800180030004800700030005000180068006000400058ffffffffffffffff,
        0x0040ffffffffffff0008ffffffffffff0070ffffffffffff0028ffffffffffff,
        0x002000380028ffff001800000040ffff006000600040ffff000000200060ffff,
        0xffffffffffffffffffffffffffffffffffffffffffffffffffffffffffffffff,
        0x0070003800300058000000500028006000680000004800600008006000480000,
    ),
    (
        0x0020004800380038ffffffffffffffffffffffffffffffffffffffffffffffff,
        0x002800500018004000680058006800380060002800000068ffffffffffffffff,
        0x0010ffffffffffff0018ffffffffffff0028ffffffffffff0060ffffffffffff,
        0x003000480060ffff002800680058ffff000000000070ffff006000680068ffff,
        0xffffffffffffffffffffffffffffffffffffffffffffffffffffffffffffffff,
        0x0038004000000060004800600000005800080028002000100060001800580060,
    ),
    (
        0x0870086008800848084808400848083008680830084808180840061408100878,
        0x0870086008800848084808400848083008680830084808180840085808100878,
        0x08700860088001e3084802440244026c08680214084801bb0840024c022c01bb,
        0x0870086008800848084808400848026c086808300848024c0840085808100878,
        0xffffffffffffffffffffffffffffffffffffffffffffffffffffffffffffffff,
        0x0870086008800848084808400848083008680830084808180840085808100878,
    ),
    (
        0x084008380858082808700880083008380838081808600858061c0858065c060c,
        0x0840083808580828087008800830083808380818086008580880084008280838,
        0x084008380858084808700840084801ab08380830025c024c08800858065c060c,
        0x084008380858082808700880083008300838081808600818088008400828060c,
        0xffffffffffffffffffffffffffffffffffffffffffffffffffffffffffffffff,
        0x0840083808580828087008800830083808380818086008580880084008280838,
    ),
    (
        0x000008680008083008400828086008600848085008280878065c061c0664067c,
        0x0860086808600028084008280860086000100850082808780810083808380840,
        0x08600868086001eb08400234021401a3084808180860019308100214082801eb,
        0x08600868086008300840082808600838084808500828026c081008380838067c,
        0xffffffffffffffffffffffffffffffffffffffffffffffffffffffffffffffff,
        0x0860086808600830084008280860086008480850082808780810083808380840,
    ),
    (
        0x08600018086008680810086008380870087808100858087008800840064c065c,
        0x0880084800200830081000600838007808480810085800200818087008580810,
        0x088008480840018b08100880020c083800400244021402140078026c08380234,
        0x088008480840086800780860083802140078081000580214001800c10858022c,
        0xffffffffffffffffffffffffffffffffffffffffffffffffffffffffffffffff,
        0x0880084808400868081008600838087008780810085808700818087008580810,
    ),
    (
        0x088008480840000808580870081008680818083808300820081806740858066c,
        0x003800000840086808580860081008700878007000f108700870082808680870,
        0x08480850081001c30070026c023402240878022c0828019b0818061c066c025c,
        0x0848085008100870081000200060024c08780838085808700818087000100234,
        0xffffffffffffffffffffffffffffffffffffffffffffffffffffffffffffffff,
        0x0848085008100870085808700810086808180838083008200870082808680870,
    ),
    (
        0x0848085008100870105810501058104010781040105810280654087006440840,
        0x0848085008100870021c08700008086808180838083008201050106810201088,
        0x07df10701090105808580870021c018b08180850026c021c087006140204065c,
        0x007808f1001810580858087008100244081800380830023c0870082808680204,
        0xffff08f108e109010a7408c90a840a4c0a4c08e90a4c0a340e7c0a340a4c0891,
        0x000000000038018b001000780018003000500050000800380020003806440010,
    ),
    (
        0x06c5063c0644062c10801090104010481048041008b108c910500e6c10201088,
        0x06c507ff08e10901005800d90a8408c90a4c07c708b108c91090105010381048,
        0x07b71048106810380a740a641058104000501040105810280a6c0a3410200a1c,
        0x000808c1001010380a7408c908c110400a4c08e908b10a340a6c08c108d90a1c,
        0xffffffff08b908d90a4408f108c109f30a7408b908b109eb0e4c0e6c0e8c0a1c,
        0x0018007000e100e9004000080040007000780030006000180010005000100018,
    ),
    (
        0x066c07d707c70634105010381070107004181028107010681090106810381048,
        0x007807d7006808d90a440a3c0a5c0a2c01930a840a3408e11020104810481050,
        0x00781078107010400a440a3c10400a2c0a740a840a3410680e7c0a1c10381048,
        0x0058007808e910400a440a3c09010a2c0a740a440a3410680a3c090108c11048,
        0xffff08e108e909c30a640a3c09010a2c0a440a84089908e10a3c08c108c10a5c,
        0x002000600068000800080000007800080254001800780050005800d100080040,
    ),
    (
        0x06a5062408e908e1102010701048108010581060103810881020104810481050,
        0x07e707df0078007807bf0a6c08a908e10a4408c90a640a641028108010681020,
        0x00181058105010780a6410381070107007970a2c10380a640a3c105010480a7c,
        0x000008e1000810780a6408c108a910700a4408c908d1108802340a540a2c0a7c,
        0xffff0901ffff08e1ffff08c108a909c3ffff0a2c08d108a90a4c0a1c08b908a9,
        0x0028007800580010022c00480060000000480058026c00b1024c000800780078,
    ),
    (
        0x06e5065c08c90030067410801020107810881020106810801028108010681020,
        0x06e507bf002808c106b50a4c07b708b90a1407df0099007006f5103810781080,
        0x07c7065c10200a030a841070104810800a1410200a3c108000580a1410681020,
        0x00400070007802040a8400f908e11080002000780891108000200a1408b90a5c,
        0xffff08c908d108c1ffff0a4c08e108e10a5c08c90a3c0a3c0e8c0a140a5c08b9,
        0x00400020007800a900680099012a004000200081021400f101eb005800a10070,
    ),
    (
        0x06ad08c9060c00280e740e3c062c061c10281048104010301080103810781080,
        0x06ed08c908d1003000e900380081000806ed08f9006800e91080089108f1099b,
        0x07cf0a5c0a14108000501080102010780a5c10480a1410300a7c103810781050,
        0x0e5408c900a10e3c00c90028007010780a5c00f908b90a74004800000a5c1050,
        0xffffffffffff09cbffff0a6c0a5c0993ffff08f90a140a740a1c090108f10993,
        0x00580810004001930058003800700038004000990000027c0193007000c10058,
    ),
    (
        0x081008100018099b106808880e540e240860086008180458083008480e540e3c,
        0x081008100848099b07ef0888082808400860086008180848083008480a2c0820,
        0x0810100f0fd7099b0820019b02240a740860025c019b0a6c083010480e540a24,
        0x081008100848108008200888082808400040086008180a64083008480e541080,
        0xffffffff0fb7096209e308910a140a6c08b1089908b90a6c0e54089908a908e9,
        0x08100018084800a1082008880828084008600860081808480830084802140820,
    ),
    (
        0x0828088008f100400e440fd70fbf0880045008400fa70848059b05eb0e4c0e7c,
        0x0828088008f108f9085008180850088008880840087008280820086008200828,
        0x08280a440a2c0a3c085001930122022c0888084010400e8408200a3c08200204,
        0x0828088008f10a3c085008180850088008880840087010300820086008200828,
        0xffffffff094209e308c90a0308f108b90c480a640fa708b108990f9f0e1c0a03,
        0x0828088000c90091085008180850088008880840087008280820086008200828,
    ),
    (
        0x083008700028081808500e240e6c0e640e4c0e640e1c0e440ec508e105db0614,
        0x0830004800c9081808180810088808180a64007808880860086808e108180850,
        0x0a440a3c0e3c0a44027c0810085008180a6401db020c10880868065408180224,
        0x08300a5c0e3c0a440818021c088808180a6400580888027c086808e108180850,
        0xffffffff0fbf0a0308a909db0a6409420ee50c400fe709fb0ec50e740e4c0a24,
        0x0830087008780818081808100888081800700828088808600868000008180850,
    ),
    (
        0x08380888086808200fb70e5c0e3408100f05041808700478048902b508880820,
        0x00680888086808200078085808700810000008280a7c08c10a5c0fc708880888,
        0x08380a740a5c0a1401b3085808700810085801eb0a7c0e4c0a5c081802440993,
        0x0e1c088808680a1400c108580870027c085808680a7c082800a9081808880888,
        0xffffffff0ff7096a0eed09e309ab09db0f050e440e34095208f90e5c0ad508d9,
        0x0838088808680820007808580870081008580868002800400078081808880888,
    ),
    (
        0x08500830088800480efd08580e640e7c08300891088808c10fcf0868066c0880,
        0x08500830006008b900c908a9093a085008300891020c090109fb086808b10880,
        0x08300f9f0ff70a7408180fc7027c027c083004100a24090109fb086801b31080,
        0x08380a2c08880a74087808100e641048083000e10a24090109fb086808b11020,
        0x0cb909930962093a08e90fef0fff089108b909bb0e440a6408d90c680a2c0a74,
        0x0850083008880030087800280030085008300068020c026c0040086800200880,
    ),
    (
        0x086800f9085008b908780e440880084008500e34081008600868086008d10828,
        0x086800e908880a7c087808480048004000e908a908100a8c0fb7088008d10868,
        0x086810200a6c09a30a3c01c3093a08800850086801930a8c09a301ab016a01fb,
        0x086808300a6c081808680848093a022c0850004800b90a8c0078088000810868,
        0x09db0ed50982095208f10acd0ff709820e7c0af50e740e1c099b0aed0a34099b,
        0x086800e908500048086808480880084808500048081000700018088000380868,
    ),
    (
        0x0078003000b108b1103010981038105008581070102808990ecd10580a241030,
        0x0a84082808910089082008a108800848085008680a240078104010580a1c1030,
        0x0850023c105809930e2408180888023401db0a8c0a2c09e3001802640a1c0a4c,
        0x0850082808500e74007008a900a1084800c908a90a2c105809a30e1c0a240634,
        0x0c700c38089109930a140af5090908a908e10a8c0a2c08990ecd0fe708c90a4c,
        0x00480828002000400070002000a101f300300038011200280264007800500008,
    ),
    (
        0x006808280901067c0e54102810600818107003e70faf08281030107008180888,
        0x09c3002008d909a3002000f900700afd00700a1c00e100401030107010301038,
        0x0a1c1090091a0a7c08780a840af510900193011a0a541038026410700a740274,
        0x0a1c0e7c08d908b100e9001000e910500a540a1c0a5410380a8c007800700a2c,
        0x0c4008a90c5008c90efd0a840af50afd0a540a1c0e030a840efd0e8c0efd0a2c,
        0x000800680010007801eb005800e900c901c30060004000780048002000600038,
    ),
    (
        0x000800c9001009a30e2408a91098102808801038109810700e3c081010300850,
        0x026400c9091a08b106bd0020003001a301db0a140a8c021c06cd081010281060,
        0x09bb09ab10881028086808a910980a1c08801050108010700234081001a31030,
        0x0a7408b1089109a30a3c026c00c10909088008910a8c0a1c021408100a8c025c,
        0x09c309ab09c309720a340f9f089909090a1c0ae50a5409090c6808e90a8c09b3,
        0x006800c900080050002000680058027c088000100058002001cb081001a301ab,
    ),
    (
        0x09f30684091a060c106010200e3c102010980868083804080797081810981098,
        0x025c00780909021c07d70068078f00c900910a5c08e9024c1078102810980a64,
        0x0e6410981078103008880a8c0a6c0a2403971078046010580797102801db1098,
        0x0a1400680909103000f9021408d910200285022c08380a140038001000200e2c,
        0x0db309bb09bb08e90ef5089908d909a309f308d90a740a140a8c0a6408990ac5,
        0x00780010001800700888023400c10010009101db08380850088801c300680020,
    ),
    (
        0x05db08b9016a084010280838108010600a6408a903d70afd07e7107808300932,
        0x03ef09bb00a10274026c08f9084001f307bf00e10a740a540850107808301090,
        0x0a74108010980274078f083808401060003010380a1c0a540397027c08301090,
        0x08f100080a5c08b9088808380880106000b9082800f90a7c088800c908300ac5,
        0x08f10c580aad09bb0f4608f90fbf0a1c0dcb0aad08c109b30a340a2c09620b7e,
        0x00e9003000280840011a0838084002340010087800b900d90850001000300050,
    ),
    (
        0x06ed08f908d9085810781068093a10900909085810200a8c09a3109008481078,
        0x08f1027402a5025c00c1018b01ab0abd01c30038024c08800828109008481078,
        0x0a14104002c50c60064c08480880105001c30aad024c088008280274084801ab,
        0x089108f902c50214027c068d00b9105809090a4c0810088008280aad08480c90,
        0x09ab09eb099309eb09bb0c600a6c0abd0e1c0a5c0a0b0aa50a6408a10a740a64,
        0x045002d502c5085800c100100122004800c900700880088008280274084800e9,
    ),
    (
        0x067408d10878085008800e6c109010580285107808800838085008880e5c0818,
        0x021400d908500858011a083008b1012208800858019b00d906e5088808601098,
        0x0e2c0c401060027c01eb109801ab0a03038f09a301120478088801c30a240818,
        0x0a3400f908a90a24088008e908b106bd02ed0858082006240a740888086002ed,
        0x0f9f0c40092208d10c4808d1092a09d30a0b0a140b3e0afd0e440a9509cb0ebd,
        0x08580048083000280880083002640068077e0078082008380081088800400048,
    ),
    (
        0x01bb08e908a900680e6c1058084008d908400848085008500858102808701060,
        0x01bb0878027c08a109fb086808f9027c09d3087000f9088808580a240a240848,
        0x0a240a640a240a2409fb08680e24062402ed084809220888085809f308700244,
        0x0a240a4c0e34088806bd0868026408d900e90e6c00f1085008580b0d00e90244,
        0x0f1e0c200e5c0c780a030fbf0ad50bbf0ead09ab0a9d0d010fef099b08e90b05,
        0x08180878082000680112086801eb016a08400848024c08880068006808600818,
    ),
    (
        0x085806a50818086008300e3408680e2c0ed50fff092a0aa504f9088008600848,
        0x00c108a9081800990830083801fb08f1022409a3086808380c681020087009bb,
        0x085810070a1c0e240830020c0868027409d30828086808380a54012201830848,
        0x082008a90a2402740ecd02cd0030027408c108b10234107002ed012a0870027c,
        0x0c2010070e34095a0fef0c30099b09eb08c10fff0fef08f108a90c200c800b26,
        0x0820000802a50860083001420868024401930870006800e9003800a900700848,
    ),
    (
        0x08880820082808a110980878063409bb0fcf082010480e940888083010280830,
        0x0a2402d50828090901b30878020c09bb08a1090101930850109809d310170818,
        0x0a840e1c0e5c0a540a140e6c0e64020408a1026c083808c102140e3c109809bb,
        0x0a6c001008180a5400910a4408400a24084008700a1c106008500a2400910830,
        0x092a0dd308a9098a0a0b0e340a4c0ab509db0ad50a8c0be70c180aad0faf0899,
        0x088800f908180000067c087801ab00180099085808680030012a027c08700830,
    ),
    (
        0x07360634067c06140e9d0868105006bd08f90870092208300942082008400860,
        0x073609db0a8c0a840868017a01b30a44016a09eb09220a4c0a74082008400860,
        0x0e5c0274027c1050062c0a2c060c0a440060099b09d30a7c0850088808780830,
        0x024408200a8c1050046008a10091047809d30afd0a4408300942082008400860,
        0x0e240fd70c600add0edd0a740dab095a0ed50fbf09120b0d09420b0d0c780aa5,
        0x024406a5083808800828014a02950820027c03e7062c08300593082008780860,
    ),
    (
        0x069508b107af034607c7063c0e9409eb08d910880868109008281020087809ab,
        0x069502440ad50a2c08800a4408d1085806fd014a01cb013a0a540a95087808f9,
        0x0a3402d5023c0a6c092a0fef0e94046007e70e8c0644109001fb0a8401f31038,
        0x0e740204023c021c08600e6c060c10900274006806cd109006a50a8400f90274,
        0x0fbf0e240e7c0b3e09eb0bbf0b1e09120899098a09eb08910e5c0c480b2e08c9,
        0x021c0840023c0850064c07ff00910858006006dd0850017a00d9015a013a01eb,
    ),
    (
        0x0091078f0830088806c51040070e06340eb5099b062c0614089107af08500858,
        0x00910ae50089095a06fd090104a90a8c084002fd005802cd0891083008500858,
        0x09f31017025408380e6c10400a74063405e30870085006140a7409a308500860,
        0x00c10a6402540e540e6c014a0e1c06340eb50888020c06140a640a5c08500858,
        0x0e2c0c680faf0912101709eb09a309fb08910e340fb708a10cf109a30e9d09a3,
        0x072e0858025408380081082004a90089038f088803d7000008580132085000f1,
    ),
    (
        0x064c09a3091208800edd10780a74099b077e0880080710981060087809091028,
        0x09e302040254023c0a0308b9017a0a5c0922011a080708b90878087807970830,
        0x0c60027c0c38023c063c10480e6c0a5c07c706841090109809c30878026c027c,
        0x04500ae50c380878063c09090a74025406cd016a00c910980705087809010848,
        0x0cf90ab50c6809b30e9d0b050fef0a0b08f109930e2c09db0c4809f30c18091a,
        0x00d908200224023c07c70644067c064c02c5011a066c021c087808780840025c,
    ),
    (
        0x0654099b093208780cd107e70e1c0820059309a3093208e9084807ef08801058,
        0x00d9099b021403460756019309fb0aa5015a07e708780af5084808b9088008b1,
        0x024c099b0820107007b70a3410780e6c041807e708780e740848082008800858,
        0x0e240a6c0a1c023c0cd1047808680e6c0eed0e8c0a5c08f908780c8809b30818,
        0x09f30a1c093209db0cd10da30c180fa70eed0c5009320aad09720c880c900c90,
        0x08780818082803af00f1019301d3025402ed07e708780172084800b908800858,
    ),
    (
        0x062c0674017a098a067c1088064c0828082008880878062c06ad0edd093a1040,
        0x0a3403c70a0b08100a0b012a09320b0d08f9099b0afd08400bd707ef10800a0b,
        0x0e240ae50da30a2c0e9404d90e440478079f10801098084001e30a6c08401040,
        0x0a8c0a140efd03af0edd06640e940b0d068408800850064408f108d909621040,
        0x0fff0ddb09d3092a0deb0aad0ac50b9f09220add0fff0cc10c800a6c0aed0c58,
        0x024c03c7073607b701b3068d070e06bd068408800162040800b1010201b30112,
    ),
    (
        0x00f108a9063c012206fd0e1c0e2409120fb71068063c104006dd07f7108808e1,
        0x07050214097a025407e7082008e9019b06ad00c10acd03260aa5103009b31070,
        0x09e309a3063c025407c708200a1c1030064c0fb70e3c106007c707f709b31070,
        0x0e2c0214023402540e8c02dd072608f906ad061c063c0e840c6800990b2e1070,
        0x0a8c10170bdf0e540e940bdf09f308f9091a09520b7e0e7c0dbb0e3c09420c88,
        0x070502c5023406d50860017a00080878079f082003ff065c039707af016a016a,
    ),
    (
        0x061407f70112099306f506440fcf085806540664103008400878096a0eb508a1,
        0x021c08d90a4c0bf70091095208a103ff07c709ab00b10a030993096a07af1040,
        0x0c6801db08180e5405f3100f067c0c3007bf0e7406cd0a5c0891023c10700850,
        0x0c200aed0e8c089906d50e84070e0c900edd0e7c08d90e2c06b5096a0c881058,
        0x0f8608a1092a0aed0dcb0e130da30c400e2c09d30c600e4409c30c4009fb0c50,
        0x065c01bb00890810075607ef034e082808200306063c0840016a083001ab033e,
    ),
    (
        0x092a0858014208d1092a058b05a308f908701098066c065406d50ef5106009fb,
        0x0a2c09090244032e09ab00a102cd0b970274017a01db03f706d507cf094a0901,
        0x0a2c0c30026c03af0e8409eb01b30e8c0e0b0fd7064c06540a3407cf0a5c1028,
        0x06ad027c0244020c0c880acd0e440234049108c106740ae506d50edd09090901,
        0x0ecd0fdf0da30bc70f6e0de309820e8c09010aa50ad5099b0cb909cb0e940c20,
        0x046804890244024c00a902ed071e0888068d00e10593065406d507cf02fd0634,
    ),
    (
        0x070e087808700142057a06540e8c08a108a90684067408880e9d1088100f08f1,
        0x0a5409eb09d30ba704b101420cb909eb00b1074e0a9d051a08e908d910880a8c,
        0x0a5401fb0a3404b90deb066c0cb90c880e7c0674065c0810018b10881050067c,
        0x026c026c0acd10900ec5066c00f90e94068d0ad50e3c041004f90410060c08e1,
        0x0c500aa509a30cb90af50deb0eed09620f150abd0fd70a440d420cb10add0932,
        0x01fb01d301bb02d5079706bd04580634039702fd0840005800f905eb01830420,
    ),
    (
        0x072e079f092a09bb0d01095a0e440e5c05e30e440dcb0e4c108808c90ed50909,
        0x0a6c0285027403af02dd07ff02240aad07a702240b7e0aad093a07ff0a7c0aa5,
        0x0d9b01bb0fef0bb701f30da303df07cf0dcb05c301db0b970bd7067c0c8809b3,
        0x04480e3c0e7c10480d010e5c0a6c06e50e5c0e54067c0e740aa50b0504080cf9,
        0x0cd90a9d0e940eb50fbf0b9f09420c900c070afd0ac5093a0ca109eb0c500c18,
        0x026c02ad0418034602dd061c0726054a064403df067c074e079f01eb06bd03b7,
    ),
    (
        0x04e904d1064c08c107360e13067c0b7e0ead0fb707bf0982103808d90fb70b7e,
        0x022c0a1402e50b9f07360a14027c08e901cb0aa5022c029507f707bf0912091a,
        0x0a8c0e640bdf0fe7046002040624105809f30e1c07bf01cb078f0fc710800bdf,
        0x0a5c0ef50e4c0bbf0eed0e1c08f10e9d08e102dd0e4408400ebd0abd06bd0aad,
        0x09e30e5409ab0f7e09b30eed0a9510170cc10c6809930b970c780ba70c280acd,
        0x03ef01e30448045807d7067c064c07af04a9038f07bf0193036e07ff0244060c,
    ),
    (
        0x07cf0912066401db0ec5080707b7093a0fff06740e340952079f0ff70e34093a,
        0x08910af509f309eb08e90a0309db025c01eb036e0aed022c0eed08c9097a0a6c,
        0x0e541088079f046803bf0fbf0204025c0a0b0c500684060c0da3099b05db0e5c,
        0x0a840a840089106008e90e240aa510300e24027c0e940ac506dd0c180c380e64,
        0x0acd0dbb09f30c070ce90ae50c0f0c800bff09b30eed0ca909eb0de30d010baf,
        0x02850634050a087804b10797004807a704c105c307360766077607c7058b052a,
    ),
    (
        0x08180060017209db0f6e0820098a0e3c069d07ef0909092208e90ec50efd0942,
        0x00e902a50b6e02cd0099027c01a30982076602c50ad5039f09db0abd099b1028,
        0x0e4c05c30e1c06540c38065405a307970e9401830c58061c01cb0a8c0e3c0264,
        0x0e4c0c400e5407b708c90f0d0a4c0ee50f0d0766045806bd0c3802c502240eed,
        0x1017099b09fb0deb09ab0f5e0b0d0ba70a0309420aad0c3008f10e030f1e0bd7,
        0x0470035e017a0654014204e1072e03ff0776076606cd07a7080706d507860397,
    ),
    (
        0x072607bf097a079707e7060308180e9d0644098a09fb09cb05d30f9f094a095a,
        0x01e30d2201520aa508b9089907ff0962010a013a01eb0ad50972097208990bf7,
        0x0387038710480ee5066c0bdf0faf0e5c0c07109006640cc10a4c0fbf09a30e7c,
        0x04e90e540a4410700f6604500e2c0b5e00890e4404d1069d0ed50ce900e10e6c,
        0x09220ef5094a0faf093a0d520faf100709620cd90acd0ad50cf90ebd0dbb09e3,
        0x062c0244033e01eb06950132066c01420870016a05d3047806fd0183045005fb,
    ),
    (
        0x07e7079709d3019b0e940909072e0f6e039709ab096a0912077e0ed50e1c0a03,
        0x03870a2409320b97089907bf0ad503af009902e50b56025c0a03091209c30ae5,
        0x026c0fd701a30888045803af1038042807a707df10500fff027c0a6406440e24,
        0x0e6c0c300c8802b502c506240e6c0e6406f5043000d102fd0ca1025406641060,
        0x091a0e1c0acd0ba7098a0d090e0b092a0e0b0f6e0dcb0d110e340eb50eb509c3,
        0x072605bb01a30624038f07bf08180428000005eb00e9039f04b1031e03df0366,
    ),
    (
        0x07760091016208d9061c100f0fdf0ee507c70e840eed0f4e0fb70d9b09420fff,
        0x027c02ed029d094a0d220b05030e0af5096208c10aa5012a09cb09f30c800a14,
        0x0a7c0c200a0b0e1c0dcb06030e2c09f30e5c0bf7103007cf035e05eb10170478,
        0x04f90440020404a904200e440cb90c3006b50e340e5c0d010c180c9000991098,
        0x0e740e9d0ebd0b660f8e0bef0c500c07095a0cf10bff09420ca90c900c880d09,
        0x0089044002fd02f502f5048001f3037604a10684078f086804f9023c071e072e,
    ),
    (
        0x05c3008100a901b30cb10e94089909420f56074e105008f90b76078f0faf0366,
        0x092a028d09cb03cf01830ac501cb0b0500a10abd0a0b09e30da309420a6c0c07,
        0x0e940c3804700a5c0a5401b301a30e3c04380c180e0b02240c8007af0468018b,
        0x0cf90a1c0a140c580e9d046008e906c506950e1c0e340c900ee504a10a6c02f5,
        0x0f8e0b0d09120fdf0d010d820f050da30baf0acd0cd108b90c500afd099b0c38,
        0x0376041803a704b907e70489074e0450001807f7028506fd077e073607d70489,
    ),
    (
        0x0a6408a100d107360cc10ecd098209090ff70512094a096a06140ebd07760e44,
        0x01cb09b301d3097209c30cf90aa50a4c025c03460942099b08d90fdf0ddb0bc7,
        0x0de303c70f6610200e7410880c90053203b70e6404280ca90468065c0fa7066c,
        0x0a2c0c380a74065c06f509520f2e0fb704d90eed0ebd0c48020c0afd0d01063c,
        0x08c10bb70fff0baf096a0f460ea50dab0cc909620df309120c600ed50dd30909,
        0x07cf04c902950736077601a306e507bf073e05db042806dd03ef075e0430068d,
    ),
    (
        0x063400d100e900c9049906840f8e09b30cd108d907e7073e0f8607970f96094a,
        0x032e0b0d09930a9d0d6209e3010a09c309f3094202c501ab0a0b0cb90b8e08f1,
        0x0acd048909ab0bc70e8c0e5c0a4c05420d9b109805f301ab04380c2004400f26,
        0x0a4404d10a3c04800e44047006ed0e240ca90edd0e1c0a6c06f50c680e7c023c,
        0x0cc10b5e0dcb097a0bc70dc30bd70dfb09ab0f360b560ec5092a0a540b5e0fe7,
        0x032e04d102ed04600562066c0068077e0450015a069d04d9074e061405db07e7,
    ),
    (
        0x061c09010962079f0ce905a3094a10980f0d0e7c078f0f76091a05f30fff09b3,
        0x0008072e0a4402bd07af02e50d720a240e0b023c021c0b8609010aed0d820982,
        0x0e6c03ff05d3069d03e710900bf710170e540c070bdf0a740ba70fd7064c0410,
        0x06f504180aed08c104d904a90c300a5c0e84001004500acd0ca90ca9029d0214,
        0x0d6a09db0b6e0fe70d220e840abd08b10bcf0c0709620d8a0b7609220d6a0cf9,
        0x023c01b3027403cf062c078604f9071e051a013a070506f5002807f703970450,
    ),
    (
        0x071600890942070e09ab0fa710780fbf06ed072e0da3091a0cd10d220f3e0fe7,
        0x08b90abd0142096a0b5e025c02a5093a0a8c02dd08990abd078f10880b050b0d,
        0x05e3082001ab01ab0b9f0deb0f3e1007061c05e30f460a4c0e5c10170480021c,
        0x05cb0e4c0664062402440abd0ad50d5a0e2c0a9d04480ad500990c480ca10932,
        0x0de309120cb10bf709db0c400e9d0c4809c30cd10f7e0b660af50e940c580e34,
        0x071605e303b7030e06f507cf06ad074e075e073e02ad06ed03cf033e039f05a3,
    ),
    (
        0x030603ff07a7016205eb08f10f2e09f30fc70fcf059b07ff04a90f1e071e06e5,
        0x036608a109eb0c0709e309420b0d0d9b08d9095201830387079f0af50b26071e,
        0x03660d9b06741048026c0fcf022c07ef0bff0204018304200c3805c306840868,
        0x0c780e9d044808e9053a04890e340ecd04700ea50afd05010cf10e840ecd0448,
        0x0bbf0f6e0ddb0ecd0f3e0c380bf70ead093a0a9d0a030b760d320f1e0b3e0bcf,
        0x041801f30306069d057a079f047806e50418073607460512075e057202b5071e,
    ),
    (
        0x0922056a0152015a05420f2e0faf0fb7100f065c0f9f08b1074e0fcf07cf0f3e,
        0x08e107f70b360aed04580ae509a30be701e3037e029d0b76091a092209cb0baf,
        0x0c7009b30f4605fb0a2c023c04180b970387065c023c0fb702b50dcb021c051a,
        0x0f150e34050a0c200e840c8004800acd017a0e640e6406ed00f90a950d110ead,
        0x0ad50ca10fcf094a0b0d0f2e0baf0b4e09720faf0db30edd091a0cc10d820c68,
        0x04f10450047002c50786004004e105d303cf010a01a3069d0204072605fb04e1,
    ),
    (
        0x0a3c00e107b701a30fa705d30f0507660e0b0e5407d70ec506fd0f960fbf07e7,
        0x03260ca102850bff01c30264035e01eb095a0b0507df00c909eb0f560d6a0add,
        0x03cf10500f9f05db07970bb7060308070b97058b0fe71017045002540c6005fb,
        0x0e5c0e8c0a2c102000b9063c0e5c02a504c10d090a9d08d906ed042804910d3a,
        0x100f0d9b0f760bd70d620dab0dbb0b760c0f0d8a0e9d0ab50be70dbb0cf10cb9,
        0x067c0366067404080450016a018307c706ad0705073e075607c7017203460162,
    ),
    (
        0x091a0a5400f9093a1017057209420f8e0b760572036e0f1e0d1a0e640f1e0fc7,
        0x07160add0b4601bb023c01b301db09cb01fb015a03ff00810f8609eb09fb0a84,
        0x03ff0fe70fff062404400fb709f30f4e0baf023c0d92063409b30c9005eb0e74,
        0x04d90eb50c5008d9093a00b906ad020c0f1503460e74089100e902dd062406e5,
        0x09bb0ecd0d9b10170b5e0abd0b4e0d9b08e90cc109bb0d9b0d820dcb0ab50952,
        0x03f7075605b307af079f077605e3019b07cf06d503f70603069d07760522011a,
    ),
    (
        0x07b708070786011a032e07860e7c097a06cd07160f5e061c0ce910500ea5068d,
        0x0b9f08990b660cb9032e0cf10b5e0c07094a032e09f301420b260f6e09bb0b76,
        0x0aad0c28052a0deb09b30418100f059b059302540de30f4e0204043003f70254,
        0x0aad0e6c0e5c0e9406840ec50ec50d3a09010cf10f760ce90cc100d90a540891,
        0x0abd09720b660b6e10070f0d0f8e0ca10b860bd70cd90dfb0b660ca90b860d42,
        0x0797057a0582050a05d3035e0705063c0664071607b707f703df012a03f702ed,
    ),
    (
        0x032607cf077e063c0df3095207460f5e0cb908d105d30efd0ddb0d2a0982074e,
        0x019b09d30122015201320aad0bd70d220942075e0aad01020b760baf09820a54,
        0x0bff0da3103004580e440fa7018b0da3060310170fff05bb04600fcf09cb0e4c,
        0x08c10b050aa5063c04e90e540c480add04a902e504100efd0450009104400d1a,
        0x0edd0d220dd30c990d6a0cc10bcf0ec509420cc90b160cb10c400da30b460ae5,
        0x0634064c04c106f5026c04f10346056a062c072e04b107ff07af028d011a031e,
    ),
    (
        0x07ef072e0746073e0f8606dd0f860ef505f30d8a0ec50fd705420786077e08a9,
        0x09bb00a100d903560e34094a00c9013a01f30b4601220152096a0dfb0c0f0f4e,
        0x0d6a08400dd30b3e0d8a09e303f701d301f3102804400c5004400e8c05ab07e7,
        0x064c04580901106806ad06540408041000a102bd044007360c200acd00d904f9,
        0x0baf0fc70ed50d6a0b2e0cf909220dbb0acd0b1e09e30c380f960c180cc90da3,
        0x06950306087002ed06d5030e087804c10102057203a707360489063c077e030e,
    ),
    (
        0x0532061c08200091079f0fc709fb08b90f8605db0f360ebd075e057a0f360766,
        0x070e09e309bb02d5092201ab01320b6e012a09bb0bff0a9d075e0f660e0b0d2a,
        0x03af0cc906341090079f0c0f0a0310680be705ab0c300dfb0bdf057204300d7a,
        0x0f0d061c0e440ae508a90d1104280c60029d02cd062c0eed0cb1057204a10952,
        0x093209b30f660f660b360bb70f860aa50d620d2a0f260abd0d2a0dab0db30cc1,
        0x05320776077602a500e907560428026c029d0397039f0470035e057a0830032e,
    ),
    (
        0x077e034e0091016a0f960e7c07f70f4e057a0f4e0fd70f660d3a068d0f050fa7,
        0x0a0b02c505520de309520a340bcf056a08e9015209e302fd0f8e0bdf08c10b46,
        0x04f10ddb0c500df3065405a30f2e0d4a05f305930be70e6c0afd0ff707e70448,
        0x0ad50a440c2005a30e740faf0d010edd0cc900890eed0e5c06bd06d5067c0edd,
        0x0d1a0e3c0f1e0fef0a950fe70b160cf10c990a030ba70d090d6a0d720c680e2c,
        0x03660316049904e903bf034603d707ef0470055a04a904e105d3058203ef058b,
    ),
    (
        0x037e075605b300f90f360dab0e0b09520d82092a0b560f050e940b760e84092a,
        0x02dd0b6e05a303760a54073603460bd70387091a0bdf04f1092209820d5a0bd7,
        0x09ab0d22058b0fbf0438059b05fb10380a8c0faf0f4e04f102e50baf038702f5,
        0x02fd0e74029d06a504380c2804a10ead00e10cd90ead0aad01720cb9068d0c20,
        0x0c990ac50d010d090f360f1e0d4a0bd70db30d1109f30d320c900b760e840cb1,
        0x05cb06ad05a3076606a5085006030776059b0102019b035e0172017a038f05eb,
    ),
    (
        0x013a06e5012a013a0d6a0faf0f460ec5056a0d2a0f460d2210480e13095a07af,
        0x013a01bb028d0ad50bd709720d3a04c10952057a015202b508b10d420b3e0d92,
        0x032e0df3043003e70db30e9d0c5005d303ff07b71020057a05fb0e130e740438,
        0x0b3e0cf90c800b6e0e540ce10f150e4c0cc1029504b104d10438028d0cd10cb9,
        0x0aad0f1e0dbb0e940bb70aa50f460d1a0b160b970d3a0deb0dc30d9b0b7e0abd,
        0x013a04a903ef02bd0532036e05a305db054207b706440746070e01ab022c05bb,
    ),
    (
        0x033e00b1013a0962077e0dcb0ef50807068d05420fff07860fff076e097a076e,
        0x0a95019b013203ff077e0a9d050a0baf07cf0183032e03560ebd0f26092a0d8a,
        0x05db0e4c038f07970de30fff039f0e030336046803df0f9f043005820c68024c,
        0x0a9d0cc90cd10cc90ab50e8c0ed50cc9069d0ead0cf904910d320ed50f8608d9,
        0x0d22094a09eb0d5a0ab5096a0d5a0ca9094a0ead0f960bbf0d220a0b0d090d1a,
        0x056a0122077e056a05c30397051a072e049107cf03df049103af03e7017a0346,
    ),
    (
        0x06cd07b705c3095a08280d520f3609ab0e240fbf0f560d320e7c06d50d6a06ad,
        0x091a075e016209db093a0da300e10ca1019b0264036600890bb70aad0b2e0aad,
        0x05a30eb5051a0448024c038f0ff7071e0ad50fbf0e4401c3091a04a102240fe7,
        0x0cf108e90ebd0f7e06c50e2c0254071e039f05820aad0a540c80033e0cb10db3,
        0x0ba7098a0dab0abd09620c0f0ddb0cc10b660b460d620cf909320d4a08e10982,
        0x067407ef03bf0776052a0214035e01d3053204e901930552056a029501c30726,
    ),
    (
        0x09db0142075601f30d820b860fef072e054a10070e6407cf05ab0fb706dd0d1a,
        0x03ff0cf90b0d039f0274034604d101930bff01a302cd09820fbf0d220a95095a,
        0x0b9f0b760bb70d1a03cf0bd703cf1098065c10880e8c05b301db07ef05c30428,
        0x0ae50ca10add0af50cc1029d0e7c0cf10e3c09420f6e06a50edd0c6000c902cd,
        0x0ae50c180add0df30bd709720d320f460f9f0d090f760d6a09930c990a950dab,
        0x0387043803af0582058b020c04d1070e0336032e051a0152054204d1035e0306,
    ),
    (
        0x075604a9076607cf0f660f0d0f5e0d1a050a0ff709420d1a0f960de306bd0387,
        0x0183012a03ef098a0d5a0b6e035603ef00a9051a03970ae508c10afd0d110d22,
        0x0da30fdf0193056a02850fd704380dfb0c80020c02540f260356043804480593,
        0x0c500c600ed50a950f860ecd0df308e90cb10e84034608d10ead0c400f9602d5,
        0x0d5a0cc90d820ed50abd0f050b97091a0ae50b660dfb0b1e0d5a0ca10c480d4a,
        0x018303df0542055203ef070506ed041805f30489035e07760562076602e5074e,
    ),
    (
        0x050a060309fb035610070f5e09720dd30cc90f660e03092a07c706950d8a0489,
        0x0d1a034e0d6a05db01db014a02dd0b4e01020306037e00f90bff0f860de30b2e,
        0x0d22039f0828038f03970faf0dab0b4e06140e540f560d7204800e540d9b0dfb,
        0x0e8c0e840e1c0e640b7e06dd0d0904380ead0e740f260d72052207760ed50501,
        0x0d920bcf0ae50c600b7e0a9d0d220d010b360baf0c300b7e098a0d620de30fa7,
        0x037e0552080703760582019b04e90542017a01fb036603f7030e034e010a06a5,
    ),
    (
        0x04d906c5073e09cb0d620e8c0e1306740ebd0e240d920f0d0fbf0e8c068d04f9,
        0x0ddb0a0309010c180a6c058b033e03bf03b7093a003002ed0b360b0d0bef0932,
        0x0a6c0a540dcb0f4609bb01f303d70e0b0e440fff0bb7041006440684067c0bf7,
        0x0cb90e5c0bc70add03b7013a0b360a340e8c041807360e7c04400a3c02a50c88,
        0x0b66095a0c180dbb0d1a09cb0cc90b260e440b760d32093209120d2a0d3a0d52,
        0x03060387060305cb0193058b075605b3070e0418077e051a059b011a069d0285,
    ),
    (
        0x01e3066408d101d3100f0e740ecd0797067407c7051a09a30e1c0ead04f9072e,
        0x09220bcf092203ef0deb008100d1078f01320716030602140b460a6c0a9d0ba7,
        0x0c2010680f8603c70c0f0d010c0f09930c480bef0f1e0b6603df05bb018b01e3,
        0x0f3e0c200b0d077e0a1400810ef50d9b0ed500f10f150dc303df0ec5055a0d8a,
        0x0b9f091a0b360c200ca108e10d820cc909b309c30f3e096a0bb70bdf0ea50d92,
        0x02f5037607cf058b04e1057a02ed078f06e50542053a06bd06a50428030e0356,
    ),
    (
        0x015a01db01f3069d0b8e06740dfb0eb50efd0dfb0664050102c5097203c7036e,
        0x09eb0a6c0a6c083800b1098a04e10de30112014208f90d110b6e0d4a0c990909,
        0x03ef0fff0d010ead05220ff70d520a8c056209eb0f360c400501060301e304e1,
        0x0ecd0e1c0e740ead0285056a001002ed0b3e03af03b707050532026c021c0254,
        0x0d9b0d720aed0e5c0b8e09fb0fdf0d720abd0c0f0e0b0c400b970bef0c990ec5,
        0x0736039f05f308880522056a022c050104f9060303b7067c07e701f303c7015a,
    ),
    (
        0x04c105f300a104e90ddb0da3051a0fd703e70d9b061404890c40064c038f0d4a,
        0x0e4409420a1c089109bb03cf0dbb095a039f01eb08c9049109d309e3098a0bbf,
        0x0c400fef03af079f031e0fdf0d9b09db01cb1068106804680d22033e03a7033e,
        0x0d7a0e640f860f46089100c90a540b7601620b7602b502a50cd10e3c0264039f,
        0x0b7e0f7e0cc10d010d820d420d920f5609520c180bcf0db30b560d220da30cd9,
        0x02fd037e069d071e002806d503cf06f503e7070e02cd053a014a056a0112070e,
    ),
    (
        0x066408f1097200580e3c0f460f1510300ae506141078066c070506ad09010da3,
        0x089906ad0d7a00c902240b760b7e094a024402a503df0bef0a34076609a309e3,
        0x0e1309d305b30e8c0af501cb0ddb03ff020c0eed0e2c0deb03e701db0c500430,
        0x08e90b260b660d4a0bd70ae50ca90f96051a06dd0c600e9402ad04c900a9031e,
        0x0eed0bc70d7a0f56094a0d4a0d6a0edd100f093a0d920d820b5e09c30cf90ddb,
        0x02b50705078604c90397032e08580410033e05cb04d905ab07cf076e06dd07af,
    ),
    (
        0x04b904c90366014a0e8c07760d7a100f04a10c6006dd04e1037608e90b86061c,
        0x07970cd90bff0b2e025c09b303d70d7a02c50132017a05120de30dbb0fef0ca1,
        0x063c0fcf0faf0fcf0ae5045804e90244007803df10070234027402c501bb05bb,
        0x0edd0ad50bff0e6c02b50a1c0f5e072e06c500d90f4e0e6c0376035600d10480,
        0x0d1109620d720f0d0c580f6e0d720b1e0dfb0b260ca10f6e0d3a0df30ee509d3,
        0x0766055a061406030705033e0766062405db041004d106240376016a014206e5,
    ),
    (
        0x0489064c05ab01c3038f0fef0fff0d4a0cd909720d8a0e5c0f8e08a90b7e0532,
        0x03af0d7a022c0a9502440a8c0993050a0c0f00b9013a01eb09e30d320bf70b26,
        0x0e8c0c680fb70c7002c50a9d074603f70a240d9b0a4c04080603030605a301a3,
        0x0b860add0ca90b1e04400bbf02fd0cc108b100e9009104e903c70e9400b10410,
        0x0f0d0d3a0abd0fd709720c070d52093a0fc70e0b0d110ddb0cb10b1e0912094a,
        0x05db04a1076e075e030606a507460336041003760316058202a50306038705c3,
    ),
    (
        0x07a708c1055a061c0d220deb0efd0d820edd0d620d4a05e30f360fe706a5031e,
        0x096209120cb100c1072e0deb0b97057a037600d1022403ef09c30f460c07097a,
        0x011a10380db30fef0d22067c03060a3407ef085804f90830024c03a701c30582,
        0x0ebd0ce10eb50d620b46039f0e5402240bd704700cc1053200c9018b02b502bd,
        0x08b90b660ce109820fb70f760fe70baf0f560982094208c9092209620b260b86,
        0x031604d9070504990654047806d5076e053a04f102fd04c90756035e029d0460,
    ),
    (
        0x097200a9039f00b102a510300edd0d3a0e940ead0dbb10170634100707c70fd7,
        0x00b902950a7400b103a70b360a640ac5013a09c30dd305b30d6a10070ad50a2c,
        0x0e740faf039f0c180366105003a70d010e2c05f30c480baf030e0244043801f3,
        0x0e7c0b2e0ecd0326036e02ad0bcf0ac50dbb052a0eb5090906ad028503ef04a1,
        0x097a09420c0709420cb10bf70edd0d3a092a0be70c48091a09b30f5609a30eed,
        0x00b90224012a07ef0366052207f702d5051205930532041003b705db01f30776,
    ),
    (
        0x099308e1035e096a0ce10dfb05520fff030e08f106cd035e06f5072603bf04d9,
        0x07cf0d520a9509fb0d7204b903060dbb03bf011207d7036e0f150a030f660e0b,
        0x0c280e740d420fa7057a01830d320a6c063c0f4e051a032601420664032e05d3,
        0x0b5e00c90bbf027c0c380ea503060c2804580f760552074e014a02e5052a068d,
        0x0d820f0d0efd0c480cb909620acd09720d9b0efd0f360e740add0be70cd10bb7,
        0x0326079707d70480016a05fb05d305bb06b5061c075605e304780501027407df,
    ),
    (
        0x01120000073601e307560c9007050b36051a03760f1e05eb0dbb0756067c04e9,
        0x00c9023c043800f1026407ef04b109fb0ca1051200890be70ee5094a07d70993,
        0x0e1c04b9075e0cc901a307ef0a8c0410060c0d620a5c074605db0542055a055a,
        0x06c504b9070e0d9200810542023c0b05042002d509420edd0d8a06a506440f6e,
        0x0f5609a30e640c500c180bd70ae50b160be70b4e0d7a0c500fc70d010d721017,
        0x01bb05d3018b05bb027c072604c10356042003bf048904c100b90705023407a7,
    ),
    (
        0x05820644071607050f0d0d010d820f46055a071e076e09620bff0a0b05220654,
        0x082000b104f901b30dd308b1094a0ba7018b026c03160dcb0d2a08e909930efd,
        0x0e0b0c500d720fd705bb03b709bb0d320e9d0b76077e0a0b0c90022c02b505c3,
        0x0ec50ead0edd108805620f26066c089906340b1e074610280397054a0a34065c,
        0x0f7e09820f360b260d5a0ef509520ff70b7e0f960faf0f2e0b0509e30cc10d8a,
        0x059b071607f707a7039f055a049104d9081001120776054a0501073e06b504c1,
    ),
    (
        0x07bf00f100f106f50fbf10070f3e0932103009fb0c3808d90e8c073608f10522,
        0x03df0499024c011a07760a7c05cb01cb0c8000a104280e0b0eb50b460cb1098a,
        0x01b30d4a09a30e640b5e04800dbb047002340e9404500bdf0dfb066c04a10828,
        0x0d110a7405720c38062c07860b970f3e0aed0c48057a0c280e24037e0aed0776,
        0x0ead0b56096a0e9d0c070d720d110e740aed0c480ecd0ee50d620ef50e640b9f,
        0x02dd0499030e052a012201c303970460034e0468033604a9021c037e032605d3,
    ),
    (
        0x02ad03a701b306030f8e0d4a0f0d0716091207af0fc705320be708b10d92050a,
        0x053a08b103d702c507b7057a0797048901bb097a052a0b660a8c0d920b5609eb,
        0x054a0d3210380f2601c3071e0da301db06640888074e09d30c4003560c580838,
        0x0d320edd04600ddb02fd04b10491095207160d92023c03af0b3602140e840460,
        0x09820e0b0b050ebd0c200ce10972100f0b260dcb0c280da30ce10b050dcb0be7,
        0x0408057204d90501078f02c5021407160654054a012a045801420387042004b9,
    ),
    (
        0x012a089103e7002006d504a10d9209fb0d0107050b7e07760acd070e0e940746,
        0x039f0d3a08e9014a0891039f09d306030d010b560c40034e0d920b4e0b1e0ce9,
        0x010a0cb107760baf0603079f0e130f05051203c706340ca1060c0f760cf91078,
        0x06fd037e033e0cb10b2e0899065c0dd304e1089902fd0d11092a0b5e07760ae5,
        0x0f5e0af50f9f0de30bbf0b760e2c0b6e0f360b360aed0fff0c200c600ef50edd,
        0x03e7036e01f30522046801830010028d05b301d304f903a701e3077e0410077e,
    ),
    (
        0x02c501fb010a0552065c096a06bd0e8c067c098205b30b8e0e540ee510700ddb,
        0x0b760ad50bc70b6600e104910b4e09320489043005eb099309b30bf70a8c0a34,
        0x03f710300a8c04e9090103df040810480b160df304a90cf10b5e0880074e0810,
        0x0274064c0542071600990bd70d5a0d090b7e0ca1092a06030674064c0cf10e84,
        0x09d3092a0f0d0aa50e1c0d1a0d8a0fc70f7e0fcf0ea50bef0fb710600bf70faf,
        0x015a060303c70099033e031e02a503bf02f5064c025c06c5005004b907660468,
    ),
    (
        0x029506cd080700e107ef074e08b9100710070d6a05bb05ab09220d3204f1064c,
        0x06bd071e08a9040802950552051a01e30b97098208e1098a0a9d099b0d010b4e,
        0x0183030e059b0ba702540c780cc9051a015a0a4c0b16031605b309620d7a0e2c,
        0x04a102b503260cf10899064401e30d6207560776033e097a0ce90c9904c90e4c,
        0x0dcb0da30fa70cd10c380e030fcf0f660de30d4a0b860c0f0c280d090ed50bef,
        0x05c303ef032e0562038705cb078f05e30458042002e501e302c5035603b706fd,
    ),
    (
        0x041801d30132ffff08b9066c0afd108810500ea50b660f4604200b5e08f90e74,
        0x02cd05120a240c5002c504890122089103c709320ab5ffff100709a30ab50f2e,
        0x0888056203a707af0c3007c708380baf09a307af09620922ffff07bf034e032e,
        0x06140d720c680ed50dcb094a06840f2e023408d90a840962030e0532ffff0c40,
        0x10070dab0bef0b4e0cc90ea50ec50d090cf9100f0c180fe70f360baf1017ffff,
        0x0132014200b10705045802dd0366ffff02cd02dd0468ffff061cffffffffffff,
    ),
    (
        0x010affffffffffff03df06c508e908f107cf08b909cbffff0d320f260d09ffff,
        0x038f0a6400f1ffff0b9f04f10bbfffff05bbffffffffffff0c0f0be70aed0972,
        0x030e01cb0736075effff035603970afdffff0fc704d10726ffff0c30ffffffff,
        0x061c055a08990ecd0c4802edffff06840afd0468ffff0ebdffffffffffff0c30,
        0x0af50c880ee5ffff0d09ffffffffffff0b0dffffffffffffffffffffffffffff,
        0x034602bd0460ffff066cffffffffffff018bffffffffffffffffffffffffffff,
    ),
    (
        0xffffffffffffffff0b0509eb0da3ffff0952ffffffffffff0cb9ffffffffffff,
        0x0858ffffffffffff091affffffffffffffffffffffffffff0ce10a2c0f5effff,
        0xffff03b701eb073effff0a4cffffffffffff0a14ffffffffffffffffffffffff,
        0x04780b66ffff0810ffffffffffff0b16ffffffffffff04b1ffffffffffffffff,
        0x09520ee50fefffff0e34ffffffffffff0c18ffffffffffffffffffffffffffff,
        0x049904f1ffffffff0430ffffffffffffffffffffffffffffffffffffffffffff,
    ),
    (
        0xffffffffffffffff08880d42ffffffffffffffffffffffffffffffffffffffff,
        0xffffffffffffffffffffffffffffffffffffffffffffffff08f9ffffffffffff,
        0xffff0dbb0d92ffffffffffffffffffffffffffffffffffffffffffffffffffff,
        0x0c99ffffffff0285ffffffffffffffffffffffffffffffffffffffffffffffff,
        0x0972ffffffffffffffffffffffffffffffffffffffffffffffffffffffffffff,
        0x012affffffffffffffffffffffffffffffffffffffffffffffffffffffffffff,
    ),
    (
        0xffffffffffffffff0c07ffffffffffffffffffffffffffffffffffffffffffff,
        0xffffffffffffffffffffffffffffffffffffffffffffffff095affffffffffff,
        0xffff0a24ffffffffffffffffffffffffffffffffffffffffffffffffffffffff,
        0xffffffffffff0c28ffffffffffffffffffffffffffffffffffffffffffffffff,
        0x0dc3ffffffffffffffffffffffffffffffffffffffffffffffffffffffffffff,
        0x033effffffffffffffffffffffffffffffffffffffffffffffffffffffffffff,
    ),
)
SEMAPHORES = (
    (0, 14, 28, 42, 56, 70),
    (1, 15, 29, 43, 56, 71),
    (2, 16, 30, 44, 56, 72),
    (3, 17, 31, 45, 56, 73),
    (4, 18, 32, 46, 56, 74),
    (5, 19, 33, 47, 56, 75),
    (6, 20, 34, 48, 56, 76),
    (7, 21, 35, 49, 56, 77),
    (8, 22, 36, 50, 56, 78),
    (9, 23, 37, 51, 56, 79),
    (10, 24, 38, 52, 56, 80),
    (11, 25, 39, 53, 57, 81),
    (12, 26, 40, 54, 58, 82),
    (13, 27, 41, 55, 59, 83),
    (0, 14, 28, 42, 60, 84),
    (1, 15, 29, 43, 61, 85),
    (2, 16, 30, 44, 62, 86),
    (3, 17, 31, 45, 63, 87),
    (4, 18, 32, 46, 64, 88),
    (5, 19, 33, 47, 65, 89),
    (6, 20, 34, 48, 66, 90),
    (7, 21, 35, 49, 67, 91),
    (8, 22, 36, 50, 68, 92),
    (9, 23, 37, 51, 69, 93),
    (10, 24, 38, 52, 56, 70),
    (11, 25, 39, 53, 57, 71),
    (12, 26, 40, 54, 58, 72),
    (13, 27, 41, 55, 59, 73),
    (0, 14, 28, 42, 60, 74),
    (1, 15, 29, 43, 61, 75),
    (2, 16, 30, 44, 62, 76),
    (3, 17, 31, 45, 63, 77),
    (4, 18, 32, 46, 64, 78),
    (5, 19, 33, 47, 65, 79),
    (6, 20, 34, 48, 66, 80),
    (7, 21, 35, 49, 67, 81),
    (8, 22, 36, 50, 68, 82),
    (9, 23, 37, 51, 69, 83),
    (10, 24, 38, 52, 56, 84),
    (11, 25, 39, 53, 57, 85),
    (12, 26, 40, 54, 58, 86),
    (13, 27, 41, 55, 59, 87),
    (0, 14, 28, 42, 60, 88),
    (1, 15, 29, 43, 61, 89),
    (2, 16, 30, 44, 62, 90),
    (3, 17, 31, 45, 63, 91),
    (4, 18, 32, 46, 64, 92),
    (5, 19, 33, 47, 65, 93),
    (6, 20, 34, 48, 66, 70),
    (7, 21, 35, 49, 67, 71),
    (8, 22, 36, 50, 68, 72),
    (9, 23, 37, 51, 69, 73),
    (10, 24, 38, 52, 56, 74),
    (11, 25, 39, 53, 57, 75),
    (12, 26, 40, 54, 58, 76),
    (13, 27, 41, 55, 59, 77),
    (0, 14, 28, 42, 60, 78),
    (1, 15, 29, 43, 61, 79),
    (2, 16, 30, 44, 62, 80),
    (3, 17, 31, 45, 63, 81),
    (4, 18, 32, 46, 64, 82),
    (5, 19, 33, 47, 65, 83),
    (6, 20, 34, 48, 66, 84),
    (7, 21, 35, 49, 67, 85),
    (8, 22, 36, 50, 68, 86),
    (9, 23, 37, 51, 69, 87),
    (10, 24, 38, 52, 56, 88),
    (11, 25, 39, 53, 57, 89),
    (12, 26, 40, 54, 58, 90),
    (13, 27, 41, 55, 59, 91),
    (0, 14, 28, 42, 60, 92),
    (1, 15, 29, 43, 61, 93),
    (2, 16, 30, 44, 62, 70),
    (3, 17, 31, 45, 63, 71),
    (4, 18, 32, 46, 64, 72),
    (5, 19, 33, 47, 65, 73),
    (6, 20, 34, 48, 66, 74),
    (7, 21, 35, 49, 67, 75),
    (8, 22, 36, 50, 68, 76),
    (9, 23, 37, 51, 69, 77),
    (10, 24, 38, 52, 56, 78),
    (11, 25, 39, 53, 57, 79),
    (12, 26, 40, 54, 58, 80),
    (13, 27, 41, 55, 59, 81),
    (0, 14, 28, 42, 60, 82),
    (1, 15, 29, 43, 61, 83),
    (2, 16, 30, 44, 62, 84),
    (3, 17, 31, 45, 63, 85),
    (4, 18, 32, 46, 64, 86),
    (5, 19, 33, 47, 65, 87),
    (6, 20, 34, 48, 66, 88),
    (7, 21, 35, 49, 67, 89),
)
NEEDS = (
    (
        0xffffffffffffffffffffffffffffffff,
        0xffffffffffffffffffffffffffffffff,
        0xffffffffffffffffffffffffffffffff,
        0xffffffffffffffffffffffffffffffff,
        0xffffffffffffffffffffffffffffffff,
        0xffffffffffffffffffffffffffffffff,
    ),
    (
        0xffffffffffffffffffffffffffffffff,
        0xffffffffffffffffffffffffffffffff,
        0xffffffffffffffffffffffffffffffff,
        0xffffffffffffffffffffffffffffffff,
        0xffffffffffffffffffffffffffffffff,
        0xffffffffffffffffffffffffffffffff,
    ),
    (
        0xffffffffffffffffffffffffffffffff,
        0xffffffffffffffffffffffffffffffff,
        0xffffffffffffffffffffffffffffffff,
        0xffffffffffffffffffffffffffffffff,
        0xffffffffffffffffffffffffffffffff,
        0xffffffffffffffffffffffffffffffff,
    ),
    (
        0xffffffffffffffffffffffffffffffff,
        0xffffffffffffffffffffffffffffffff,
        0xffffffffffffffffffffffffffffffff,
        0xffffffffffffffffffffffffffffffff,
        0xffffffffffffffffffffffffffffffff,
        0xffffffffffffffffffffffffffffffff,
    ),
    (
        0xffffffffffffffffffffffffffffffff,
        0xffffffffffffffffffffffffffffffff,
        0xffffffffffffffffffffffffffffffff,
        0xffffffffffffffffffffffffffffffff,
        0xffffffffffffffffffffffffffffffff,
        0xffffffffffffffffffffffffffffffff,
    ),
    (
        0xffffffffffffffffffffffffff00ffff,
        0xffffffffffffffffffffffffffffffff,
        0xffffff1cff0e0effff0eff1cff0e0e1c,
        0xffffffffffffff0effffff0effffffff,
        0xffffffffffffffffffffffffffffffff,
        0x46464646464646464646464646464646,
    ),
    (
        0xffffffffffffffffffffffff00ffffff,
        0xffffffffffffffffffffffffffffffff,
        0xffffffffffffff1cffff0effffff00ff,
        0xffffffffffffffffffffffffffffff00,
        0xffffffffffffffffffffffffffffffff,
        0x47474747474747474747474747474747,
    ),
    (
        0xffffffffffffffffffffffff010101ff,
        0xffffffffffffffffffffffffffffffff,
        0xffffff1dff0f0f1dffffff1dff0fff1d,
        0xffffffffffffffffffffff0fffffff01,
        0xffffffffffffffffffffffffffffffff,
        0x48484848484848484848484848484848,
    ),
    (
        0xffffffffffffffffffffffffffff0202,
        0xffffffffffffffffffffffffffffffff,
        0xffffff1effff10ffffff10ffff10ffff,
        0xffffffffffffffffffffff10ffffffff,
        0xffffffffffffffffffffffffffffffff,
        0x49494949494949494949494949494949,
    ),
    (
        0xffffffffffffffffffffffffff03ff03,
        0xffffffffffffffffffffffffffffffff,
        0xffffff1fffff11ffffffffffffff0311,
        0xffffffffffffff11ffffffffffffffff,
        0xffffffffffffffffffffffffffffffff,
        0x4a4a4a4a4a4a4a4a4a4a4a4a4a4a4a4a,
    ),
    (
        0xffffffff4b4b4b4b4b4b4b4bffffffff,
        0xffffffffffffffffffffffff4b4b4b4b,
        0x214b4bffffff12ffffff12ffffff12ff,
        0xff2fff4bffffff12ffffff12ffffffff,
        0xffff2f2f132f1313132f13130513132f,
        0xffffffffffffffffffffffffffff04ff,
    ),
    (
        0xff0505054c4c4c4c4c05ffffff05ffff,
        0x2f21ffffffffff2fff21ff2f4c4c4c4c,
        0x224c4cffff13ffffffffffffffffffff,
        0xff30ff4cffff2fffffff2fff132f2f13,
        0xffff30301430ff221430ff2106ff05ff,
        0xffffffffffffffffffffffffffffffff,
    ),
    (
        0x06ff22064d4d4d4d064c4cffffffffff,
        0xff22ffffffff14ffff14ff304d4d4d4d,
        0xff4d4dffffffffffffffffffff14ffff,
        0xffff314dff143014ffff144c143030ff,
        0xff31ff2215ffffff15ff30ffffffff14,
        0xffffffffffffffffffffffffffffffff,
    ),
    (
        0xff07ff314e4e4e4e4d4dffffffffffff,
        0x2323ffffff15ff31ffff15154e4e4e4e,
        0xff4e4effffffffff23154dffffffffff,
        0xffffff4eff3131ffff31314dff151515,
        0xff32ffffffffff23ffffff3116ff31ff,
        0xffffffffffffffffffffffffffffffff,
    ),
    (
        0xffff32ff084f4f4f4eff4effffffffff,
        0x3224ff32ff16243216ffffffff4f4f4f,
        0x24084f24ffffffffff4e16ffffffffff,
        0xffffff16163232ffffff324eff16ffff,
        0xff3333ffffffffff17ffffff09ff16ff,
        0xffffffffffffffffffffffff24ffffff,
    ),
    (
        0xffff09ff0a0a09094fff4fffffffffff,
        0x33ffffffffffffff3333ffff4fff3325,
        0x2518184fffffffffff4f174f17ffffff,
        0x0affff0a33ffffffffff3317ffffffff,
        0xffffff25ffffffffffffffff18ffffff,
        0xff50ffffffffffffffffffffffffffff,
    ),
    (
        0xffffffffffff0a0affffffffffffffff,
        0xffffff5026ffffffffffffffffffffff,
        0xff2626ffff26ff18ffff2618ffffff18,
        0xffffffffffffffffffffffffffff50ff,
        0xffff272627ff18ff3534ffff0aff3434,
        0x50ff50ff50505050505050505050ff50,
    ),
    (
        0xffffffff0b2727ffffff27ffffffffff,
        0xffffff51ffffffffffffffffffffffff,
        0xff1919ffffffffffffffff0bffffffff,
        0xffff5119ffffffffffffffffffffffff,
        0xffff35ff1919ffff1affffff3527ffff,
        0x5151ff35515151515151515151515151,
    ),
    (
        0xffffffffff0c0c0cff0cff0c36ffffff,
        0xffffffffffffffffffffffffffffffff,
        0xff1affff1affffffffffffffffffffff,
        0xffffff1affffffff52ffffffff52ffff,
        0xffff28ff361affff361a28ffffffffff,
        0x5252525252525252ff52525252ff5252,
    ),
    (
        0xffffffff290d0dff37ffffffff37ffff,
        0xffffffffffffffffffffff535329ffff,
        0xff1b1bffffffffffffffff0dffffffff,
        0x0dffff1bffffff1bffff53ffffffffff,
        0xffff29ff371bffffff0dff3737ff37ff,
        0x53535353ff5353535353ffffff535353,
    ),
    (
        0xffffffff2affff00ffffffffffffffff,
        0xffffff54ff5454ffff54ffffffffffff,
        0xff1cffffff1cffffffffffffffffffff,
        0xff0eff0effff00ffffff545454ff54ff,
        0x2b1dffff0eff1cff0e1cffff2a00ffff,
        0x545454ff54ffff5454ffffffff54ff54,
    ),
    (
        0xffffffffff01ffffff01ffffffffffff,
        0xffffffffffffffffff55ffff1dff55ff,
        0xff55ff55ffffffffffffffff55ffffff,
        0xffffffffffffffffffffff55ffff2bff,
        0x1d2bff1d0f0f1dff01ff01ffffffffff,
        0x55ff55ff5555555555ff55ffff55ff55,
    ),
    (
        0xffffff5656565656ff56562cffffffff,
        0xffff2cffff2cffffffffffff56561056,
        0xff10561effffffff1e10ff1effffff10,
        0xffffffffffffffffffff1056ff0256ff,
        0xffffffff10ff2c2c2cffffffffff2cff,
        0xff56ffffffffffffffffffffffffffff,
    ),
    (
        0xffff2d03ff5757ffff03ffffffffffff,
        0x1fffffffffffff11ffffffff57575757,
        0xff57ffffff111157ffffffffffff11ff,
        0xffff57ffffffffff1111115711ffff11,
        0x032dffffffffffffffff1f11ff0303ff,
        0xffffffffffffffffffffffffffffffff,
    ),
    (
        0xffffffffffffff58ff5858ff04ffffff,
        0xffffffffffffffffff12ffff2eff5858,
        0x20ff5858ffff5812ffffff58ffffffff,
        0xff2effffffffff2effff1212ffff12ff,
        0xffff20ff12ffffff122eff2e122effff,
        0xffffffffffffffff58ffffffff5820ff,
    ),
    (
        0x21ffff05ffffffffffffffffffffffff,
        0xffffffff21ff21ffff132fffff5959ff,
        0xff5959ffff131313ff59ffff21ffff59,
        0xffff2f592f052f5905ffff13ffffff05,
        0x0513ff2fffffffffff2f13ffffff2f13,
        0xffffffff59ffffffffff59595921ffff,
    ),
    (
        0xff30ffffffffffffffffffff22ffff30,
        0x14ffff14ff30ffffffffff14ff5aff5a,
        0xffff5affffffffffffff5affffffffff,
        0x30ffffffffffff5affffff5affff5aff,
        0xffff30ff22ffffff0614ff2214ffff22,
        0xffffff5aff5a5affff5affff5affffff,
    ),
    (
        0xffffffff5bffffffff5b5bffffffffff,
        0xff15ff15ffffffffffff15ffff5bff5b,
        0xffffffff07ffffffffffffffffffffff,
        0xff5bffffffffff5b3115ffffff15ff15,
        0x1523ff23ffffffffffff23ffffffffff,
        0xffff155bffffffffffffff5b5bff5bff,
    ),
    (
        0xff32ff5cff08ffffffffffffffffffff,
        0xffffffffffffff32ffffffffffffffff,
        0x08ffffffffffff5cffffffffffffff5c,
        0x16ff3216ffff5cffffffffff5cff5cff,
        0xffffff32ffff32ff24ffffffffff2408,
        0x5cff5cff5c5cffffffff085cff5cffff,
    ),
    (
        0xffffffff09ffffffffff5dffffffffff,
        0xffffffff5dff5dff5d5dffffffffff5d,
        0xff1717ffffffff09ffffffffff255dff,
        0x17ffff5dffffff5dff09ffff5d33ff17,
        0xffff09ff25ffffffffff331725ffffff,
        0x5d5d5dffff5dff33ffffff5dffffffff,
    ),
    (
        0xff0affffff0affffff26ffffffffffff,
        0x18ff46ffffffffffffff46ffff46ff46,
        0xff26180affffffffffffffffff26ffff,
        0xffffffffff18ffff18ff18ffffffffff,
        0x0affffffffff2626ffff26ffffffffff,
        0x34ffff4646ff46ffffffffffffffffff,
    ),
    (
        0xff47ffff47ff0bffffff470bffffffff,
        0xffff47ffffffffff47ffffff474727ff,
        0xff0bffffffffff0bff19ffffffffffff,
        0x19ffffffff47ffffffffff47ffff35ff,
        0xffffff3527ffffff19ffffffffffffff,
        0x47ffffffffffffffffffffffffffff47,
    ),
    (
        0xff0cffffffff48ff36ffffffffffffff,
        0x36ffff1affffff48ffffffffffffffff,
        0xffffffffffffffffff2828ffffffffff,
        0xffffff48ffffff1aff1a1aff36ff48ff,
        0x0cffff3636ffffffffffffffffff1aff,
        0x1aff48ffffffffffffff0cffff48ff48,
    ),
    (
        0xffffff3729ffffff49ffffffffffff29,
        0xff2949ffffffffff37ffffffffffff49,
        0xffffff1bffffff1bff0d0dffffffffff,
        0x0dffffffffffffffffffff49ff49ffff,
        0x29ffffffffffffffff37ff37ffff3737,
        0x1bff1bffff29ff49ffffffffffffffff,
    ),
    (
        0xffffffffffffffffffffffffffffffff,
        0xffffffffff2affffffffffff4affffff,
        0xffffffffff4a4affffffffffff1cffff,
        0xffffff00ffffff00ffffff00ff0eff4a,
        0xff00ffff1cffffffffffff2affffffff,
        0xff4a0e4a00ffffffff4affffffff4aff,
    ),
    (
        0xff1dffffff4bffffffffffffffffff4b,
        0x1dffffffffffffffffff1dffffffffff,
        0xffffffffffffffff1dffffffffffffff,
        0xffffff4b01ffffff2b2bff4bffffffff,
        0xffffffffffffffffffffffffffffffff,
        0xffffff0fff01ff01ffff01ff4b4bffff,
    ),
    (
        0xffffffffff1effffffff2cffffffff4c,
        0xff1effffffffffffffffff10ff4cffff,
        0xffffff4cffff4cffffffffffffffffff,
        0xffffffff02ffffff2cffff4cffffffff,
        0xffffff1effffffffffffffffffffffff,
        0xff4cff102cffffffff1e4cff4cff4cff,
    ),
    (
        0xff03ffffff4dff4dffffff032dff1fff,
        0xffff114dffffffffffffff4dffff4dff,
        0xffffffffff1103ffffffffffffffffff,
        0x11ffffffffffff11ffffffffffffff4d,
        0xff1f1fff1fff2dffffffffffffffffff,
        0xff11ff03ffffffff03ffffffffffff2d,
    ),
    (
        0xffffffffffffffffffffff4e2eff4eff,
        0xffffffffffffffffffffffffff4effff,
        0xffffffffffffff4effff4effff20ffff,
        0xff12ff12ffffffff2e0404ffffffff4e,
        0xffffffffff12ffff20202effffffffff,
        0xff2e12ffffffffffffffff04ffffffff,
    ),
    (
        0xffffffffffffffffffffffffffffffff,
        0xffff4fffffff4fffffffffffffffffff,
        0xffffffffff4fff13ffffff13ffffffff,
        0xffffffff0505ffffffffffffff4fffff,
        0xffffffffff21ffffffffffffffffffff,
        0xff21ffffffffffffffffffffffffff13,
    ),
    (
        0xffffffffffffffffff50ffffffff50ff,
        0xffffffffffffffffffffffffffffffff,
        0xffffffffffffffffffff06ffffffffff,
        0xffffffffffffffff30ffffffffffff50,
        0xffffffffffffffff14ffffffffffffff,
        0xffff1414ffffffff06ff22063022ffff,
    ),
    (
        0xffff07ff07ff51ffffffffffffffffff,
        0xffffffffffffffffff31ffffffffffff,
        0xffff51ffffffffffff07ffffff5151ff,
        0x1515ffffffffff07ffffffffffffffff,
        0xffffff31ff23ffff3115ffffffffffff,
        0x23ff23ffff3115ffffffffffffffffff,
    ),
    (
        0xff24ffffffffffffffffffffff52ffff,
        0xffff16ffffffffffffffffffff2416ff,
        0xffff24ffffffffffffffffffffffffff,
        0xffffffffffffff08ffffffffffffff16,
        0xffffffffff16ffffffffffffff16ffff,
        0xff16ffff16ffff1608ff08ff24ffffff,
    ),
    (
        0xffffffffffffffffffffffffffffffff,
        0x33ffffffffffffffffffffffff25ffff,
        0xffffffffffffffffffffffffffffffff,
        0x53ffffffffffffffffffffff33ffffff,
        0xffff2533ffffff25ffffffffffffffff,
        0xff1709ffffffffff09ff25ffffffffff,
    ),
    (
        0xffffffffffffffffffffffffffffffff,
        0xffffffffffffffffffff18ff34ff54ff,
        0xffffffffffffffffffffffffffffffff,
        0xffffffffffffffffffffffffffffffff,
        0xffffffffffffffffffffffffffffff34,
        0xffffffffffffff34ffffffff26ffff18,
    ),
    (
        0xffffffffffffffffffffffffffffffff,
        0xffff35ffffffffffffffffffffffffff,
        0xffffffffffffffffffffffffffffffff,
        0xffffffffffffffffffffffffffffffff,
        0xffffff27ffffffffffffffffff0bffff,
        0xff19ff0bffffffffff0bffffffffffff,
    ),
    (
        0x0cffffffffffffffffffffffffffffff,
        0xffffffff56ffffffffffffffffffffff,
        0xff0cffff0cffffffffffffffffffffff,
        0xffffffffffffffffffff1affffffffff,
        0xffffffffffffff2836ffffffffffffff,
        0xffff1affff28ffffffff28ffffffff1a,
    ),
    (
        0xffffffffffffff29ffffffffffffffff,
        0xffffffffffffffffffff37ffffffffff,
        0xffffffffffffffffffff5729ffffffff,
        0xffff0dffffffffffffffffffffffffff,
        0xffffffffffffffffffffffffffffffff,
        0xffffffffffffffffffffffffffffffff,
    ),
    (
        0xffffffffffffffffffffff1cffffffff,
        0xffffffff1cffffffffffff3cffffffff,
        0x58ffffffffffffffffffffffffffffff,
        0xffffffffffffffffffffffffffffffff,
        0xffff2affffffffffffffffffffffffff,
        0xffffffffffffff1cffffffffffffffff,
    ),
    (
        0xffffffffffffffffffffffffffffffff,
        0xffffffff1dffffffffffffffffffffff,
        0xffffffffffffffffff0fffffffffffff,
        0xffffffffffffffffffffffffffffffff,
        0xffffffffffffff0fffffffffffffffff,
        0xffffffffffffffffffffffffffffffff,
    ),
    (
        0xffffffff5affffffffffffffffffffff,
        0xffffffffff10ffffffffffffffff1eff,
        0xffffffffffffffffffffffffffffffff,
        0xffffffffffffff5affffffffffffffff,
        0xffffffffffff2cffffffffffffffffff,
        0xffffff02ffffffffffffffff102cffff,
    ),
    (
        0x2dffffff03ff2dffffff2d03ffff5bff,
        0xffffffff2dffffffffffffff1f2dffff,
        0xffffffffffffffffffffffffffffffff,
        0xffffffffffffffffffffffffffffffff,
        0xffffffffffffffffffffffffffffff03,
        0xffffffffffffffffffffff2dffffffff,
    ),
    (
        0xffffff40ffffffffffffffffffffffff,
        0xffffffffffffffffffffffffffffffff,
        0xff04ffff12ffffffffffffffffffffff,
        0xffffffffffffffffffffffffffffffff,
        0xffffffffffffffffffffff20ff202eff,
        0xffffffffff04ffff2effffffffffffff,
    ),
    (
        0xffffffffffffffffffffffffff2fffff,
        0xffffffffffffffffffffffffffffffff,
        0xffffffff5dffffffffffffffffffffff,
        0xffffffffffffffffffffffffffffffff,
        0xffff2fffffffffffff0521ffffffffff,
        0xffff13ffffffffff21ffffffffffffff,
    ),
    (
        0xffffffffffffffffffffffffffffffff,
        0xffffffffffffffffffffffffffffffff,
        0xffff14ffffffffffffffffffffffffff,
        0xffffffffffffffffffffffffffffffff,
        0xffff06ffffffffffffffffffffffffff,
        0x06ffffffffffffffff30ffffffffffff,
    ),
    (
        0xffffffff31ffffffffffffffffffffff,
        0xffffffffffffffffffffffffffffffff,
        0xffffff15ffffffff15ffffffffffffff,
        0xffffffffffffffffffffffffffffffff,
        0x31ffffffffffffff07ffffffff15ffff,
        0xffffffffffff3115ffff23ffffffffff,
    ),
    (
        0xffffffffffffff08ffffffffffffffff,
        0xffffffffffffffffffffffffffffffff,
        0xffff24ffff16ffffffffffff44ffffff,
        0xffffffffffffffffffffffffffffffff,
        0xffffffffffffff16ffffffffffffffff,
        0xffffffffffffffffffffffffffffffff,
    ),
    (
        0xffffffffffffff49ff25ff25ffffffff,
        0xffff25ffffffffffffffffffffffffff,
        0x17ffffffffffffffffff09ffffffffff,
        0xffffffffffffffffffffffffffffffff,
        0xffffffffffffffff33ffffffffffffff,
        0xffffff09ffff09ffffffffffff33ffff,
    ),
    (
        0xffffffffffffffffffffffffffffffff,
        0xffffffffffffffff34ff26ffffffffff,
        0xffffffffffffffffffffffffffffffff,
        0xffffff0affffffffffff18ffffffffff,
        0xffffff34ffffffff26ffffffffffffff,
        0xffffffffffffffffffffffffffffffff,
    ),
    (
        0xffffffffffffff4bffffffffffffffff,
        0xffffffffffffff27ffffffffffffffff,
        0xff0bffffffffffffffffffffffffffff,
        0xffffffff0bffffffffffff4bffffff0b,
        0xffffffff2719ffffffffffffffffffff,
        0xff35ffffffff19ffffffffff35ffffff,
    ),
    (
        0xffffffffffffff4cffffffff28ffffff,
        0xffffffffffffffffff1affffffffff36,
        0xffffffff4cffffffffffffffffffffff,
        0xffffffffffffffffffffffffffffffff,
        0xffffffffffffffffffffffffffffffff,
        0xffffffffffffffffffffffffffffffff,
    ),
    (
        0xffffffffffffffffffff29ffffffff0d,
        0xffffffffffffffffffffffffffff4dff,
        0xffffffffffffffffffffffffffffff1b,
        0xffffffffffffffffffffffffffff1bff,
        0x29ffffff1cffffffffffffff37ffffff,
        0xffffffffffffffffffffffffffffffff,
    ),
    (
        0xffffffffffffffffffffff4effffffff,
        0xffffffffffffffffffffffffff1cffff,
        0xffffffffffffffffffffffffffffffff,
        0xffffffffffffff2affffffffffffffff,
        0xffffffffffffffffffffffffffffffff,
        0xffffffffffffffffffffffffffffffff,
    ),
    (
        0xffffffff1dffffffffffffffffffff4f,
        0xffffffffffffffffffffffffffffffff,
        0xffff3d4fffffffffffffffffffffffff,
        0xffffffffffffffffffffffffffffffff,
        0xffffffffffff0fffff1dff1dffffffff,
        0xffff1dffffffffffffffffffffffffff,
    ),
    (
        0xffffffffffff2cffffffffffffffffff,
        0xffffffffffffffffffffffffff2cffff,
        0xffffffffffffffffffffffffff02ffff,
        0xffffffffffff5050ffffffffffffffff,
        0xffffffff2cffffffffffffff02ffffff,
        0xff1effffffffffffffffffff2cffffff,
    ),
    (
        0xffffffffffffffffffffff1fffffffff,
        0xffffffffffffffffffffffffffff51ff,
        0xffffffffffffffff11ffffff3fffffff,
        0xffff51ff03ff2d2dffffffffffffffff,
        0x1fffff03ffffffffffffffffffffffff,
        0x11ffffffffffffffffffff2dffffffff,
    ),
    (
        0xff40ffffffffffffffffffffffffffff,
        0xffffffffffffffffffffffffffffffff,
        0xffffffffffffffffffffffffffffffff,
        0xffffffffffffffffff04ffffffffffff,
        0xffffffff20ffffffffffffffff12ffff,
        0xff12ffffffffffffffffffffffffffff,
    ),
    (
        0xffff41ff05ffffffffffffffffffffff,
        0xffffffffffffffffffffffffffffffff,
        0xffffffffffffffffffffffffffffffff,
        0xffffffffffffffffffffffffffffffff,
        0xffffffffffff05ffffffff21ffffffff,
        0xffffffffffffffffffffffffffffffff,
    ),
    (
        0xffffffffffffffffffffffffffffffff,
        0xffffffff30ffffffffff42ffffffffff,
        0xffffffff42ffffff54ffffffffffffff,
        0xffffffffffffffffffffffffffffffff,
        0x22ffffffffffffffff22ffff30ffffff,
        0xffffffffffffffffff06ff22ff22ffff,
    ),
    (
        0xffffffffffffffffffffffffffffffff,
        0xffffffffffffffffffffffffffff15ff,
        0xffffffffffffffffffffffff43ffff55,
        0xffffffff07ffffffffffffffffffffff,
        0xffffffffffffff07ffffffff0707ffff,
        0xffffffffffffffffffffffffffffffff,
    ),
    (
        0xffffffffffffffffffffffffffffffff,
        0xffffffffffffffffffffffff32ffffff,
        0xffffffffffffffff08ffffffffffffff,
        0xffffffffffffffffffffffffffffffff,
        0x08ffffffffffffffff16ffffffffff32,
        0xffffffffffffffffffffffffffffffff,
    ),
    (
        0xffffffffffffffffffffffffffff45ff,
        0xffffffffffffffffffffffffffffffff,
        0xffffffffffffffffffff25ffffffffff,
        0xffffff17ffffffffffffffffffffffff,
        0xff17ffffffff25ffffffffffffffffff,
        0xffffffffffffffffffffffffffffffff,
    ),
    (
        0xffffffffffffffffffffffffffffffff,
        0xffffffffffffffffffffffffffffffff,
        0xff58ffffffff0affffffffffffffffff,
        0xffffffffffffffff18ffffffffffffff,
        0xff34ffffffffffffffffffffffffffff,
        0xffffffffffffffffffffffffffffffff,
    ),
    (
        0xffffffffffffffffffffffffffffffff,
        0xffffffffffffffffffffffffffffffff,
        0xffffffffffffffffffffffffffff27ff,
        0xffffffffffffffffffffffffffffffff,
        0x0bffffffff35ffffffffffffffffffff,
        0xffffffffffffffffffffffff35ffffff,
    ),
    (
        0xffffffffffffffffffffffffffffffff,
        0xffffffffffffffffffffffffffffffff,
        0xffffffffffffffffffffffffffffffff,
        0xffffffffffffffffffffffff1affffff,
        0xffffff36ffffffffffffffffffffff0c,
        0x1affffffff1affffffffffffffffffff,
    ),
    (
        0xffffffffffffffffffffffffffffffff,
        0xffffffffffffffffffffffffffffffff,
        0xffffffffffffffffffffffffffffffff,
        0xffffffff37ffffffffffffffffffffff,
        0xffffffffffffffffffffffffffffffff,
        0xffffffffffffffffffffffffffffffff,
    ),
    (
        0xffffffffffffffffffffffffffffffff,
        0xffffffffffffffffffffffffffffffff,
        0xffffffffffffffffffffffff1cffffff,
        0xffffffffffffffffffffffffffffffff,
        0xff2affffff0effffffffffffffffffff,
        0xffffffffffffffffffffffffffffffff,
    ),
    (
        0xffffffffffffffffffff5dffffffffff,
        0xffffffffffffffffffffffffffffffff,
        0xffffffffffffffffffffffffffffff3d,
        0xffffffffffffffffffffffffffffffff,
        0xffffffffffffffffffffffffffffffff,
        0xffffffffffffffffffffffffffffffff,
    ),
    (
        0xffffffffffffffffffffffffffffffff,
        0xffffffffffffffffffffffffffffffff,
        0xffffffffffffffffffffffffffffffff,
        0xffffffffffffffffffffffffffffffff,
        0xffffffffff02ffffffffffffffffffff,
        0xffffffffffffffffffffffffffffffff,
    ),
    (
        0xffffffffffffffffffffffffffffffff,
        0xffffffffffffffffffffffffffffffff,
        0xffffffffffffffffffffffffffffffff,
        0xffffffffffffffffffffffffffffffff,
        0xffffffffffffffffffffffffffffffff,
        0xffffffffffffffffffffffffffffffff,
    ),
    (
        0xffffffffffffffffffffffffffffffff,
        0xffffffffffffffffffffffffffffffff,
        0xffffffffffffffffffffffffffffffff,
        0xffffffffffffffffffffffffffffffff,
        0xffffffffffffffffffffffffffffffff,
        0xffffffffffffffffffffffffffffffff,
    ),
    (
        0xffffffffffffffffffffffffffffffff,
        0xffffffffffffffffffffffffffffffff,
        0xffffffffffffff13ffffffffffffffff,
        0xffffffffffffffffffffffffffffffff,
        0xffffffffffffffffffffffffffffffff,
        0xffffffffffffffffffffffffffffffff,
    ),
    (
        0xffffffffffffffffffffffffffffffff,
        0xffffffffffffffffffffffffffffffff,
        0xffffffffffffffffffffffffffffffff,
        0xffffffffffffffffffffffffffffffff,
        0xffffffffffffffffffffffffffffffff,
        0xffffffffffffffffffffffffffffffff,
    ),
    (
        0xffffffffffffffffffffffffffffffff,
        0xffffffffffffffffffffffffffffffff,
        0xff23ffffffffffffffffffffffffffff,
        0xffffffffffffffffffffffffffffffff,
        0xffffffffffffffffffffffffffffffff,
        0xffffffffffffffffffffffffffffffff,
    ),
    (
        0xffffffffffffffffffffffffffffffff,
        0xffffffffffffffffffffffffffffffff,
        0xffffffffffffffffffffffffffffffff,
        0xffffffffffffffffffffffffffffffff,
        0xffffffffffffffffffffffffffffffff,
        0xffffffffffffffffffffffffffffffff,
    ),
    (
        0xffffffffffffffffffffffffffffffff,
        0xffffffffffffffffffffffffffffffff,
        0xffffffffffffffffffffffffffffffff,
        0xffffffffffffffffffffffffffffffff,
        0xffffffffffffffffffffffffffffffff,
        0xffffffffffffffffffffffffffffffff,
    ),
    (
        0xffffffffffffffffffffffffffffffff,
        0xffffffffffffffffffffffffffffffff,
        0xffffffffffffffffffffffffffffffff,
        0xffffffffffffffffffffffffffffffff,
        0xffffffffffffffffffffffffffffffff,
        0xffffffffffffffffffffffffffffffff,
    ),
    (
        0xffffffffffffffffffffffffffffffff,
        0xffffffffffffffffffffffffffffffff,
        0xffffffffffffffffffffffffffffffff,
        0xffffffffffffffffffffffffffffffff,
        0xffffffffffffffffffffffffffffffff,
        0xffffffffffffffffffffffffffffffff,
    ),
    (
        0xffffffffffffffffffffffffffffffff,
        0xffffffffffffffffffffffffffffffff,
        0xffffffffffffffffffffffffffffffff,
        0xffffffffffffffffffffffffffffffff,
        0xffffffffffffffffffffffffffffffff,
        0xffffffffffffffffffffffffffffffff,
    ),
    (
        0xffffffffffffffffffffffffffffffff,
        0xffffffffffffffffffffffffffffffff,
        0xffffffffffffffffffffffffffffffff,
        0xffffffffffffffffffffffffffffffff,
        0xffffffffffffffffffffffffffffffff,
        0xffffffffffffffffffffffffffffffff,
    ),
    (
        0xffffffffffffffffffffffffffffffff,
        0xffffffffffffffffffffffffffffffff,
        0xffffffffffffffffffffffffffffffff,
        0xffffffffffffffffffffffffffffffff,
        0xffffffffffffffffffffffffffffffff,
        0xffffffffffffffffffffffffffffffff,
    ),
    (
        0xffffffffffffffffffffffffffffffff,
        0xffffffffffffffffffffffffffffffff,
        0xffffffffffffffffffffffffffffffff,
        0xffffffffffffffffffffffffffffffff,
        0xffffffffffffffffffffffffffffffff,
        0xffffffffffffffffffffffffffffffff,
    ),
)
LATE = (
    (0x0000, 0x0889, 0x0000, 0x7777, 0x0000, 0x0000),
    (0x0000, 0x09eb, 0x0000, 0x7777, 0x0000, 0x0000),
    (0x000c, 0x0dcb, 0x0111, 0x7777, 0x0000, 0x0000),
    (0x0008, 0x0cfe, 0x0111, 0x7777, 0x0000, 0x0000),
    (0x000d, 0x0ccd, 0x1111, 0x7777, 0x0000, 0x0000),
    (0x8fb1, 0xf040, 0x3faf, 0x0888, 0x0000, 0x8000),
    (0x6f77, 0xf012, 0x0eff, 0x8989, 0x0000, 0x8000),
    (0xbfff, 0xf308, 0x3e7f, 0x888d, 0x0000, 0x8000),
    (0xb7ff, 0xe351, 0x2df7, 0x08df, 0x0000, 0x8000),
    (0xdcf7, 0xff47, 0x6ffe, 0x171d, 0x0000, 0xc800),
    (0x60f7, 0x9ce6, 0x83df, 0xffbc, 0x7fff, 0x0000),
    (0xf7ef, 0x83ff, 0xd1db, 0xcf77, 0x3fff, 0x0000),
    (0xf8af, 0xa33f, 0xdfdf, 0xf777, 0x7fff, 0x0000),
    (0x79af, 0x8aff, 0xd7fb, 0xf761, 0x577f, 0x0800),
    (0xfcfb, 0xa77f, 0xb9bf, 0xf7f7, 0x77ff, 0x0000),
    (0xfb1f, 0xf3ff, 0x2df7, 0x3ffd, 0x177f, 0x0000),
    (0xfffb, 0xb79c, 0xef6f, 0xd86d, 0x3fff, 0x8080),
    (0x6fb9, 0xf804, 0x7fdf, 0x9fff, 0x3fff, 0x98e0),
    (0xfff7, 0xf605, 0x5ffd, 0xbea3, 0x3fff, 0xcc08),
    (0x6b7e, 0xb88e, 0x75f3, 0xc59d, 0x3fff, 0x8680),
    (0xff7f, 0x6fa7, 0xf7e6, 0x1bfe, 0xffff, 0xc880),
    (0xf7ff, 0x0f9a, 0xafdf, 0xff7f, 0xffff, 0xa680),
    (0x7bde, 0x6fff, 0xff7d, 0x8cff, 0xffff, 0x40e0),
    (0xd6bf, 0x1fee, 0xf7f3, 0xfedb, 0xffff, 0x0004),
    (0x2bff, 0x5b5f, 0xbc9b, 0x7fff, 0xffff, 0xc5da),
    (0xbcef, 0x7f3f, 0xf7fd, 0xeffd, 0xffff, 0x1342),
    (0x3fdf, 0x6e9d, 0xff9f, 0x6777, 0xffff, 0xccf8),
    (0x7f9f, 0x4eff, 0x33fe, 0xef2c, 0xffff, 0xde6a),
    (0xa6ef, 0xdffb, 0xf7fb, 0xfbef, 0xffff, 0xa9b4),
    (0xf2df, 0xefff, 0x3f5f, 0xff3f, 0xffff, 0xebe2),
    (0xf7ff, 0xefef, 0xabbf, 0xf75f, 0xffff, 0xadc0),
    (0xad6f, 0x1aff, 0x97fd, 0xfdf6, 0xffff, 0xeaec),
    (0xff8f, 0x8bff, 0xff3b, 0xbf57, 0xffff, 0xfec8),
    (0xf3ff, 0xfeee, 0xbbff, 0xffff, 0xffff, 0xd9fb),
    (0xff4f, 0xcf7f, 0xffdb, 0xff77, 0xffff, 0xffbc),
    (0xd6bf, 0x3dbf, 0x5bff, 0xeb3f, 0xffff, 0xddf9),
    (0xfe5f, 0x92f8, 0x9ff3, 0xffff, 0xffff, 0xfffb),
    (0xdf7f, 0xbfff, 0xdedb, 0x6ff7, 0xffff, 0x7fff),
    (0xffff, 0xffde, 0xfff7, 0xfef6, 0xffff, 0xfffd),
    (0xefbb, 0xbfff, 0xefff, 0xdfff, 0xffff, 0xffff),
    (0x37ff, 0xdfde, 0xfadf, 0xff7f, 0xffff, 0xf7ff),
    (0xdfff, 0xffff, 0xfeef, 0xffdf, 0xffff, 0xffdf),
    (0xffff, 0xffff, 0xf6ef, 0xdfff, 0xffef, 0x7fff),
    (0xffff, 0xfebf, 0xf7ff, 0xffff, 0xffff, 0xffff),
    (0xefff, 0xfbf7, 0xfffd, 0xfdfb, 0xffff, 0xf6ff),
    (0xf7ee, 0xffff, 0xfff7, 0x75cb, 0xffff, 0xfffd),
    (0xbbff, 0xf7ff, 0xffeb, 0xff7d, 0xefff, 0xffff),
    (0xffbf, 0xdfff, 0xff5f, 0xdffb, 0xffff, 0xf7ff),
    (0x5fff, 0xdfff, 0xffff, 0xffbf, 0xffff, 0xffff),
    (0xff7f, 0xee7b, 0xffdf, 0x75ff, 0xffff, 0xffff),
    (0xfeff, 0xfaff, 0xdfff, 0xffff, 0xfff7, 0xffff),
    (0xeddf, 0x7fff, 0xdfaf, 0xff7b, 0xffff, 0xfeff),
    (0xefff, 0xffdf, 0xff5f, 0xef7f, 0xffff, 0xffff),
    (0xb7fe, 0xf9ff, 0xf6ff, 0xbff7, 0xffff, 0xfeef),
    (0xffff, 0xffbf, 0xfff7, 0xfffe, 0xffff, 0xf6ff),
    (0xfffe, 0xfffc, 0x7fdf, 0xfff7, 0xffff, 0xfffd),
    (0xffff, 0xffff, 0xf7fb, 0xfeff, 0xffff, 0xffef),
    (0xffff, 0xfdff, 0xd7af, 0xffff, 0xdfff, 0xeffe),
    (0xfff3, 0xffff, 0xbfff, 0xf5f3, 0xffff, 0xfcff),
    (0xe7ff, 0x7f7f, 0x7fef, 0xfcef, 0xfff7, 0xdffd),
    (0xffbf, 0xbffb, 0xf7ff, 0xffff, 0xbfff, 0xffff),
    (0xf5ff, 0xffff, 0xffef, 0xffff, 0xdfff, 0xffff),
    (0xffbf, 0xffff, 0x7fab, 0xf7f7, 0xf7df, 0xff7f),
    (0xf6f3, 0xfffd, 0xffff, 0xffff, 0xfff7, 0xfffe),
    (0x7f7f, 0xffbf, 0xffff, 0xfff6, 0xffff, 0xffff),
    (0xffff, 0xafff, 0xfddf, 0xffff, 0xfffd, 0xffff),
    (0xfdff, 0xff7f, 0xffff, 0xbfff, 0xffff, 0xbfff),
    (0x7fff, 0xffff, 0xfffd, 0xfbf7, 0xffff, 0xffff),
    (0xfffe, 0x7bf7, 0xffff, 0xefff, 0xffff, 0xffff),
    (0xffff, 0xffff, 0xffff, 0xf7ff, 0xffff, 0xffff),
    (0xffff, 0xfbff, 0xfff7, 0xbfff, 0xffff, 0xffff),
    (0xffff, 0xffff, 0xffff, 0xffff, 0xfffe, 0xffdf),
    (0xfbff, 0xffff, 0xffff, 0xffff, 0xffff, 0xffff),
    (0xffff, 0xffff, 0xffff, 0xffff, 0xffff, 0xffff),
    (0xffff, 0xffff, 0xffff, 0xffff, 0xffff, 0xffff),
    (0xffff, 0xfeff, 0xffff, 0xffff, 0xffff, 0xffff),
    (0xffff, 0xffff, 0xffff, 0xffff, 0xffff, 0xffff),
    (0xffff, 0xffff, 0xbfff, 0xffff, 0xffff, 0xffff),
    (0xffff, 0xffff, 0xffff, 0xffff, 0xffff, 0xffff),
    (0xffff, 0xffff, 0xffff, 0xffff, 0xffff, 0xffff),
    (0xffff, 0xffff, 0xffff, 0xffff, 0xffff, 0xffff),
    (0xffff, 0xffff, 0xffff, 0xffff, 0xffff, 0xffff),
    (0xffff, 0xffff, 0xffff, 0xffff, 0xffff, 0xffff),
    (0xffff, 0xffff, 0xffff, 0xffff, 0xffff, 0xffff),
    (0xffff, 0xffff, 0xffff, 0xffff, 0xffff, 0xffff),
    (0xffff, 0xffff, 0xffff, 0xffff, 0xffff, 0xffff),
    (0xffff, 0xffff, 0xffff, 0xffff, 0xffff, 0xffff),
    (0xfffe, 0xfffe, 0xfffe, 0xfffe, 0xfffe, 0xfee8),
    (0xfee8, 0xfee8, 0xfee8, 0xfee8, 0xe880, 0xe880),
    (0xe880, 0xe880, 0xe880, 0xe880, 0xe880, 0xc800),
    (0xc000, 0x8000, 0xc000, 0xc000, 0x8000, 0x8000),
    (0x8000, 0x8000, 0x8000, 0x8000, 0x8000, 0x8000),
)
LATE_BY = 7
NO_WAIT = 0xFF
GAIN_STEP = 4
SLOTS = 33
UNITS = 129
UNIT = 16
LANES = 128
STARTS = (0, 8, 16, 24, 32, 40, 48, 56, 64, 72, 80, 88, 96, 104, 112, 120)
OPPOSITE = (1, 0, 3, 2, 5, 4)
ORDER = (5, 3, 1, 2, 0, 4)
SENDS = 6
NOTHING = 0xFFFF


SIZES = dict(zip(STARTS, (b - a for a, b in zip(STARTS, STARTS[1:] + (UNITS,)))))


def size_of(entry):
    return 0 if entry == NOTHING else SIZES[entry % UNITS]


def neighbour_position(p, d):
    x, y = divmod(p, 4)
    if d == 0:
        x = (x + 1) % 4
    if d == 1:
        x = (x + 3) % 4
    if d == 2:
        y = (y + 1) % 4
    if d == 3:
        y = (y + 3) % 4
    return 4 * x + y


def signed(word):
    return word - (1 << 32) if word >= 1 << 31 else word


def entries(step, d):
    return [(PLAN[step][d] >> (16 * p)) & 0xFFFF for p in range(16)]


def mask_of(flags):
    return sum(1 << p for p, flag in enumerate(flags) if flag)


def gather_kernel(re_ref, im_ref, held, part, part_in, send_sem, recv_sem, load_sem, pair_sem):
    bins = re_ref.shape[0]
    tiles = re_ref.shape[1]
    fr = lax.axis_index("fr")
    sr = lax.axis_index("sr")
    sc = lax.axis_index("sc")
    z, x, y = sr // 4, sr % 4, sc
    p = 4 * x + y
    steps = len(PLAN)

    xp, xm = (x + 1) % 4, (x + 3) % 4
    yp, ym = (y + 1) % 4, (y + 3) % 4
    zp, zm = (z + 1) % 4, (z + 3) % 4
    targets = (
        (fr, 4 * z + xp, y),
        (fr, 4 * z + xm, y),
        (fr, sr, yp),
        (fr, sr, ym),
        (fr, 4 * zp + x, y),
        (fr, 4 * zm + x, y),
    )
    ahead = (4 * (xp - x), 4 * (xm - x), yp - y, ym - y, 16, -16)
    twin = (1 - fr, sr, sc)
    shift = 16 * (y % 2)

    barrier = pltpu.get_barrier_semaphore()
    for device in targets + (twin,):
        pl.semaphore_signal(barrier, inc=1, device_id=device, device_id_type=MESH)
    loads = []
    for f in range(bins):
        for half in range(2):
            for i, ref in enumerate((re_ref, im_ref)):
                place = 4 * f + 2 * half + i
                source = ref.at[f, :, :, pl.ds(half * LANES, LANES)]
                target = held.at[pl.ds(place * tiles, tiles)]
                loads.append(pltpu.make_async_copy(source, target, load_sem.at[0]))
    for load in loads:
        load.start()

    everything = held.at[pl.ds(0, UNITS - 1)]
    pltpu.make_async_copy(everything, everything, load_sem.at[0]).wait()
    pl.semaphore_wait(barrier, 7)

    def chosen(step, d):
        words = [jnp.int32(signed((PLAN[step][d] >> (32 * i)) & 0xFFFFFFFF)) for i in range(8)]
        words = [jnp.where(y < 2, words[i], words[i + 1]) for i in range(0, 8, 2)]
        word = jnp.where(
            x < 2,
            jnp.where(x == 0, words[0], words[1]),
            jnp.where(x == 2, words[2], words[3]),
        )
        return lax.shift_right_logical(word, shift) & 0xFFFF

    def needed(step, d):
        words = [jnp.int32(signed((NEEDS[step][d] >> (32 * i)) & 0xFFFFFFFF)) for i in range(4)]
        word = jnp.where(
            x < 2,
            jnp.where(x == 0, words[0], words[1]),
            jnp.where(x == 2, words[2], words[3]),
        )
        return lax.shift_right_logical(word, 8 * y) & 0xFF

    def guarded(mask, action):
        if mask == 0:
            return
        if mask == 0xFFFF:
            action()
            return
        pl.when((lax.shift_right_logical(jnp.int32(mask), p) & 1) == 1)(action)

    def transfer(step, d, source, target, size, arrival):
        return pltpu.make_async_remote_copy(
            src_ref=held.at[pl.ds(source, size)],
            dst_ref=held.at[pl.ds(target, size)],
            send_sem=send_sem.at[SENDS * d + step % SENDS],
            recv_sem=recv_sem.at[arrival],
            device_id=targets[d],
            device_id_type=MESH,
        )

    def for_each_size(sizes, action, among=0xFFFF):
        for size in sorted(set(sizes) - {0}):
            guarded(mask_of(v == size for v in sizes) & among, functools.partial(action, size))

    def send(step, d):
        waits = mask_of((NEEDS[step][d] >> (8 * q)) & 255 != NO_WAIT for q in range(16))

        def arrived(size):
            transfer(step, d, 0, UNITS, size, needed(step, d)).wait_recv()

        def action(size):
            source = chosen(step, d)
            transfer(step, d, source, source - UNITS * ahead[d], size, SEMAPHORES[step][d]).start()

        sizes = [size_of(v) for v in entries(step, d)]
        for_each_size(sizes, arrived, waits)
        for_each_size(sizes, action)

    def receive(step, d):
        sent = [size_of(v) for v in entries(step, d)]
        coming = [sent[neighbour_position(q, OPPOSITE[d])] for q in range(16)]
        for_each_size(coming, lambda size: transfer(step, d, 0, UNITS, size, SEMAPHORES[step][d]).wait_recv(), LATE[step][d])

    def finish(step, d):
        sent = [size_of(v) for v in entries(step, d)]
        for_each_size(sent, lambda size: transfer(step, d, 0, UNITS, size, SEMAPHORES[step][d]).wait_send())

    exchange = pltpu.make_async_remote_copy(
        src_ref=part,
        dst_ref=part_in,
        send_sem=pair_sem.at[0],
        recv_sem=pair_sem.at[1],
        device_id=twin,
        device_id_type=MESH,
    )

    for step in range(steps):
        if step >= LATE_BY:
            for d in range(6):
                receive(step - LATE_BY, d)
        for d in ORDER:
            if step >= SENDS:
                finish(step - SENDS, d)
            send(step, d)
        if step == 0:
            total = jnp.zeros((tiles, UNIT, LANES), jnp.float32)
            for i in range(4 * bins):
                piece = held[pl.ds(i * tiles, tiles)].astype(jnp.float32)
                total += piece * piece
            total = total.reshape(tiles * UNIT, LANES)
            power = jnp.sum(total.T, axis=0, keepdims=True)
            part[...] = jnp.broadcast_to(power, part.shape)
            exchange.start()
        if step == GAIN_STEP:
            exchange.wait()
            power = part[...] + part_in[...]
            gain = 1.0 / jnp.sqrt(power * (1.0 / 2048.0))
            gain = jnp.concatenate([gain, gain], axis=0)
            high = gain.astype(jnp.bfloat16).astype(jnp.float32)
            middle = (gain - high).astype(jnp.bfloat16).astype(jnp.float32)
            low = gain - high - middle
            row = lax.broadcasted_iota(jnp.int32, (UNIT, LANES), 0)
            rest = jnp.where(row == 1, middle, low)
            held[UNITS - 1] = jnp.where(row == 0, high, rest).astype(jnp.bfloat16)
    for step in range(steps - LATE_BY, steps):
        for d in range(6):
            receive(step, d)
    for step in range(steps - SENDS, steps):
        for d in range(6):
            finish(step, d)


def gathered(re, im):
    bins, tiles = re.shape[:2]
    steps = len(PLAN)
    return pl.pallas_call(
        gather_kernel,
        out_shape=jax.ShapeDtypeStruct((SLOTS * UNITS, UNIT, LANES), jnp.bfloat16),
        in_specs=[pl.BlockSpec(memory_space=pltpu.HBM)] * 2,
        out_specs=pl.BlockSpec(memory_space=pltpu.VMEM),
        scratch_shapes=[
            pltpu.VMEM((8, 128), jnp.float32),
            pltpu.VMEM((8, 128), jnp.float32),
            pltpu.SemaphoreType.DMA((6 * SENDS,)),
            pltpu.SemaphoreType.DMA((max(map(max, SEMAPHORES)) + 1,)),
            pltpu.SemaphoreType.DMA((1,)),
            pltpu.SemaphoreType.DMA((2,)),
        ],
        compiler_params=pltpu.CompilerParams(
            collective_id=0, has_side_effects=True, vmem_limit_bytes=24 << 20
        ),
        name="gather_blocks",
    )(re, im)


GROUP = 11


def gain_row(tile):
    wide = tile.astype(jnp.float32)
    return wide[0:1] + wide[1:2] + wide[2:3]


def spectra(held, f, first):
    halves = [held[pl.ds(first + 32 * f + 16 * h, 16)].reshape(256, LANES) for h in range(2)]
    return jnp.concatenate(halves, axis=1)


def cross_kernel(plan, held, out, order, staged, own_column, sem, order_sem):
    bins = out.shape[0]
    fetch = pltpu.make_async_copy(plan, order, order_sem)
    fetch.start()
    own_row = gain_row(held[UNITS - 1]) * (1.0 / 16.0)
    own_column[...] = jnp.broadcast_to(own_row, (128, 128)).T
    fetch.wait()

    def group(i, carry):
        for j in range(GROUP):
            place = i * GROUP + j
            first = order[0, place] * UNITS
            weight = own_column[...] * gain_row(held[first + UNITS - 1])
            for f in range(bins):
                mine, other = spectra(held, f, 0), spectra(held, f, first)
                full = lax.dot_general(
                    mine, other, (((1,), (1,)), ((), ())), preferred_element_type=jnp.float32
                )
                staged[place, f, :, :128] = (full[:128, :128] + full[128:, 128:]) * weight
                staged[place, f, :, 128:] = (full[128:, :128] - full[:128, 128:]) * weight
            pltpu.make_async_copy(staged.at[place], out.at[:, place], sem).start()
        return carry

    lax.fori_loop(0, SLOTS // GROUP, group, 0)
    pltpu.make_async_copy(staged, staged, sem).wait()


def local(spec_re, spec_im, offsets):
    bins, rows, segs = spec_re.shape
    tiles = rows // UNIT
    re = spec_re.reshape(bins, tiles, UNIT, segs)
    im = spec_im.reshape(bins, tiles, UNIT, segs)
    re = pltpu.with_memory_space_constraint(re, pltpu.HBM)
    im = pltpu.with_memory_space_constraint(im, pltpu.HBM)
    held = gathered(re, im)
    cross = pl.pallas_call(
        cross_kernel,
        in_specs=[pl.BlockSpec(memory_space=pl.ANY), pl.BlockSpec(memory_space=pltpu.VMEM)],
        out_specs=pl.BlockSpec(memory_space=pltpu.HBM),
        out_shape=jax.ShapeDtypeStruct((bins, SLOTS, rows, 256), jnp.float32),
        scratch_shapes=[
            pltpu.SMEM((1, SLOTS), jnp.int32),
            pltpu.VMEM((SLOTS, bins, rows, 256), jnp.float32),
            pltpu.VMEM((rows, rows), jnp.float32),
            pltpu.SemaphoreType.DMA,
            pltpu.SemaphoreType.DMA,
        ],
        compiler_params=pltpu.CompilerParams(vmem_limit_bytes=30 << 20),
        name="cross_products",
    )(offsets, held)
    return cross[:, None]


def solution(mesh):
    placed = (P("fr", ("sr", "sc"), None), P("fr", ("sr", "sc"), None), P(("sr", "sc"), None))
    return jax.shard_map(
        local,
        mesh=mesh,
        in_specs=placed,
        out_specs=P("fr", ("sr", "sc"), None, None, None),
        check_vma=False,
    )
```

time: 81.5 us -> 79.4 us (0.974); the launches traced: 79.9 us -> 79.2 us
  no operation moved by 1% of the time
where the time goes in v5:
time: 79.4 us; the launch traced here: 79.2 us
  Pallas kernels  79.1 us (100%)
    pallas_call x1, Pallas kernels, gathered(): pl.pallas_call(gather_kernel, out_shape=jax.ShapeDtypeStruct((SLOTS * UNI...  72.2 us
    pallas_call x1, Pallas kernels, local(): pl.pallas_call(cross_kernel, in_specs=[pl.BlockSpec(memory_space=pl.ANY),...  6.87 us

profile of v5, /device:TPU:30, one launch (start us, length us, event | category | flops | bytes accessed | tf_op | source)
XLA Modules:
  0.0 79.2 jit_solution(3114402694328372927)
XLA Ops:
  0.0 0.0 copy-start
  0.0 72.2 %gather_blocks.1.held = bf16[4257,16,128]{2,1,0:T(8,128)(2,1)S(1)} custom-call(bf16[4,8,16,256]{3,2,1,0:T(8,128)(2,1)} %bitcast.5, bf16[4,8,16,256]{3,2,1,0:T(8,128)(2,1)} %bitcast.6), custom_call_target="tpu_custom_call" | custom-call | tf_op jit(solution)/shard_map/gather_blocks/pallas_call | solution.py:1878
  72.2 0.0 copy-done
  72.2 6.9 %cross_products.1 = f32[4,33,128,256]{3,2,1,0:T(8,128)} custom-call(s32[1,33]{1,0:T(1,128)S(1)} %copy-done, bf16[4257,16,128]{2,1,0:T(8,128)(2,1)S(1)} %gather_blocks.1.held), custom_call_target="tpu_custom_call" | custom-call | tf_op jit(solution)/shard_map/cross_products/pallas_call | solution.py:1946
Async XLA Ops:
  0.0 72.2 %copy-start = (s32[1,33]{1,0:T(1,128)S(1)}, s32[1,33]{1,0:T(1,128)}, u32[]{:S(2)}) copy-start(s32[1,33]{1,0:T(1,128)} %plan.1) | copy-start | bytes 400
